TPU v7x, 32 devices: a whole 2x2x4 slice. The times are simulated.
32 devices in a mesh: tm: 8 (over y, x, core), tx: 4 (over z).
Axes of the slice: x: 2, y: 2, z: 4, core: 2. Of those that a mesh axis runs over, the one named last changes fastest.
Arguments:
- state: float32 [8, 64, 256, 128], P('tm', 'tx'), may hold values from -6 to 6
- force: float32 [8, 64, 256, 128], P('tm', 'tx'), may hold values from -6 to 6
- u_init: float32 [64, 256, 128], P('tx'), may hold values from -6 to 6
- kappa: float32 [64, 256], P('tx'), may hold values from 0.1 to 2
- rates: float32 [128], replicated, may hold values from 0.05 to 4
- basis: float32 [128, 128], replicated, may hold values from -1 to 1, as said below
Outputs:
- correction: float32 [8, 64, 256, 128], P('tm', 'tx')
Inputs may be any that keep to these rules, and one draw needn't show every extreme that they name: basis is an orthogonal matrix.
All inputs are finite; a program needn't handle non-finite values.
Results may differ from a plain program's by a relative error of at most 0.0003.
Values sent between devices are 32-bit elements; how exact they have to be, the bound alone decides.
No kernel may reach another device: no remote copies, remote signals or barrier semaphores. Data moves between devices by JAX's collectives and lax.ppermute only.
A program may use at most 64 MiB of HBM per device.

v0:
```python
import math

import jax
import jax.numpy as jnp
from jax import lax
from jax.sharding import PartitionSpec as P

ALPHA = 0.05
TWO_PI = 2.0 * math.pi


def extended(block, sides, width):
    for axis, dim in sides:
        count = lax.axis_size(axis)
        forward = [(i, i + 1) for i in range(count - 1)]
        backward = [(target, source) for source, target in forward]
        low = lax.ppermute(
            lax.slice_in_dim(block, block.shape[dim] - width, None, axis=dim), axis, forward
        )
        high = lax.ppermute(lax.slice_in_dim(block, 0, width, axis=dim), axis, backward)
        block = jnp.concatenate([low, block, high], axis=dim)
    return block


def from_behind(array, axis, by):
    count = lax.axis_size(axis)
    pairs = [(i, i + by) for i in range(count) if 0 <= i + by < count]
    return lax.ppermute(array, axis, pairs)


def neighbours(padded):
    return (
        padded[..., 2:, 1:-1, :]
        + padded[..., :-2, 1:-1, :]
        + padded[..., 1:-1, 2:, :]
        + padded[..., 1:-1, :-2, :]
    )


def relax(source, kappa_b, real_den, imag_den, rims):
    magnitude = real_den * real_den + imag_den * imag_den

    def divide(numer):
        return jnp.stack(
            [
                (numer[0] * real_den + numer[1] * imag_den) / magnitude,
                (numer[1] * real_den - numer[0] * imag_den) / magnitude,
            ]
        )

    field = divide(source)
    for repeat in range(2):
        field = divide(source + kappa_b * rims(field))
    return field


def cell_rims(field):
    padded = extended(field, (("tm", 3), ("tx", 2)), 1)
    return neighbours(padded)


def on_device(state, force, u_init, kappa, rates, basis):
    highest = lax.Precision.HIGHEST
    column_size = state.shape[3]
    steps_total = lax.axis_size("tm")
    here = lax.axis_index("tm")
    earlier = from_behind(state, "tm", 1)
    earlier = jnp.where(here == 0, u_init[None], earlier)
    padded = extended(state, (("tx", 1),), 1)
    padded = jnp.pad(padded, ((0, 0), (0, 0), (1, 1), (0, 0)))
    beside_all = neighbours(padded)
    coords = jnp.dot(state.reshape(-1, column_size), basis, precision=highest)
    vertical = jnp.dot(coords * rates, basis.T, precision=highest).reshape(state.shape)
    kappa_b = kappa[None, :, :, None]
    residual = (
        force
        - (state - earlier)
        - vertical
        - kappa_b * (4.0 * state - beside_all)
        - 0.5 * state**3 / (1.0 + state * state)
    )
    modal = jnp.dot(residual.reshape(-1, column_size), basis, precision=highest).reshape(
        state.shape
    )
    decay = jnp.log(ALPHA) / steps_total
    scaled = modal * jnp.exp(decay * here.astype(jnp.float32))
    gathered = lax.all_to_all(scaled, "tm", split_axis=2, concat_axis=0, tiled=True)
    block_y = gathered.shape[2]
    indices = jnp.arange(steps_total)
    steps_f = indices.astype(jnp.float32)
    products = (indices[:, None] * indices[None, :] % steps_total).astype(jnp.float32)
    angles = TWO_PI * products / steps_total
    cosine = jnp.cos(angles)
    sine = jnp.sin(angles)
    flat_cells = gathered.reshape(steps_total, -1)
    spectrum = jnp.stack(
        [
            jnp.dot(cosine, flat_cells, precision=highest),
            -jnp.dot(sine, flat_cells, precision=highest),
        ]
    ).reshape((2,) + gathered.shape)
    factor = jnp.exp(decay)
    theta = TWO_PI * steps_f / steps_total
    shift_re = 1.0 - factor * jnp.cos(theta)
    shift_im = factor * jnp.sin(theta)
    start = here * block_y
    kappa_cells = lax.dynamic_slice_in_dim(kappa, start, block_y, 1)[None, :, :, None]
    real_den = shift_re[:, None, None, None] + rates + 4.0 * kappa_cells
    imag_den = shift_im[:, None, None, None] + jnp.zeros_like(real_den)
    solved = relax(spectrum, kappa_cells, real_den, imag_den, cell_rims)
    flat_re = solved[0].reshape(steps_total, -1)
    flat_im = solved[1].reshape(steps_total, -1)
    times = (
        jnp.dot(cosine, flat_re, precision=highest) - jnp.dot(sine, flat_im, precision=highest)
    ) / steps_total
    times = times * jnp.exp(-decay * steps_f)[:, None]
    back = lax.all_to_all(
        times.reshape(gathered.shape), "tm", split_axis=0, concat_axis=2, tiled=True
    )
    return jnp.dot(back.reshape(-1, column_size), basis.T, precision=highest).reshape(state.shape)


def solution(mesh):
    return jax.shard_map(
        on_device,
        mesh=mesh,
        in_specs=(
            P("tm", "tx", None, None),
            P("tm", "tx", None, None),
            P("tx", None, None),
            P("tx", None),
            P(),
            P(),
        ),
        out_specs=P("tm", "tx", None, None),
        check_vma=False,
    )
```

profile of v0, /device:TPU:0, one launch (start us, length us, event | category | flops | bytes accessed | tf_op | source)
XLA Modules:
  0.0 164.9 jit_solution(18260656128730488843)
XLA Ops:
  0.0 0.0 copy-start
  0.0 3.9 %collective-permute-start = (f32[1,16,256,128]{3,2,1,0:T(8,128)}, f32[1,16,256,128]{3,2,1,0:T(8,128)}, u32[]{:S(2)}, u32[]{:S(2)}) collective-permute-start(f32[1,16,256,128]{3,2,1,0:T(8,128)} %param.6), channel_id=1, source_target_pairs={{0,4},{4,8},{8,12},{12,16},{16,20},{20,24},{24,28},{1,5},{5,9},{9,... | collective-permute-start | bytes 6291464 | tf_op jit(solution)/shard_map/ppermute | solution.py:28
  3.9 1.0 fusion.95
  4.9 1.3 collective-permute-start.1
  6.2 4.9 %collective-permute-start.2 = (f32[1,1,256,128]{3,2,1,0:T(8,128)S(1)}, f32[1,1,256,128]{3,2,1,0:T(8,128)S(1)}, u32[]{:S(2)}, u32[]{:S(2)}) collective-permute-start(f32[1,1,256,128]{3,2,1,0:T(8,128)S(1)} %get-tuple-element.21), channel_id=1, source_target_pairs={{0,1},{1,2},{2,3},{4,5},{5,6},{6,7},{8,9},{9,10},{10,11},{12,13},{... | collective-permute-start | bytes 393224 | tf_op jit(solution)/shard_map/ppermute | solution.py:17
  11.1 0.0 copy-done
  11.1 3.4 %convolution_multiply_fusion = f32[4096,128]{1,0:T(8,128)S(1)} fusion(f32[4096,128]{1,0:T(8,128)} %bitcast.61, f32[128,128]{1,0:T(8,128)S(1)} %copy-done, f32[128]{0:T(128)} %param.10), kind=kOutput, calls=%fused_computation.8 | convolution fusion | flops 805830656 | bytes 4260352 | tf_op jit(solution)/shard_map/dot_general | solution.py:72
  14.6 0.0 copy-start.1
  14.6 3.1 %fusion.96 = f32[4096,128]{1,0:T(8,128)} fusion(f32[4096,128]{1,0:T(8,128)S(1)} %convolution_multiply_fusion, f32[128,128]{1,0:T(8,128)S(1)} %copy-done), kind=kOutput, calls=%fused_computation.159 | convolution fusion | flops 805306368 | bytes 4259840 | tf_op jit(solution)/shard_map/dot_general | solution.py:73
  17.7 0.0 copy-start.2
  17.7 0.0 copy-start.3
  17.8 0.0 copy-start.5
  17.8 0.0 collective-permute-done.1
  17.8 0.0 collective-permute-done.2
  17.8 0.0 copy-done.1
  17.8 0.2 select_maximum_fusion
  18.0 0.0 collective-permute-done
  18.0 1.3 copy-done.2
  19.3 0.0 copy-done.3
  19.3 0.6 copy-done.5
  20.0 4.9 %multiply_bitcast_fusion = f32[1,16,256,128]{3,2,1,0:T(8,128)S(1)} fusion(f32[1,16,256,128]{3,2,1,0:T(8,128)S(1)} %copy-done.1, f32[1,18,258,128]{3,2,1,0:T(8,128)S(1)} %select_maximum_fusion, f32[1,1,256,128]{3,2,1,0:T(8,128)S(1)} %collective-permute-done.2, f32[1,1,256,128]{3,2,1,0:T(8,128)S(1)} %collective-permute-done.1, ...), kind=kOutput, calls=%fused_computation.87 | convolution fusion | flops 815792128 | bytes 17121284 | tf_op jit(solution)/shard_map/dot_general | solution.py:82
  24.9 2.5 %copy.10 = f32[1,16,256,128]{3,1,0,2:T(8,128)} copy(f32[1,16,256,128]{3,2,1,0:T(8,128)S(1)} %multiply_bitcast_fusion) | data formatting | bytes 4194304 | tf_op jit(solution)/shard_map/mul | solution.py:86
  27.4 0.0 copy-start.4
  27.4 13.5 %all-to-all-start = ((f32[1,16,256,128]{3,1,0,2:T(8,128)}), f32[1,16,256,128]{3,1,0,2:T(8,128)S(1)}, u32[]{:S(2)}, u32[]{:S(2)}) async-start(f32[1,16,256,128]{3,1,0,2:T(8,128)} %copy.10), calls=%async_computation | async-start | bytes 4194304 | tf_op jit(solution)/shard_map/all_to_all | solution.py:87
  41.0 0.1 broadcast_multiply_fusion
  41.1 0.0 copy-done.4
  41.1 0.1 broadcast_add_fusion
  41.2 26.4 %all-to-all-done = f32[1,16,256,128]{3,1,0,2:T(8,128)S(1)} async-done(((f32[1,16,256,128]{3,1,0,2:T(8,128)}), f32[1,16,256,128]{3,1,0,2:T(8,128)S(1)}, u32[]{:S(2)}, u32[]{:S(2)}) %all-to-all-start) | async-done | bytes 2097184 | tf_op jit(solution)/shard_map/all_to_all | solution.py:87
  67.6 1.9 %copy.15 = f32[1,16,8,32,128]{4,3,1,2,0:T(8,128)} copy(f32[1,16,8,32,128]{4,1,3,2,0:T(8,128)S(1)} %bitcast.62) | data formatting | bytes 4194304 | tf_op jit(solution)/shard_map/all_to_all | solution.py:87
  69.5 2.0 %reshape.165 = f32[8,65536]{1,0:T(8,128)S(1)} reshape(f32[8,1,16,32,128]{4,3,2,0,1:T(8,128)} %bitcast.63) | data formatting | bytes 4194304 | tf_op jit(solution)/shard_map/reshape | solution.py:95
  71.5 1.9 %fusion.69 = f32[8,65536]{1,0:T(8,128)S(1)} fusion(f32[8,65536]{1,0:T(8,128)S(1)} %reshape.165), kind=kOutput, calls=%fused_computation.130 | convolution fusion | flops 50332544 | bytes 4194304 | tf_op jit(solution)/shard_map/dot_general | solution.py:98
  73.4 1.9 %convolution_negate_fusion = f32[8,65536]{1,0:T(8,128)S(1)} fusion(f32[8,65536]{1,0:T(8,128)S(1)} %reshape.165), kind=kOutput, calls=%fused_computation.2 | convolution fusion | flops 50856832 | bytes 4194304 | tf_op jit(solution)/shard_map/dot_general | solution.py:99
  75.3 1.0 fusion.17
  76.4 1.3 collective-permute-start.3
  77.7 1.3 collective-permute-start.4
  79.0 0.0 collective-permute-done.3
  79.0 2.7 %collective-permute-done.4 = f32[2,8,16,1,128]{4,1,3,2,0:T(8,128)S(1)} collective-permute-done((f32[2,8,16,1,128]{4,1,3,2,0:T(8,128)S(1)}, f32[2,8,16,1,128]{4,1,3,2,0:T(8,128)S(1)}, u32[]{:S(2)}, u32[]{:S(2)}) %collective-permute-start.4) | collective-permute-done | bytes 131104 | tf_op jit(solution)/shard_map/ppermute | solution.py:20
  81.7 1.3 collective-permute-start.5
  83.0 4.6 %collective-permute-start.6 = (f32[2,8,1,34,128]{4,1,3,2,0:T(8,128)S(1)}, f32[2,8,1,34,128]{4,1,3,2,0:T(8,128)S(1)}, u32[]{:S(2)}, u32[]{:S(2)}) collective-permute-start(f32[2,8,1,34,128]{4,1,3,2,0:T(8,128)S(1)} %get-tuple-element.10), channel_id=1, source_target_pairs={{0,1},{1,2},{2,3},{4,5},{5,6},{6,7},{8,9},{9,10},{10,11},{12,13},{... | collective-permute-start | bytes 835592 | tf_op jit(solution)/shard_map/ppermute | solution.py:17
  87.6 3.0 %collective-permute-done.5 = f32[2,8,1,34,128]{4,1,3,2,0:T(8,128)S(1)} collective-permute-done((f32[2,8,1,34,128]{4,1,3,2,0:T(8,128)S(1)}, f32[2,8,1,34,128]{4,1,3,2,0:T(8,128)S(1)}, u32[]{:S(2)}, u32[]{:S(2)}) %collective-permute-start.5) | collective-permute-done | bytes 278560 | tf_op jit(solution)/shard_map/ppermute | solution.py:20
  90.6 1.7 %collective-permute-done.6 = f32[2,8,1,34,128]{4,1,3,2,0:T(8,128)S(1)} collective-permute-done((f32[2,8,1,34,128]{4,1,3,2,0:T(8,128)S(1)}, f32[2,8,1,34,128]{4,1,3,2,0:T(8,128)S(1)}, u32[]{:S(2)}, u32[]{:S(2)}) %collective-permute-start.6) | collective-permute-done | bytes 278560 | tf_op jit(solution)/shard_map/ppermute | solution.py:17
  92.3 3.6 %fusion.8 = f32[2,8,16,32,128]{4,1,3,2,0:T(8,128)S(1)} fusion(f32[2,8,16,1,128]{4,1,3,2,0:T(8,128)S(1)} %collective-permute-done.3, f32[1,8,16,32,128]{4,1,3,2,0:T(8,128)S(1)} %get-tuple-element.14, f32[1,8,16,32,128]{4,1,3,2,0:T(8,128)S(1)} %get-tuple-element.13, f32[2,8,16,1,128]{4,1,3,2,0:T(8,128)S(1)} %collective-permute-done.4, ...), kind=kLoop, calls=%fused_computation.29 | loop fusion | flops 18874368 | bytes 13404160 | tf_op jit(solution)/shard_map/add | solution.py:53
  95.9 1.0 fusion.20
  97.0 4.3 %collective-permute-start.7 = (f32[2,8,16,1,128]{4,1,3,2,0:T(8,128)S(1)}, f32[2,8,16,1,128]{4,1,3,2,0:T(8,128)S(1)}, u32[]{:S(2)}, u32[]{:S(2)}) collective-permute-start(f32[2,8,16,1,128]{4,1,3,2,0:T(8,128)S(1)} %get-tuple-element.18), channel_id=1, source_target_pairs={{0,4},{4,8},{8,12},{12,16},{16,20},{20,24},{24,28},{1,5},{5,9},{9,... | collective-permute-start | bytes 393224 | tf_op jit(solution)/shard_map/ppermute | solution.py:17
  101.4 1.3 collective-permute-start.8
  102.7 0.0 collective-permute-done.7
  102.7 3.3 %collective-permute-done.8 = f32[2,8,16,1,128]{4,1,3,2,0:T(8,128)S(1)} collective-permute-done((f32[2,8,16,1,128]{4,1,3,2,0:T(8,128)S(1)}, f32[2,8,16,1,128]{4,1,3,2,0:T(8,128)S(1)}, u32[]{:S(2)}, u32[]{:S(2)}) %collective-permute-start.8) | collective-permute-done | bytes 131104 | tf_op jit(solution)/shard_map/ppermute | solution.py:20
  106.0 4.4 %collective-permute-start.10 = (f32[2,8,1,34,128]{4,1,3,2,0:T(8,128)S(1)}, f32[2,8,1,34,128]{4,1,3,2,0:T(8,128)S(1)}, u32[]{:S(2)}, u32[]{:S(2)}) collective-permute-start(f32[2,8,1,34,128]{4,1,3,2,0:T(8,128)S(1)} %get-tuple-element.8), channel_id=1, source_target_pairs={{0,1},{1,2},{2,3},{4,5},{5,6},{6,7},{8,9},{9,10},{10,11},{12,13},{... | collective-permute-start | bytes 835592 | tf_op jit(solution)/shard_map/ppermute | solution.py:17
  110.5 1.5 collective-permute-start.9
  112.0 2.9 %collective-permute-done.10 = f32[2,8,1,34,128]{4,1,3,2,0:T(8,128)S(1)} collective-permute-done((f32[2,8,1,34,128]{4,1,3,2,0:T(8,128)S(1)}, f32[2,8,1,34,128]{4,1,3,2,0:T(8,128)S(1)}, u32[]{:S(2)}, u32[]{:S(2)}) %collective-permute-start.10) | collective-permute-done | bytes 278560 | tf_op jit(solution)/shard_map/ppermute | solution.py:17
  114.9 4.7 %collective-permute-done.9 = f32[2,8,1,34,128]{4,1,3,2,0:T(8,128)S(1)} collective-permute-done((f32[2,8,1,34,128]{4,1,3,2,0:T(8,128)S(1)}, f32[2,8,1,34,128]{4,1,3,2,0:T(8,128)S(1)}, u32[]{:S(2)}, u32[]{:S(2)}) %collective-permute-start.9) | collective-permute-done | bytes 278560 | tf_op jit(solution)/shard_map/ppermute | solution.py:20
  119.6 3.6 %fusion.3 = f32[2,8,16,32,128]{4,1,3,2,0:T(8,128)S(1)} fusion(f32[2,8,16,1,128]{4,1,3,2,0:T(8,128)S(1)} %collective-permute-done.7, f32[1,8,16,32,128]{4,1,3,2,0:T(8,128)S(1)} %get-tuple-element.12, f32[1,8,16,32,128]{4,1,3,2,0:T(8,128)S(1)} %get-tuple-element.11, f32[2,8,16,1,128]{4,1,3,2,0:T(8,128)S(1)} %collective-permute-done.8, ...), kind=kLoop, calls=%fused_computation.12 | loop fusion | flops 18874368 | bytes 13404160 | tf_op jit(solution)/shard_map/add | solution.py:53
  123.2 0.3 fusion.94
  123.5 0.1 add.208
  123.6 0.2 add.206
  123.8 2.2 %fusion.36 = f32[8,65536]{1,0:T(8,128)S(1)} fusion(f32[8,65536]{1,0:T(8,128)S(1)} %bitcast.72, f32[8,65536]{1,0:T(8,128)S(1)} %bitcast.70, f32[8,65536]{1,0:T(8,128)S(1)} %bitcast.67, f32[8]{0:T(128)S(1)} %get-tuple-element.24, f32[8]{0:T(128)S(1)} %get-tuple-element.23, f32[65536]{0:T(1024)S(1)} %bitcast.74), kind=kOutput, calls=%fused_computation.81 | convolution fusion | flops 54002560 | bytes 8650816 | tf_op jit(solution)/shard_map/dot_general | solution.py:114
  126.1 2.4 %fusion = f32[8,65536]{1,0:T(8,128)S(1)} fusion(f32[8,65536]{1,0:T(8,128)S(1)} %fusion.36, f32[8,65536]{1,0:T(8,128)S(1)} %bitcast.71, f32[8,65536]{1,0:T(8,128)S(1)} %bitcast.73, f32[8,65536]{1,0:T(8,128)S(1)} %bitcast.68, f32[8]{0:T(128)S(1)} %exponential_multiply_fusion, f32[8]{0:T(128)S(1)} %get-tuple-element.24, f32[8]{0:T(128)S(1)} %get-tuple-element.23, ...), kind=kOutput, calls=%fused_computation.1 | convolution fusion | flops 55051136 | bytes 10748000 | tf_op jit(solution)/shard_map/dot_general | solution.py:114
  128.5 0.4 copy.12
  128.9 32.7 %all_to_all.30 = f32[8,16,32,128]{3,2,1,0:T(8,128)S(1)} all-to-all(f32[8,16,32,128]{3,2,1,0:T(8,128)S(1)} %copy.12), channel_id=1, replica_groups=mesh['tm'=8,'tx'=4] {'tm'}, dimensions={0} | all-to-all | bytes 4194304 | tf_op jit(solution)/shard_map/all_to_all | solution.py:117
  161.5 0.2 copy.13
  161.8 3.1 %convolution_bitcast_fusion = f32[1,16,256,128]{3,2,1,0:T(8,128)} fusion(f32[16,256,128]{2,1,0:T(8,128)S(1)} %bitcast.65, f32[128,128]{1,0:T(8,128)S(1)} %copy-done), kind=kOutput, calls=%fused_computation.91 | convolution fusion | flops 805306368 | bytes 4259840 | tf_op jit(solution)/shard_map/dot_general | solution.py:120
  (7 shorter events, 0.2 us)
Async XLA Ops:
  0.0 11.1 %copy-start = (f32[128,128]{1,0:T(8,128)S(1)}, f32[128,128]{1,0:T(8,128)}, u32[]{:S(2)}) copy-start(f32[128,128]{1,0:T(8,128)} %param.11) | copy-start | bytes 196612
  0.0 18.0 %collective-permute-start = (f32[1,16,256,128]{3,2,1,0:T(8,128)}, f32[1,16,256,128]{3,2,1,0:T(8,128)}, u32[]{:S(2)}, u32[]{:S(2)}) collective-permute-start(f32[1,16,256,128]{3,2,1,0:T(8,128)} %param.6), channel_id=1, source_target_pairs={{0,4},{4,8},{8,12},{12,16},{16,20},{20,24},{24,28},{1,5},{5,9},{9,... | collective-permute-start | bytes 6291464 | tf_op jit(solution)/shard_map/ppermute | solution.py:28
  4.9 12.9 %collective-permute-start.1 = (f32[1,1,256,128]{3,2,1,0:T(8,128)S(1)}, f32[1,1,256,128]{3,2,1,0:T(8,128)S(1)}, u32[]{:S(2)}, u32[]{:S(2)}) collective-permute-start(f32[1,1,256,128]{3,2,1,0:T(8,128)S(1)} %get-tuple-element.22), channel_id=1, source_target_pairs={{1,0},{2,1},{3,2},{5,4},{6,5},{7,6},{9,8},{10,9},{11,10},{13,12},{... | collective-permute-start | bytes 393224 | tf_op jit(solution)/shard_map/ppermute | solution.py:20
  6.2 11.6 %collective-permute-start.2 = (f32[1,1,256,128]{3,2,1,0:T(8,128)S(1)}, f32[1,1,256,128]{3,2,1,0:T(8,128)S(1)}, u32[]{:S(2)}, u32[]{:S(2)}) collective-permute-start(f32[1,1,256,128]{3,2,1,0:T(8,128)S(1)} %get-tuple-element.21), channel_id=1, source_target_pairs={{0,1},{1,2},{2,3},{4,5},{5,6},{6,7},{8,9},{9,10},{10,11},{12,13},{... | collective-permute-start | bytes 393224 | tf_op jit(solution)/shard_map/ppermute | solution.py:17
  14.6 3.2 %copy-start.1 = (f32[1,16,256,128]{3,2,1,0:T(8,128)S(1)}, f32[1,16,256,128]{3,2,1,0:T(8,128)}, u32[]{:S(2)}) copy-start(f32[1,16,256,128]{3,2,1,0:T(8,128)} %param.6) | copy-start | bytes 6291460
  17.7 1.6 copy-start.2
  17.7 1.6 copy-start.3
  17.8 2.2 %copy-start.5 = (f32[1,16,256,128]{3,2,1,0:T(8,128)S(1)}, f32[1,16,256,128]{3,2,1,0:T(8,128)}, u32[]{:S(2)}) copy-start(f32[1,16,256,128]{3,2,1,0:T(8,128)} %param.7) | copy-start | bytes 6291460
  27.4 13.7 %copy-start.4 = (f32[128]{0:T(128)S(1)}, f32[128]{0:T(128)}, u32[]{:S(2)}) copy-start(f32[128]{0:T(128)} %param.10) | copy-start | bytes 1540
  27.4 40.1 %all-to-all-start = ((f32[1,16,256,128]{3,1,0,2:T(8,128)}), f32[1,16,256,128]{3,1,0,2:T(8,128)S(1)}, u32[]{:S(2)}, u32[]{:S(2)}) async-start(f32[1,16,256,128]{3,1,0,2:T(8,128)} %copy.10), calls=%async_computation | async-start | bytes 4194304 | tf_op jit(solution)/shard_map/all_to_all | solution.py:87
  76.4 2.6 %collective-permute-start.3 = (f32[2,8,16,1,128]{4,1,3,2,0:T(8,128)S(1)}, f32[2,8,16,1,128]{4,1,3,2,0:T(8,128)S(1)}, u32[]{:S(2)}, u32[]{:S(2)}) collective-permute-start(f32[2,8,16,1,128]{4,1,3,2,0:T(8,128)S(1)} %get-tuple-element.20), channel_id=1, source_target_pairs={{0,4},{4,8},{8,12},{12,16},{16,20},{20,24},{24,28},{1,5},{5,9},{9,... | collective-permute-start | bytes 393224 | tf_op jit(solution)/shard_map/ppermute | solution.py:17
  77.7 4.0 %collective-permute-start.4 = (f32[2,8,16,1,128]{4,1,3,2,0:T(8,128)S(1)}, f32[2,8,16,1,128]{4,1,3,2,0:T(8,128)S(1)}, u32[]{:S(2)}, u32[]{:S(2)}) collective-permute-start(f32[2,8,16,1,128]{4,1,3,2,0:T(8,128)S(1)} %get-tuple-element.19), channel_id=1, source_target_pairs={{4,0},{8,4},{12,8},{16,12},{20,16},{24,20},{28,24},{5,1},{9,5},{13... | collective-permute-start | bytes 393224 | tf_op jit(solution)/shard_map/ppermute | solution.py:20
  81.7 8.9 %collective-permute-start.5 = (f32[2,8,1,34,128]{4,1,3,2,0:T(8,128)S(1)}, f32[2,8,1,34,128]{4,1,3,2,0:T(8,128)S(1)}, u32[]{:S(2)}, u32[]{:S(2)}) collective-permute-start(f32[2,8,1,34,128]{4,1,3,2,0:T(8,128)S(1)} %get-tuple-element.9), channel_id=1, source_target_pairs={{1,0},{2,1},{3,2},{5,4},{6,5},{7,6},{9,8},{10,9},{11,10},{13,12},{... | collective-permute-start | bytes 835592 | tf_op jit(solution)/shard_map/ppermute | solution.py:20
  83.0 9.3 %collective-permute-start.6 = (f32[2,8,1,34,128]{4,1,3,2,0:T(8,128)S(1)}, f32[2,8,1,34,128]{4,1,3,2,0:T(8,128)S(1)}, u32[]{:S(2)}, u32[]{:S(2)}) collective-permute-start(f32[2,8,1,34,128]{4,1,3,2,0:T(8,128)S(1)} %get-tuple-element.10), channel_id=1, source_target_pairs={{0,1},{1,2},{2,3},{4,5},{5,6},{6,7},{8,9},{9,10},{10,11},{12,13},{... | collective-permute-start | bytes 835592 | tf_op jit(solution)/shard_map/ppermute | solution.py:17
  97.0 5.6 %collective-permute-start.7 = (f32[2,8,16,1,128]{4,1,3,2,0:T(8,128)S(1)}, f32[2,8,16,1,128]{4,1,3,2,0:T(8,128)S(1)}, u32[]{:S(2)}, u32[]{:S(2)}) collective-permute-start(f32[2,8,16,1,128]{4,1,3,2,0:T(8,128)S(1)} %get-tuple-element.18), channel_id=1, source_target_pairs={{0,4},{4,8},{8,12},{12,16},{16,20},{20,24},{24,28},{1,5},{5,9},{9,... | collective-permute-start | bytes 393224 | tf_op jit(solution)/shard_map/ppermute | solution.py:17
  101.4 4.6 %collective-permute-start.8 = (f32[2,8,16,1,128]{4,1,3,2,0:T(8,128)S(1)}, f32[2,8,16,1,128]{4,1,3,2,0:T(8,128)S(1)}, u32[]{:S(2)}, u32[]{:S(2)}) collective-permute-start(f32[2,8,16,1,128]{4,1,3,2,0:T(8,128)S(1)} %get-tuple-element.17), channel_id=1, source_target_pairs={{4,0},{8,4},{12,8},{16,12},{20,16},{24,20},{28,24},{5,1},{9,5},{13... | collective-permute-start | bytes 393224 | tf_op jit(solution)/shard_map/ppermute | solution.py:20
  106.0 8.9 %collective-permute-start.10 = (f32[2,8,1,34,128]{4,1,3,2,0:T(8,128)S(1)}, f32[2,8,1,34,128]{4,1,3,2,0:T(8,128)S(1)}, u32[]{:S(2)}, u32[]{:S(2)}) collective-permute-start(f32[2,8,1,34,128]{4,1,3,2,0:T(8,128)S(1)} %get-tuple-element.8), channel_id=1, source_target_pairs={{0,1},{1,2},{2,3},{4,5},{5,6},{6,7},{8,9},{9,10},{10,11},{12,13},{... | collective-permute-start | bytes 835592 | tf_op jit(solution)/shard_map/ppermute | solution.py:17
  110.5 9.1 %collective-permute-start.9 = (f32[2,8,1,34,128]{4,1,3,2,0:T(8,128)S(1)}, f32[2,8,1,34,128]{4,1,3,2,0:T(8,128)S(1)}, u32[]{:S(2)}, u32[]{:S(2)}) collective-permute-start(f32[2,8,1,34,128]{4,1,3,2,0:T(8,128)S(1)} %get-tuple-element.7), channel_id=1, source_target_pairs={{1,0},{2,1},{3,2},{5,4},{6,5},{7,6},{9,8},{10,9},{11,10},{13,12},{... | collective-permute-start | bytes 835592 | tf_op jit(solution)/shard_map/ppermute | solution.py:20
where the time goes:
time: 166 us; the launch traced here: 165 us
  waiting for transfers between devices  44.7 us (27%)
  starting transfers between devices  43.6 us (26%)
  blocking collectives  32.7 us (20%)
  matrix products  23 us (14%)
  local copies, waits for them, and re-layouts  10.7 us (6%)
  other arithmetic  9.89 us (6%)
    all_to_all x1, blocking collectives, on_device(): lax.all_to_all(times.reshape(gathered.shape), 'tm', split_axis=0, concat_...  32.7 us
    all_to_all x1, waiting for transfers between devices, on_device(): lax.all_to_all(scaled, 'tm', split_axis=2, concat_axis=0, tiled=True)  26.4 us
    ppermute x5, starting transfers between devices, extended(): lax.ppermute(lax.slice_in_dim(block, block.shape[dim] - width, None, axis...  19.5 us
    ppermute x5, waiting for transfers between devices, extended(): lax.ppermute(lax.slice_in_dim(block, 0, width, axis=dim), axis, backward)  13.7 us
    all_to_all x1, starting transfers between devices, on_device(): lax.all_to_all(scaled, 'tm', split_axis=2, concat_axis=0, tiled=True)  13.5 us
    add x2, other arithmetic, relax(): field = divide(source + kappa_b * rims(field))  7.25 us
    ppermute x5, starting transfers between devices, extended(): lax.ppermute(lax.slice_in_dim(block, 0, width, axis=dim), axis, backward)  6.68 us
    dot_general x1, matrix products, on_device(): jnp.dot(residual.reshape(-1, column_size), basis, precision=highest)  4.88 us
  transfers between devices with their start and end apart: 12, of which 7 were waited for; matrix products, arithmetic and copies ran while one was open for 5% of the time, Pallas kernels for 0%

commit v1 on v0

v1 whole, which is shorter than its diff:
```python
import functools

import jax
import jax.numpy as jnp
from jax import lax
from jax.experimental import pallas as pl
from jax.experimental.pallas import tpu as pltpu
from jax.sharding import PartitionSpec as P


ALPHA = 0.05
REACH = 2
F32 = jnp.float32
BF16 = jnp.bfloat16
MIB = 2**20


def split(value):
    high = value.astype(BF16)
    return high, (value - high.astype(F32)).astype(BF16)


def dot(left, right):
    return jnp.dot(left, right, preferred_element_type=F32)


def shifted(array, axis, by):
    count = lax.axis_size(axis)
    pairs = [(i, i + by) for i in range(count) if 0 <= i + by < count]
    return lax.ppermute(array, axis, pairs)


def cut(value, rows, out, base, blocks):
    size = value.shape[0]
    block = size // blocks
    tall = block + 2 * REACH
    rows[pl.ds(REACH, size), :] = value
    for target in range(blocks):
        out[target, pl.ds(base, tall), :] = rows[pl.ds(block * target, tall), :]


def fill_weights(weights, first_half, second_half):
    depth = first_half.shape[0]
    first_high, first_low = split(first_half)
    weights[:depth, :depth] = first_high
    weights[:depth, depth:] = first_low
    if second_half is None:
        weights[depth:, :depth] = first_high
        weights[depth:, depth:] = jnp.zeros_like(first_low)
    else:
        second_high, second_low = split(second_half)
        weights[depth:, :depth] = second_high
        weights[depth:, depth:] = second_low


def times_matrix(value, weights):
    depth = value.shape[1]
    wide = dot(jnp.concatenate(split(value), axis=1), weights[...])
    return wide[:, :depth] + wide[:, depth:]


def residual_kernel(
    blocks, inner, state, other, initial, force, low, high, kappa, rates, basis, out,
    here, past, pushed, parts, rows, levels, turned, weights, loads, stores,
):
    columns, size, depth = state.shape
    tall = size // blocks + 2 * REACH
    step_here = lax.axis_index("tm")
    odd = step_here % 2 == 1
    first = step_here == 0
    if inner:
        mine = list(range(2, columns - 2))
        wide = list(range(1, columns - 1))
    else:
        mine = [0, 1, columns - 2, columns - 1]
        wide = [0, 1, 2, columns - 3, columns - 2, columns - 1]

    def load(kind, x):
        source, target = ((state, here), (other, past), (force, pushed))[kind]
        return pltpu.make_async_copy(source.at[x], target.at[x], loads.at[kind, x])

    for x in wide:
        load(0, x).start()
        if x in mine:
            load(2, x).start()

            @pl.when(odd)
            def _():
                load(1, x).start()

            @pl.when(first)
            def _():
                pltpu.make_async_copy(initial.at[x], past.at[x], loads.at[1, x]).start()

    plain = basis[...]
    fill_weights(weights, plain, -plain * rates[...])
    rows[...] = jnp.zeros_like(rows)
    index = lax.broadcasted_iota(jnp.int32, (size, depth), 0)
    levels[...] = jnp.zeros_like(levels)
    levels[:columns, :] = kappa[...]
    for part in range(size // depth):
        where = pl.ds(part * depth, depth)
        turned[where, :] = jnp.transpose(levels[:, where])

    def column(x, left, right, base):
        load(2, x).wait()

        @pl.when(jnp.logical_or(odd, first))
        def _():
            load(1, x).wait()

        center = here[x]
        up = jnp.where(index == 0, 0.0, pltpu.roll(center, 1, 0))
        down = jnp.where(index == size - 1, 0.0, pltpu.roll(center, size - 1, 0))
        square = center * center
        beside = left + right + up + down
        across = jnp.broadcast_to(pltpu.roll(turned[...], (depth - x) % depth, 1)[:, :1], (size, depth))
        value = (
            pushed[x]
            - center
            + jnp.where(jnp.logical_or(odd, first), past[x], 0.0)
            - across * (4.0 * center - beside)
            - 0.5 * (square * center) / (1.0 + square)
        )
        value_high, value_low = split(value)
        center_high, center_low = split(center)
        joined_high = jnp.concatenate([value_high, center_high], axis=1)
        joined_low = jnp.concatenate([value_low, center_low], axis=1)
        product = dot(joined_high, weights[...])
        modal = product[:, :depth] + product[:, depth:] + dot(joined_low, weights[:, :depth])
        cut(modal, rows, parts, base, blocks)

    def store(step):
        where = pl.ds(pl.multiple_of(step * 2 * tall, 8), 2 * tall)
        return pltpu.make_async_copy(parts.at[:, where, :], out.at[:, where, :], stores.at[step])

    if inner:
        load(0, 1).wait()
        load(0, 2).wait()

        def pair(step, carry):
            base = pl.multiple_of(step * 2 * tall, 8)
            for which in range(2):
                x = 2 + 2 * step + which
                load(0, x + 1).wait()
                column(x, here[x - 1], here[x + 1], base + which * tall)
            store(step).start()
            return carry

        lax.fori_loop(0, len(mine) // 2, pair, 0)
    else:
        for x in wide:
            load(0, x).wait()
        column(0, low[:size, :], here[1], 0)
        column(1, here[0], here[2], tall)
        store(0).start()
        column(columns - 2, here[columns - 3], here[columns - 1], 2 * tall)
        column(columns - 1, here[columns - 2], high[:size, :], 3 * tall)
        store(1).start()
    for step in range(len(mine) // 2):
        store(step).wait()


def prepare_kernel(
    block, count, edge, state, other, kappa, rates, basis, *rest
):
    pieces, shared = rest[:count], rest[count : 2 * count]
    modal, inverse, ending, low, high, near, far, strip, gathered, weights, loads = rest[2 * count :]
    columns, window, depth = far.shape[1:]
    broad = near.shape[1]
    chips = count + 1
    steps = 2 * chips
    size = block * steps
    tall = block + 2 * REACH
    two = REACH * tall
    room = (strip.shape[0] - broad) // 2
    here = lax.axis_index("tm")
    chip = here // 2
    odd = here % 2 == 1
    near_start = pl.multiple_of(near_begin(chip, block, broad, size), 8)

    @pl.when(odd)
    def _():
        pltpu.make_async_copy(state.at[:, pl.ds(near_start, broad), :], near, loads.at[count]).start()
        for by in range(count):
            pltpu.make_async_copy(pieces[by], far.at[by], loads.at[by]).start()

    @pl.when(jnp.logical_not(odd))
    def _():
        pltpu.make_async_copy(other.at[:, pl.ds(near_start, broad), :], near, loads.at[count]).start()
        for by in range(count):
            pltpu.make_async_copy(shared[by], far.at[by], loads.at[by]).start()

    fill_weights(weights, basis[...], None)
    total = kappa.shape[0]
    chunk = 2 * tall

    def factors(step, carry):
        base = pl.multiple_of(step * chunk, 8)
        inv = 1.0 / (1.0 + rates[...] + 4.0 * kappa[pl.ds(base, chunk), :])
        inverse[pl.ds(base, chunk), :] = inv
        power = inv
        for _ in range(steps - 1):
            power = power * inv
        ending[pl.ds(base, chunk), :] = ALPHA / (1.0 - ALPHA * power)
        return carry

    lax.fori_loop(0, total // chunk, factors, 0)
    strip[...] = jnp.zeros_like(strip)
    begin = block * here - REACH + room

    def slot(source, start, extent, index):
        strip[room + extent :, :] = jnp.zeros((strip.shape[0] - room - extent, depth), F32)
        for x in range(columns):
            strip[pl.ds(room, extent), :] = source(x)
            gathered[pl.ds(x * tall, tall), :] = strip[pl.ds(begin - start, tall), :]
        modal[index] = times_matrix(gathered[...], weights)

    pltpu.make_async_copy(state.at[:, pl.ds(near_start, broad), :], near, loads.at[count]).wait()
    slot(lambda x: near[x], near_start, broad, chip)
    far_start = window_start(chip, block, window, size)

    def far_slot(by, carry):
        pltpu.make_async_copy(pieces[0], far.at[by], loads.at[by]).wait()
        slot(lambda x: far[by, x], far_start, window, (chip - by - 1 + chips) % chips)
        return carry

    lax.fori_loop(0, count, far_slot, 0)
    whole = columns * tall
    for n in range(steps):
        left = edge[n, :two, :]
        right = edge[n, two:, :]
        if n and n % 2 == 0:
            left = left + modal[n // 2 - 1, :two, :]
            right = right + modal[n // 2 - 1, whole - two :, :]
        low[n] = left
        high[n] = right


def relax_kernel(
    block, middle, edge_low, edge_high, left, right, modal_far, kappa_far, inverse_far, ending_far, basis, out,
    known, source, older, newer, gathered, weights, modal, kappa, inverse, ending, made_out, loads, stores,
):
    steps, inner, depth = middle.shape
    tall = block + 2 * REACH
    chunk = REACH * tall
    columns = inner // tall + 2 * REACH
    total = inner + 4 * chunk
    pad = older.shape[1] - total
    front = pad // 2
    copies = [
        (inverse_far, inverse),
        (ending_far, ending),
        (left, known.at[:, pl.ds(0, chunk), :]),
        (edge_low, known.at[:, pl.ds(chunk, chunk), :]),
        (edge_high, known.at[:, pl.ds(total - 2 * chunk, chunk), :]),
        (right, known.at[:, pl.ds(total - chunk, chunk), :]),
        (modal_far, modal),
        (kappa_far, kappa),
        (middle, known.at[:, pl.ds(2 * chunk, inner), :]),
    ]
    copies = [pltpu.make_async_copy(*ends, loads.at[i]) for i, ends in enumerate(copies)]
    for copy in copies:
        copy.start()
    fill_weights(weights, jnp.transpose(basis[...]), None)
    older[:, :front, :] = jnp.zeros((steps, front, depth), F32)
    older[:, front + total :, :] = jnp.zeros((steps, pad - front, depth), F32)

    def solve(values, inv, end):
        last = values(0) * inv
        for n in range(1, steps):
            last = (values(n) + last) * inv
        return end * last

    def first(value, base):
        inv = inverse[pl.ds(base, chunk), :]
        run = solve(value, inv, ending[pl.ds(base, chunk), :])
        for n in range(steps):
            run = (known[n, pl.ds(base, chunk), :] + run) * inv
            older[n, pl.ds(base + front, chunk), :] = run

    for copy in copies:
        copy.wait()
    for base in (0, chunk, total - 2 * chunk, total - chunk):
        first(lambda n: known[n, pl.ds(base, chunk), :], base)

    def first_middle(step, carry):
        at = pl.multiple_of(step * chunk, 8)
        base = pl.multiple_of(at + 2 * chunk, 8)

        def value(n):
            made = known[n, pl.ds(base, chunk), :]
            if n and n % 2 == 0:
                made = made + modal[n // 2 - 1, pl.ds(at + chunk, chunk), :]
                known[n, pl.ds(base, chunk), :] = made
            return made

        first(value, base)
        return carry

    lax.fori_loop(0, inner // chunk, first_middle, 0)

    def term(field, base, size, n):
        beside = (
            field[n, pl.ds(base + front - 1, size), :]
            + field[n, pl.ds(base + front + 1, size), :]
            + field[n, pl.ds(base + front - tall, size), :]
            + field[n, pl.ds(base + front + tall, size), :]
        )
        return known[n, pl.ds(base, size), :] + kappa[pl.ds(base, size), :] * beside

    def second(step, carry):
        base = pl.multiple_of(step * chunk, 8) + tall
        inv = inverse[pl.ds(base, chunk), :]

        def value(n):
            made = term(older, base, chunk, n)
            source[n, :chunk, :] = made
            return made

        run = solve(value, inv, ending[pl.ds(base, chunk), :])
        for n in range(steps):
            run = (source[n, :chunk, :] + run) * inv
            newer[n, pl.ds(base + front, chunk), :] = run
        return carry

    lax.fori_loop(0, (columns + 2) // 2, second, 0)

    def third(base):
        inv = inverse[pl.ds(base, block), :]

        def value(n):
            made = term(newer, base, block, n)
            source[n, :block, :] = made
            return made

        run = solve(value, inv, ending[pl.ds(base, block), :])
        for n in range(steps):
            run = (source[n, :block, :] + run) * inv
            gathered[pl.ds(n * block, block), :] = run
        gathered[...] = times_matrix(gathered[...], weights)

    def third_pair(step, carry):
        at = pl.multiple_of(step * 2 * tall, 8)
        to = pl.multiple_of(step * 2 * block, 8)
        for which in range(2):
            third(at + chunk + which * tall + REACH)
            for n in range(steps):
                made_out[n, pl.ds(to + which * block, block), :] = gathered[pl.ds(n * block, block), :]
        store(step).start()
        return carry

    def store(step):
        where = pl.ds(pl.multiple_of(step * 2 * block, 8), 2 * block)
        return pltpu.make_async_copy(made_out.at[:, where, :], out.at[:, where, :], stores.at[step])

    lax.fori_loop(0, columns // 2, third_pair, 0)
    for step in range(columns // 2):
        store(step).wait()


SPACES = {"v": pltpu.VMEM, "h": pltpu.HBM}


def call(kernel, outs, spaces, scratch, flops, *operands):
    shapes = [jax.ShapeDtypeStruct(shape, F32) for shape, _ in outs]
    return pl.pallas_call(
        kernel,
        out_shape=shapes,
        in_specs=[pl.BlockSpec(memory_space=SPACES[space]) for space in spaces],
        out_specs=[pl.BlockSpec(memory_space=SPACES[space]) for _, space in outs],
        scratch_shapes=scratch,
        cost_estimate=pl.CostEstimate(flops=flops, bytes_accessed=10**6, transcendentals=0),
        compiler_params=pltpu.CompilerParams(vmem_limit_bytes=60 * MIB),
    )(*operands)


def paired(array, odd_only=False):
    count = lax.axis_size("tm")
    return lax.ppermute(array, "tm", [(i, i ^ 1) for i in range(count) if i % 2 or not odd_only])


def exchanged(array):
    return lax.all_to_all(array, "tm", split_axis=0, concat_axis=0, tiled=True)


def window_start(chip, block, window, size):
    return jnp.clip(2 * block * chip - 4, 0, size - window)


def near_begin(chip, block, broad, size):
    return jnp.clip(2 * block * chip - 8, 0, size - broad)


def spread(mine, chip, chips, block, window, by):
    start = window_start((chip + by) % chips, block, window, mine.shape[1])
    rows = lax.dynamic_slice_in_dim(mine, start, window, 1)
    count = 2 * chips
    return lax.ppermute(rows, "tm", [(i, (i + 2 * by) % count) for i in range(1, count - 1, 2)])


def correction(state, force, u_init, kappa, rates, basis):
    steps = lax.axis_size("tm")
    here = lax.axis_index("tm")
    chips = steps // 2
    chip = here // 2
    columns, size, depth = u_init.shape
    block = size // steps
    tall = block + 2 * REACH
    chunk = REACH * tall
    window = 2 * block + 8
    broad = 2 * block + 16
    total = columns * tall + 2 * chunk
    front = (tall + 15) // 8 * 8
    square = pltpu.VMEM((2 * depth, 2 * depth), BF16)
    mine = state[0]
    other = paired(mine)
    folded = kappa.reshape(columns, size // depth, depth)
    room = jnp.zeros((-(REACH * size // depth) % 8, depth), F32)

    def bundle(column, coefficients):
        return jnp.concatenate([column, coefficients.reshape(-1, depth), room], axis=0)

    low = shifted(bundle(mine[-1], folded[-REACH:]), "tx", 1)
    high = shifted(bundle(mine[0], folded[:REACH]), "tx", -1)
    rates_row = rates.reshape(1, depth)
    pieces = []
    for by in range(1, chips):
        pieces.append(spread(mine, chip, chips, block, window, by))

    def residual(inner, count, flops):
        return call(
            functools.partial(residual_kernel, steps, inner),
            [((steps, count * tall, depth), "h")],
            "hhhhvvvvv",
            [
                pltpu.VMEM(u_init.shape, F32),
                pltpu.VMEM(u_init.shape, F32),
                pltpu.VMEM(u_init.shape, F32),
                pltpu.VMEM((steps, count * tall, depth), F32),
                pltpu.VMEM((size + 8, depth), F32),
                pltpu.VMEM((depth, size), F32),
                pltpu.VMEM((size, depth), F32),
                square,
                pltpu.SemaphoreType.DMA((3, columns)),
                pltpu.SemaphoreType.DMA((count // 2,)),
            ],
            flops,
            mine, other, u_init, force[0], low, high, kappa, rates_row, basis,
        )[0]

    edge = residual(False, 2 * REACH, 2 * 10**9)
    edge = exchanged(edge)
    middle = residual(True, columns - 2 * REACH, 6 * 10**9)
    middle = exchanged(middle)
    shared = []
    for by in range(1, chips):
        shared.append(paired(pieces[by - 1], odd_only=True))
    ends = [array[size : size + REACH * size // depth].reshape(REACH, size) for array in (low, high)]
    kappa_wide = jnp.pad(jnp.concatenate([ends[0], kappa, ends[1]], axis=0), ((0, 0), (REACH, REACH)))
    kappa_mine = lax.dynamic_slice_in_dim(kappa_wide, here * block, tall, 1)
    kappa_cells = jnp.broadcast_to(kappa_mine[:, :, None], kappa_mine.shape + (depth,)).reshape(-1, depth)
    modal, inverse, ending, edge_low, edge_high = call(
        functools.partial(prepare_kernel, block, chips - 1),
        [
            ((chips, columns * tall, depth), "v"),
            ((total, depth), "v"),
            ((total, depth), "v"),
            ((steps, chunk, depth), "v"),
            ((steps, chunk, depth), "v"),
        ],
        "vhhvvv" + "h" * (2 * chips - 2),
        [
            pltpu.VMEM((columns, broad, depth), F32),
            pltpu.VMEM((chips - 1, columns, window, depth), F32),
            pltpu.VMEM((broad + 16, depth), F32),
            pltpu.VMEM((columns * tall, depth), F32),
            square,
            pltpu.SemaphoreType.DMA((chips,)),
        ],
        10**9,
        edge, mine, other, kappa_cells, rates_row, basis, *pieces, *shared,
    )
    left = shifted(edge_high, "tx", 1)
    right = shifted(edge_low, "tx", -1)
    back = call(
        functools.partial(relax_kernel, block),
        [((steps, columns * block, depth), "h")],
        "hhhhhhhhhv",
        [
            pltpu.VMEM((steps, total, depth), F32),
            pltpu.VMEM((steps, chunk, depth), F32),
            pltpu.VMEM((steps, total + 2 * front, depth), F32),
            pltpu.VMEM((steps, total + 2 * front, depth), F32),
            pltpu.VMEM((steps * block, depth), F32),
            square,
            pltpu.VMEM((chips, columns * tall, depth), F32),
            pltpu.VMEM((total, depth), F32),
            pltpu.VMEM((total, depth), F32),
            pltpu.VMEM((total, depth), F32),
            pltpu.VMEM((steps, columns * block, depth), F32),
            pltpu.SemaphoreType.DMA((9,)),
            pltpu.SemaphoreType.DMA((columns // 2,)),
        ],
        10**9,
        middle, edge_low, edge_high, left, right, modal, kappa_cells, inverse, ending, basis,
    )[0]
    arrived = exchanged(back).reshape(steps, columns, block, depth)
    return jnp.transpose(arrived, (1, 0, 2, 3)).reshape(1, columns, size, depth)


def solution(mesh):
    return jax.shard_map(
        correction,
        mesh=mesh,
        in_specs=(
            P("tm", "tx", None, None),
            P("tm", "tx", None, None),
            P("tx", None, None),
            P("tx", None),
            P(),
            P(),
        ),
        out_specs=P("tm", "tx", None, None),
        check_vma=False,
    )
```

time: 166 us -> 113 us (0.68)
  waiting for transfers between devices: 44.7 us -> 12.9 us
  Pallas kernels: 0 us -> 26.4 us
  matrix products: 23 us -> 0 us
  starting transfers between devices: 43.6 us -> 31.4 us
  other arithmetic: 9.89 us -> 0.2 us
  blocking collectives: 32.7 us -> 30.7 us
    pallas_call x0 -> x4, Pallas kernels: none -> 26.4 us  [call(): pl.pallas_call(kernel, out_shape=shapes, in_specs=[pl.BlockSpec(memory_sp...]
    all_to_all x1 -> x2, waiting for transfers between devices: 26.4 us -> 1.95 us  [exchanged(): return lax.all_to_all(array, 'tm', split_axis=0, concat_axis=0, tiled=True)]
    dot_general x8 -> x0, matrix products: 23 us -> none  [the longest x1 4.88 us: on_device(): jnp.dot(residual.reshape(-1, column_size), basis, precision=highest)]
    ppermute x11, starting transfers between devices: 30.1 us -> 20.3 us  [the longest x4 12.3 us: shifted(): return lax.ppermute(array, axis, pairs)]
    ppermute x11, waiting for transfers between devices: 18.3 us -> 10.9 us  [the longest x4 6.6 us: shifted(): return lax.ppermute(array, axis, pairs)]
    add x3 -> x0, other arithmetic: 7.32 us -> none  [the longest x2 7.25 us: relax(): field = divide(source + kappa_b * rims(field))]
    dynamic_slice x0 -> x1, local copies, waits for them, and re-layouts: none -> 2.76 us  [spread(): rows = lax.dynamic_slice_in_dim(mine, start, window, 1)]
    mul x1 -> x0, local copies, waits for them, and re-layouts: 2.54 us -> none  [on_device(): scaled = modal * jnp.exp(decay * here.astype(jnp.float32))]
  transfers between devices with their start and end apart: 12 -> 13, of which waited for: 7 -> 5; matrix products, arithmetic and copies ran while one was open for 5% -> 5% of each run, Pallas kernels for 0% -> 16%
where the time goes in v1:
time: 113 us; the launch traced here: 112 us
  starting transfers between devices  31.4 us (28%)
  blocking collectives  30.7 us (27%)
  Pallas kernels  26.4 us (23%)
  waiting for transfers between devices  12.9 us (11%)
  local copies, waits for them, and re-layouts  9.82 us (9%)
    all_to_all x1, blocking collectives, exchanged(): return lax.all_to_all(array, 'tm', split_axis=0, concat_axis=0, tiled=True)  30.7 us
    pallas_call x4, Pallas kernels, call(): pl.pallas_call(kernel, out_shape=shapes, in_specs=[pl.BlockSpec(memory_sp...  26.4 us
    ppermute x4, starting transfers between devices, shifted(): return lax.ppermute(array, axis, pairs)  12.3 us
    all_to_all x2, starting transfers between devices, exchanged(): return lax.all_to_all(array, 'tm', split_axis=0, concat_axis=0, tiled=True)  11.1 us
    ppermute x4, waiting for transfers between devices, shifted(): return lax.ppermute(array, axis, pairs)  6.6 us
    ppermute x4, starting transfers between devices, paired(): lax.ppermute(array, 'tm', [(i, i ^ 1) for i in range(count) if i % 2 or n...  4.37 us
    ppermute x4, waiting for transfers between devices, paired(): lax.ppermute(array, 'tm', [(i, i ^ 1) for i in range(count) if i % 2 or n...  4.3 us
    ppermute x3, starting transfers between devices, spread(): lax.ppermute(rows, 'tm', [(i, (i + 2 * by) % count) for i in range(1, cou...  3.65 us
  transfers between devices with their start and end apart: 13, of which 5 were waited for; matrix products, arithmetic and copies ran while one was open for 5% of the time, Pallas kernels for 16%

profile of v1, /device:TPU:0, one launch (start us, length us, event | category | flops | bytes accessed | tf_op | source)
XLA Modules:
  0.0 111.7 jit_solution(16279016630884236159)
XLA Ops:
  0.0 0.5 collective-permute-start
  0.5 0.7 fusion.8
  1.2 0.1 pad.13.clone
  1.3 1.0 slice_bitcast_fusion
  2.3 0.1 maximum_maximum_fusion.1
  2.4 1.3 %collective-permute-start.2 = (f32[264,128]{1,0:T(8,128)S(1)}, f32[264,128]{1,0:T(8,128)S(1)}, u32[]{:S(2)}, u32[]{:S(2)}) collective-permute-start(f32[264,128]{1,0:T(8,128)S(1)} %get-tuple-element.22), channel_id=1, source_target_pairs={{1,0},{2,1},{3,2},{5,4},{6,5},{7,6},{9,8},{10,9},{11,10},{13,12},{... | collective-permute-start | bytes 405512 | tf_op jit(solution)/shard_map/ppermute | solution.py:30
  3.7 5.1 %collective-permute-start.1 = (f32[264,128]{1,0:T(8,128)S(1)}, f32[264,128]{1,0:T(8,128)S(1)}, u32[]{:S(2)}, u32[]{:S(2)}) collective-permute-start(f32[264,128]{1,0:T(8,128)S(1)} %get-tuple-element.23), channel_id=1, source_target_pairs={{0,1},{1,2},{2,3},{4,5},{5,6},{6,7},{8,9},{9,10},{10,11},{12,13},{... | collective-permute-start | bytes 405512 | tf_op jit(solution)/shard_map/ppermute | solution.py:30
  8.9 2.8 %dynamic-slice_bitcast_fusion = (f32[16,72,128]{2,1,0:T(8,128)}, f32[16,72,128]{2,1,0:T(8,128)}, f32[16,72,128]{2,1,0:T(8,128)}) fusion(f32[1,16,256,128]{3,2,1,0:T(8,128)} %param.6, s32[]{:T(128)S(6)} %min.12, s32[]{:T(128)S(6)} %min.10, s32[]{:T(128)S(6)} %min.11), kind=kLoop, calls=%fused_computation | loop fusion | bytes 3538956 | tf_op jit(solution)/shard_map/dynamic_slice | solution.py:397
  11.7 0.7 collective-permute-start.5
  12.3 1.5 %collective-permute-start.3 = (f32[16,72,128]{2,1,0:T(8,128)}, f32[16,72,128]{2,1,0:T(8,128)}, u32[]{:S(2)}, u32[]{:S(2)}) collective-permute-start(f32[16,72,128]{2,1,0:T(8,128)} %get-tuple-element.16), channel_id=1, source_target_pairs={{4,12},{12,20},{20,28},{5,13},{13,21},{21,29},{6,14},{14,22},{22,3... | collective-permute-start | bytes 1769480 | tf_op jit(solution)/shard_map/ppermute | solution.py:399
  13.8 0.0 collective-permute-done.2.high
  13.9 0.0 copy-start.6
  13.9 1.5 %collective-permute-start.4 = (f32[16,72,128]{2,1,0:T(8,128)}, f32[16,72,128]{2,1,0:T(8,128)}, u32[]{:S(2)}, u32[]{:S(2)}) collective-permute-start(f32[16,72,128]{2,1,0:T(8,128)} %get-tuple-element.17), channel_id=1, source_target_pairs={{4,20},{12,28},{20,4},{5,21},{13,29},{21,5},{6,22},{14,30},{22,6},... | collective-permute-start | bytes 1769480 | tf_op jit(solution)/shard_map/ppermute | solution.py:399
  15.3 0.0 collective-permute-done.1.low
  15.3 0.0 copy-start.7
  15.3 0.0 collective-permute-done.other
  15.3 0.0 copy-start
  15.3 0.0 copy-done.6
  15.3 0.6 copy-done.7
  16.0 0.7 copy-done
  16.7 5.2 %shard_map.65 = f32[8,144,128]{2,1,0:T(8,128)} custom-call(f32[16,256,128]{2,1,0:T(8,128)} %bitcast.18, f32[16,256,128]{2,1,0:T(8,128)} %copy-done, f32[16,256,128]{2,1,0:T(8,128)} %initial.3, f32[16,256,128]{2,1,0:T(8,128)} %bitcast.22, f32[264,128]{1,0:T(8,128)} %copy-done.7, f32[264,128]{1,0:T(8,128)} %copy-done.6, f32[16,256]{1,0:T(8,128)} %kappa.3, ...), custom_call_target="tpu_custom_call" | custom-call | flops 2000000000 | bytes 1000000 | tf_op jit(solution)/shard_map/pallas_call | solution.py:367
  21.9 7.5 %all-to-all-start.1 = ((f32[8,144,128]{2,1,0:T(8,128)}), f32[8,144,128]{2,1,0:T(8,128)S(1)}, u32[]{:S(2)}, u32[]{:S(2)}) async-start(f32[8,144,128]{2,1,0:T(8,128)} %shard_map.65), calls=%async_computation.1 | async-start | bytes 1179648 | tf_op jit(solution)/shard_map/all_to_all | solution.py:384
  29.4 8.4 %shard_map.64 = f32[8,432,128]{2,1,0:T(8,128)} custom-call(f32[16,256,128]{2,1,0:T(8,128)} %bitcast.19, f32[16,256,128]{2,1,0:T(8,128)} %copy-done, f32[16,256,128]{2,1,0:T(8,128)} %initial.3, f32[16,256,128]{2,1,0:T(8,128)} %bitcast.23, f32[264,128]{1,0:T(8,128)} %copy-done.7, f32[264,128]{1,0:T(8,128)} %copy-done.6, f32[16,256]{1,0:T(8,128)} %kappa.3, ...), custom_call_target="tpu_custom_call" | custom-call | flops 6000000000 | bytes 1000000 | tf_op jit(solution)/shard_map/pallas_call | solution.py:367
  37.8 0.0 slice-start
  37.8 0.0 slice-start.1
  37.8 0.0 copy-start.8
  37.8 1.9 %all-to-all-done.1.edge = f32[8,144,128]{2,1,0:T(8,128)S(1)} async-done(((f32[8,144,128]{2,1,0:T(8,128)}), f32[8,144,128]{2,1,0:T(8,128)S(1)}, u32[]{:S(2)}, u32[]{:S(2)}) %all-to-all-start.1) | async-done | bytes 589856 | tf_op jit(solution)/shard_map/all_to_all | solution.py:384
  39.8 0.0 copy-start.2
  39.8 3.6 %all-to-all-start = ((f32[8,432,128]{2,1,0:T(8,128)}), f32[8,432,128]{2,1,0:T(8,128)S(1)}, u32[]{:S(2)}, u32[]{:S(2)}) async-start(f32[8,432,128]{2,1,0:T(8,128)} %shard_map.64), calls=%async_computation | async-start | bytes 3538944 | tf_op jit(solution)/shard_map/all_to_all | solution.py:384
  43.4 0.0 collective-permute-done.5.rest_2_
  43.4 0.0 copy-start.3
  43.4 1.3 %collective-permute-start.8 = (f32[16,72,128]{2,1,0:T(8,128)S(1)}, f32[16,72,128]{2,1,0:T(8,128)}, u32[]{:S(2)}, u32[]{:S(2)}) collective-permute-start(f32[16,72,128]{2,1,0:T(8,128)S(1)} %collective-permute-done.5.rest_2_), channel_id=1, source_target_pairs={{4,0},{12,8},{20,16},{28,24},{5,1},{13,9},{21,17},{29,25},{6,2},{1... | collective-permute-start | bytes 1769480 | tf_op jit(solution)/shard_map/ppermute | solution.py:380
  44.7 0.0 collective-permute-done.3.rest_0_
  44.7 1.3 %collective-permute-start.6 = (f32[16,72,128]{2,1,0:T(8,128)}, f32[16,72,128]{2,1,0:T(8,128)}, u32[]{:S(2)}, u32[]{:S(2)}) collective-permute-start(f32[16,72,128]{2,1,0:T(8,128)} %collective-permute-done.3.rest_0_), channel_id=1, source_target_pairs={{4,0},{12,8},{20,16},{28,24},{5,1},{13,9},{21,17},{29,25},{6,2},{1... | collective-permute-start | bytes 1769480 | tf_op jit(solution)/shard_map/ppermute | solution.py:380
  46.0 0.0 collective-permute-done.4.rest_1_
  46.0 1.3 %collective-permute-start.7 = (f32[16,72,128]{2,1,0:T(8,128)}, f32[16,72,128]{2,1,0:T(8,128)}, u32[]{:S(2)}, u32[]{:S(2)}) collective-permute-start(f32[16,72,128]{2,1,0:T(8,128)} %collective-permute-done.4.rest_1_), channel_id=1, source_target_pairs={{4,0},{12,8},{20,16},{28,24},{5,1},{13,9},{21,17},{29,25},{6,2},{1... | collective-permute-start | bytes 1769480 | tf_op jit(solution)/shard_map/ppermute | solution.py:380
  47.3 0.0 slice-done
  47.4 0.0 slice-done.1
  47.4 0.0 copy-done.8
  47.4 0.1 fusion.2
  47.5 0.1 broadcast_in_dim.12
  47.6 0.0 collective-permute-done.8.rest_5_
  47.6 2.2 %collective-permute-done.6.rest_3_ = f32[16,72,128]{2,1,0:T(8,128)} collective-permute-done((f32[16,72,128]{2,1,0:T(8,128)}, f32[16,72,128]{2,1,0:T(8,128)}, u32[]{:S(2)}, u32[]{:S(2)}) %collective-permute-start.6) | collective-permute-done | bytes 589856 | tf_op jit(solution)/shard_map/ppermute | solution.py:380
  49.8 2.1 %collective-permute-done.7.rest_4_ = f32[16,72,128]{2,1,0:T(8,128)} collective-permute-done((f32[16,72,128]{2,1,0:T(8,128)}, f32[16,72,128]{2,1,0:T(8,128)}, u32[]{:S(2)}, u32[]{:S(2)}) %collective-permute-start.7) | collective-permute-done | bytes 589856 | tf_op jit(solution)/shard_map/ppermute | solution.py:380
  51.9 0.9 broadcast_in_dim.13.kappa.kappa_far
  52.8 0.0 copy-done.2
  52.8 0.0 copy-done.3
  52.8 4.7 %shard_map.66 = (f32[4,576,128]{2,1,0:T(8,128)}, f32[720,128]{1,0:T(8,128)}, f32[720,128]{1,0:T(8,128)}, f32[8,72,128]{2,1,0:T(8,128)}, f32[8,72,128]{2,1,0:T(8,128)}) custom-call(f32[8,144,128]{2,1,0:T(8,128)} %copy-done.2, f32[16,256,128]{2,1,0:T(8,128)} %bitcast.20, f32[16,256,128]{2,1,0:T(8,128)} %copy-done, ...), custom_call_target="tpu_custom_call" | custom-call | flops 1000000000 | bytes 1000000 | tf_op jit(solution)/shard_map/pallas_call | solution.py:367
  57.5 1.3 %collective-permute-start.10 = (f32[8,72,128]{2,1,0:T(8,128)}, f32[8,72,128]{2,1,0:T(8,128)S(1)}, u32[]{:S(2)}, u32[]{:S(2)}) collective-permute-start(f32[8,72,128]{2,1,0:T(8,128)} %get-tuple-element.10.edge_low), channel_id=1, source_target_pairs={{1,0},{2,1},{3,2},{5,4},{6,5},{7,6},{9,8},{10,9},{11,10},{13,12},{... | collective-permute-start | bytes 884744 | tf_op jit(solution)/shard_map/ppermute | solution.py:30
  58.8 4.6 %collective-permute-start.9 = (f32[8,72,128]{2,1,0:T(8,128)}, f32[8,72,128]{2,1,0:T(8,128)S(1)}, u32[]{:S(2)}, u32[]{:S(2)}) collective-permute-start(f32[8,72,128]{2,1,0:T(8,128)} %get-tuple-element.11.edge_high), channel_id=1, source_target_pairs={{0,1},{1,2},{2,3},{4,5},{5,6},{6,7},{8,9},{9,10},{10,11},{12,13},{... | collective-permute-start | bytes 884744 | tf_op jit(solution)/shard_map/ppermute | solution.py:30
  63.4 5.3 %collective-permute-done.10.right = f32[8,72,128]{2,1,0:T(8,128)S(1)} collective-permute-done((f32[8,72,128]{2,1,0:T(8,128)}, f32[8,72,128]{2,1,0:T(8,128)S(1)}, u32[]{:S(2)}, u32[]{:S(2)}) %collective-permute-start.10) | collective-permute-done | bytes 294944 | tf_op jit(solution)/shard_map/ppermute | solution.py:30
  68.7 0.0 copy-start.4
  68.7 1.3 %collective-permute-done.9.left = f32[8,72,128]{2,1,0:T(8,128)S(1)} collective-permute-done((f32[8,72,128]{2,1,0:T(8,128)}, f32[8,72,128]{2,1,0:T(8,128)S(1)}, u32[]{:S(2)}, u32[]{:S(2)}) %collective-permute-start.9) | collective-permute-done | bytes 294944 | tf_op jit(solution)/shard_map/ppermute | solution.py:30
  70.0 0.0 copy-start.5
  70.0 0.0 all-to-all-done.middle
  70.0 0.0 copy-start.1
  70.0 0.0 copy-done.4
  70.0 0.7 copy-done.5
  70.7 0.6 copy-done.1
  71.3 8.1 %shard_map.67 = f32[8,512,128]{2,1,0:T(8,128)} custom-call(f32[8,432,128]{2,1,0:T(8,128)} %copy-done.1, f32[8,72,128]{2,1,0:T(8,128)} %get-tuple-element.10.edge_low, f32[8,72,128]{2,1,0:T(8,128)} %get-tuple-element.11.edge_high, f32[8,72,128]{2,1,0:T(8,128)} %copy-done.5, f32[8,72,128]{2,1,0:T(8,128)} %copy-done.4, ...), custom_call_target="tpu_custom_call" | custom-call | flops 1000000000 | bytes 1000000 | tf_op jit(solution)/shard_map/pallas_call | solution.py:367
  79.4 30.7 %all_to_all.15 = f32[8,512,128]{2,1,0:T(8,128)S(1)} all-to-all(f32[8,512,128]{2,1,0:T(8,128)} %shard_map.67), channel_id=1, replica_groups=mesh['tm'=8,'tx'=4] {'tm'}, dimensions={0} | all-to-all | bytes 4194304 | tf_op jit(solution)/shard_map/all_to_all | solution.py:384
  110.1 1.6 %copy.7 = f32[16,8,32,128]{3,2,1,0:T(8,128)} copy(f32[16,8,32,128]{3,2,0,1:T(8,128)S(1)} %bitcast.21) | data formatting | bytes 4194304 | tf_op jit(solution)/shard_map/transpose | solution.py:509
  (5 shorter events, 0.1 us)
Async XLA Ops:
  0.0 15.3 %collective-permute-start = (f32[16,256,128]{2,1,0:T(8,128)}, f32[16,256,128]{2,1,0:T(8,128)S(1)}, u32[]{:S(2)}, u32[]{:S(2)}) collective-permute-start(f32[16,256,128]{2,1,0:T(8,128)} %bitcast.17), channel_id=1, source_target_pairs={{0,4},{4,0},{8,12},{12,8},{16,20},{20,16},{24,28},{28,24},{1,5},{5... | collective-permute-start | bytes 6291464 | tf_op jit(solution)/shard_map/ppermute | solution.py:380
  2.4 11.4 %collective-permute-start.2 = (f32[264,128]{1,0:T(8,128)S(1)}, f32[264,128]{1,0:T(8,128)S(1)}, u32[]{:S(2)}, u32[]{:S(2)}) collective-permute-start(f32[264,128]{1,0:T(8,128)S(1)} %get-tuple-element.22), channel_id=1, source_target_pairs={{1,0},{2,1},{3,2},{5,4},{6,5},{7,6},{9,8},{10,9},{11,10},{13,12},{... | collective-permute-start | bytes 405512 | tf_op jit(solution)/shard_map/ppermute | solution.py:30
  3.7 11.6 %collective-permute-start.1 = (f32[264,128]{1,0:T(8,128)S(1)}, f32[264,128]{1,0:T(8,128)S(1)}, u32[]{:S(2)}, u32[]{:S(2)}) collective-permute-start(f32[264,128]{1,0:T(8,128)S(1)} %get-tuple-element.23), channel_id=1, source_target_pairs={{0,1},{1,2},{2,3},{4,5},{5,6},{6,7},{8,9},{9,10},{10,11},{12,13},{... | collective-permute-start | bytes 405512 | tf_op jit(solution)/shard_map/ppermute | solution.py:30
  11.7 31.7 %collective-permute-start.5 = (f32[16,72,128]{2,1,0:T(8,128)}, f32[16,72,128]{2,1,0:T(8,128)S(1)}, u32[]{:S(2)}, u32[]{:S(2)}) collective-permute-start(f32[16,72,128]{2,1,0:T(8,128)} %get-tuple-element.15), channel_id=1, source_target_pairs={{4,28},{12,4},{20,12},{5,29},{13,5},{21,13},{6,30},{14,6},{22,14},... | collective-permute-start | bytes 1769480 | tf_op jit(solution)/shard_map/ppermute | solution.py:399
  12.3 32.4 %collective-permute-start.3 = (f32[16,72,128]{2,1,0:T(8,128)}, f32[16,72,128]{2,1,0:T(8,128)}, u32[]{:S(2)}, u32[]{:S(2)}) collective-permute-start(f32[16,72,128]{2,1,0:T(8,128)} %get-tuple-element.16), channel_id=1, source_target_pairs={{4,12},{12,20},{20,28},{5,13},{13,21},{21,29},{6,14},{14,22},{22,3... | collective-permute-start | bytes 1769480 | tf_op jit(solution)/shard_map/ppermute | solution.py:399
  13.9 1.5 %copy-start.6 = (f32[264,128]{1,0:T(8,128)}, f32[264,128]{1,0:T(8,128)S(1)}, u32[]{:S(2)}) copy-start(f32[264,128]{1,0:T(8,128)S(1)} %collective-permute-done.2.high) | copy-start | bytes 405508
  13.9 32.2 %collective-permute-start.4 = (f32[16,72,128]{2,1,0:T(8,128)}, f32[16,72,128]{2,1,0:T(8,128)}, u32[]{:S(2)}, u32[]{:S(2)}) collective-permute-start(f32[16,72,128]{2,1,0:T(8,128)} %get-tuple-element.17), channel_id=1, source_target_pairs={{4,20},{12,28},{20,4},{5,21},{13,29},{21,5},{6,22},{14,30},{22,6},... | collective-permute-start | bytes 1769480 | tf_op jit(solution)/shard_map/ppermute | solution.py:399
  15.3 0.6 copy-start.7
  15.3 1.4 %copy-start = (f32[16,256,128]{2,1,0:T(8,128)}, f32[16,256,128]{2,1,0:T(8,128)S(1)}, u32[]{:S(2)}) copy-start(f32[16,256,128]{2,1,0:T(8,128)S(1)} %collective-permute-done.other) | copy-start | bytes 6291460
  21.9 17.9 %all-to-all-start.1 = ((f32[8,144,128]{2,1,0:T(8,128)}), f32[8,144,128]{2,1,0:T(8,128)S(1)}, u32[]{:S(2)}, u32[]{:S(2)}) async-start(f32[8,144,128]{2,1,0:T(8,128)} %shard_map.65), calls=%async_computation.1 | async-start | bytes 1179648 | tf_op jit(solution)/shard_map/all_to_all | solution.py:384
  37.8 9.5 %slice-start = ((f32[264,128]{1,0:T(8,128)}), f32[4,128]{1,0:T(4,128)S(1)}, s32[]{:S(2)}) async-start(f32[264,128]{1,0:T(8,128)} %copy-done.6), calls=%async_computation.3 | async-start | bytes 4096 | tf_op jit(solution)/shard_map/slice | solution.py:459
  37.8 9.5 %slice-start.1 = ((f32[264,128]{1,0:T(8,128)}), f32[4,128]{1,0:T(4,128)S(1)}, s32[]{:S(2)}) async-start(f32[264,128]{1,0:T(8,128)} %copy-done.7), calls=%async_computation.4 | async-start | bytes 4096 | tf_op jit(solution)/shard_map/slice | solution.py:459
  37.8 9.5 %copy-start.8 = (f32[16,256]{1,0:T(8,128)S(1)}, f32[16,256]{1,0:T(8,128)}, u32[]{:S(2)}) copy-start(f32[16,256]{1,0:T(8,128)} %kappa.3) | copy-start | bytes 49156
  39.8 13.0 %copy-start.2 = (f32[8,144,128]{2,1,0:T(8,128)}, f32[8,144,128]{2,1,0:T(8,128)S(1)}, u32[]{:S(2)}) copy-start(f32[8,144,128]{2,1,0:T(8,128)S(1)} %all-to-all-done.1.edge) | copy-start | bytes 1769476
  39.8 30.2 %all-to-all-start = ((f32[8,432,128]{2,1,0:T(8,128)}), f32[8,432,128]{2,1,0:T(8,128)S(1)}, u32[]{:S(2)}, u32[]{:S(2)}) async-start(f32[8,432,128]{2,1,0:T(8,128)} %shard_map.64), calls=%async_computation | async-start | bytes 3538944 | tf_op jit(solution)/shard_map/all_to_all | solution.py:384
  43.4 9.4 %copy-start.3 = (f32[16,72,128]{2,1,0:T(8,128)}, f32[16,72,128]{2,1,0:T(8,128)S(1)}, u32[]{:S(2)}) copy-start(f32[16,72,128]{2,1,0:T(8,128)S(1)} %collective-permute-done.5.rest_2_) | copy-start | bytes 1769476
  43.4 4.2 %collective-permute-start.8 = (f32[16,72,128]{2,1,0:T(8,128)S(1)}, f32[16,72,128]{2,1,0:T(8,128)}, u32[]{:S(2)}, u32[]{:S(2)}) collective-permute-start(f32[16,72,128]{2,1,0:T(8,128)S(1)} %collective-permute-done.5.rest_2_), channel_id=1, source_target_pairs={{4,0},{12,8},{20,16},{28,24},{5,1},{13,9},{21,17},{29,25},{6,2},{1... | collective-permute-start | bytes 1769480 | tf_op jit(solution)/shard_map/ppermute | solution.py:380
  44.7 5.0 %collective-permute-start.6 = (f32[16,72,128]{2,1,0:T(8,128)}, f32[16,72,128]{2,1,0:T(8,128)}, u32[]{:S(2)}, u32[]{:S(2)}) collective-permute-start(f32[16,72,128]{2,1,0:T(8,128)} %collective-permute-done.3.rest_0_), channel_id=1, source_target_pairs={{4,0},{12,8},{20,16},{28,24},{5,1},{13,9},{21,17},{29,25},{6,2},{1... | collective-permute-start | bytes 1769480 | tf_op jit(solution)/shard_map/ppermute | solution.py:380
  46.0 5.8 %collective-permute-start.7 = (f32[16,72,128]{2,1,0:T(8,128)}, f32[16,72,128]{2,1,0:T(8,128)}, u32[]{:S(2)}, u32[]{:S(2)}) collective-permute-start(f32[16,72,128]{2,1,0:T(8,128)} %collective-permute-done.4.rest_1_), channel_id=1, source_target_pairs={{4,0},{12,8},{20,16},{28,24},{5,1},{13,9},{21,17},{29,25},{6,2},{1... | collective-permute-start | bytes 1769480 | tf_op jit(solution)/shard_map/ppermute | solution.py:380
  57.5 11.2 %collective-permute-start.10 = (f32[8,72,128]{2,1,0:T(8,128)}, f32[8,72,128]{2,1,0:T(8,128)S(1)}, u32[]{:S(2)}, u32[]{:S(2)}) collective-permute-start(f32[8,72,128]{2,1,0:T(8,128)} %get-tuple-element.10.edge_low), channel_id=1, source_target_pairs={{1,0},{2,1},{3,2},{5,4},{6,5},{7,6},{9,8},{10,9},{11,10},{13,12},{... | collective-permute-start | bytes 884744 | tf_op jit(solution)/shard_map/ppermute | solution.py:30
  58.8 11.2 %collective-permute-start.9 = (f32[8,72,128]{2,1,0:T(8,128)}, f32[8,72,128]{2,1,0:T(8,128)S(1)}, u32[]{:S(2)}, u32[]{:S(2)}) collective-permute-start(f32[8,72,128]{2,1,0:T(8,128)} %get-tuple-element.11.edge_high), channel_id=1, source_target_pairs={{0,1},{1,2},{2,3},{4,5},{5,6},{6,7},{8,9},{9,10},{10,11},{12,13},{... | collective-permute-start | bytes 884744 | tf_op jit(solution)/shard_map/ppermute | solution.py:30
  68.7 1.3 %copy-start.4 = (f32[8,72,128]{2,1,0:T(8,128)}, f32[8,72,128]{2,1,0:T(8,128)S(1)}, u32[]{:S(2)}) copy-start(f32[8,72,128]{2,1,0:T(8,128)S(1)} %collective-permute-done.10.right) | copy-start | bytes 884740
  70.0 0.7 copy-start.5
  70.0 1.3 %copy-start.1 = (f32[8,432,128]{2,1,0:T(8,128)}, f32[8,432,128]{2,1,0:T(8,128)S(1)}, u32[]{:S(2)}) copy-start(f32[8,432,128]{2,1,0:T(8,128)S(1)} %all-to-all-done.middle) | copy-start | bytes 5308420

commit v2 on v1

v2 whole, which is shorter than its diff:
```python
import functools

import jax
import jax.numpy as jnp
from jax import lax
from jax.experimental import pallas as pl
from jax.experimental.pallas import tpu as pltpu
from jax.sharding import PartitionSpec as P


ALPHA = 0.05
REACH = 2
F32 = jnp.float32
BF16 = jnp.bfloat16
MIB = 2**20
VMEM_BYTES = 67043328


def split(value):
    high = value.astype(BF16)
    return high, (value - high.astype(F32)).astype(BF16)


def dot(left, right):
    return jnp.dot(left, right, preferred_element_type=F32)


def shifted(array, axis, by):
    count = lax.axis_size(axis)
    pairs = [(i, i + by) for i in range(count) if 0 <= i + by < count]
    return lax.ppermute(array, axis, pairs)


def cut(value, rows, out, base, blocks):
    size = value.shape[0]
    block = size // blocks
    tall = block + 2 * REACH
    rows[pl.ds(REACH, size), :] = value
    for target in range(blocks):
        out[target, pl.ds(base, tall), :] = rows[pl.ds(block * target, tall), :]


def fill_weights(weights, first_half, second_half):
    depth = first_half.shape[0]
    first_high, first_low = split(first_half)
    weights[:depth, :depth] = first_high
    weights[:depth, depth:] = first_low
    if second_half is None:
        weights[depth:, :depth] = first_high
        weights[depth:, depth:] = jnp.zeros_like(first_low)
    else:
        second_high, second_low = split(second_half)
        weights[depth:, :depth] = second_high
        weights[depth:, depth:] = second_low


def times_matrix(value, weights):
    depth = value.shape[1]
    wide = dot(jnp.concatenate(split(value), axis=1), weights[...])
    return wide[:, :depth] + wide[:, depth:]


def residual_kernel(
    blocks, inner, state, other, initial, force, low, high, kappa, rates, basis, out,
    here, past, pushed, parts, rows, levels, turned, weights, sides, plain_ref, rates_ref, loads, stores, extras,
):
    columns, size, depth = state.shape
    tall = size // blocks + 2 * REACH
    step_here = lax.axis_index("tm")
    odd = step_here % 2 == 1
    first = step_here == 0
    if inner:
        mine = list(range(2, columns - 2))
        wide = list(range(1, columns - 1))
    else:
        mine = [0, 1, columns - 2, columns - 1]
        wide = [0, 1, 2, columns - 3, columns - 2, columns - 1]

    def load(kind, x):
        source, target = ((state, here), (other, past), (force, pushed))[kind]
        target = target.at[x, pl.ds(8, size), :] if kind == 0 else target.at[x]
        return pltpu.make_async_copy(source.at[x], target, loads.at[kind, x])

    def level(x):
        return here[x, pl.ds(8, size), :]

    small = [(basis, plain_ref), (rates, rates_ref), (kappa, levels.at[pl.ds(0, columns), :])]
    if not inner:
        small += [(low, sides.at[0]), (high, sides.at[1])]
    small = [pltpu.make_async_copy(*ends, extras.at[i]) for i, ends in enumerate(small)]
    levels[...] = jnp.zeros_like(levels)
    for copy in small:
        copy.start()
    for x in wide:
        load(0, x).start()
        if x in mine:
            load(2, x).start()

    @pl.when(odd)
    def _():
        for x in mine:
            load(1, x).start()

    @pl.when(first)
    def _():
        for x in mine:
            pltpu.make_async_copy(initial.at[x], past.at[x], loads.at[1, x]).start()

    here[:, :8, :] = jnp.zeros((columns, 8, depth), F32)
    here[:, 8 + size :, :] = jnp.zeros((columns, 8, depth), F32)

    rows[...] = jnp.zeros_like(rows)
    for copy in small:
        copy.wait()
    plain = plain_ref[...]
    fill_weights(weights, plain, -plain * rates_ref[...])
    for part in range(size // depth):
        where = pl.ds(part * depth, depth)
        turned[where, :] = jnp.transpose(levels[:, where])

    def column(x, left, right, base, which):
        load(2, x).wait()

        @pl.when(jnp.logical_or(odd, first))
        def _():
            load(1, x).wait()

        center = level(x)
        up = here[x, pl.ds(7, size), :]
        down = here[x, pl.ds(9, size), :]
        square = center * center
        beside = left + right + up + down
        across = jnp.broadcast_to(pltpu.roll(turned[...], (depth - x) % depth, 1)[:, :1], (size, depth))
        value = (
            pushed[x]
            - center
            + jnp.where(jnp.logical_or(odd, first), past[x], 0.0)
            - across * (4.0 * center - beside)
            - 0.5 * (square * center) / (1.0 + square)
        )
        value_high, value_low = split(value)
        center_high, center_low = split(center)
        joined_high = jnp.concatenate([value_high, center_high], axis=1)
        joined_low = jnp.concatenate([value_low, center_low], axis=1)
        product = dot(joined_high, weights[...])
        modal = product[:, :depth] + product[:, depth:] + dot(joined_low, weights[:, :depth])
        cut(modal, rows.at[which], parts, base, blocks)

    def store(step):
        where = pl.ds(pl.multiple_of(step * 2 * tall, 8), 2 * tall)
        return pltpu.make_async_copy(parts.at[:, where, :], out.at[:, where, :], stores.at[step])

    if inner:
        load(0, 1).wait()
        load(0, 2).wait()

        def pair(step, carry):
            base = pl.multiple_of(step * 2 * tall, 8)
            for which in range(2):
                x = 2 + 2 * step + which
                load(0, x + 1).wait()
                column(x, level(x - 1), level(x + 1), base + which * tall, which)
            store(step).start()
            return carry

        lax.fori_loop(0, len(mine) // 2, pair, 0)
    else:
        for x in wide:
            load(0, x).wait()
        column(0, sides[0], level(1), 0, 0)
        column(1, level(0), level(2), tall, 1)
        store(0).start()
        column(columns - 2, level(columns - 3), level(columns - 1), 2 * tall, 0)
        column(columns - 1, level(columns - 2), sides[1], 3 * tall, 1)
        store(1).start()
    for step in range(len(mine) // 2):
        store(step).wait()


def modes_kernel(block, count, spans, edge, state, other, kappa, rates, basis, *rest):
    pieces = rest[:count]
    first_out, second_out, third_out, near, far, strip, gathered, weights, plain_ref, rates_ref, edges, cells, loads, stores = rest[count:]
    broad, _ = near.shape[1:]
    window = far.shape[2]
    chips = count + 1
    steps = 2 * chips
    size = block * steps
    tall = block + 2 * REACH
    room = (strip.shape[1] - broad) // 2
    here = lax.axis_index("tm")
    chip = here // 2
    odd = here % 2 == 1
    width = sum(stop - start for start, stop in spans)
    near_start = pl.multiple_of(near_begin(here, block, broad, size), 8)

    def copies(source):
        made = []
        at = 0
        for start, stop in spans:
            take = pl.ds(start, stop - start)
            put = pl.ds(at, stop - start)
            made.append((source.at[take, pl.ds(near_start, broad), :], near.at[put]))
            made += [(pieces[by].at[take], far.at[by, put]) for by in range(count)]
            at += stop - start
        return [pltpu.make_async_copy(*ends, loads.at[i]) for i, ends in enumerate(made)]

    small = [(basis, plain_ref), (rates, rates_ref), (kappa, cells)]
    if edge is not None:
        small.append((edge, edges))
    small = [pltpu.make_async_copy(*ends, stores.at[i]) for i, ends in enumerate(small)]

    @pl.when(odd)
    def _():
        for copy in copies(state):
            copy.start()

    @pl.when(jnp.logical_not(odd))
    def _():
        for copy in copies(other):
            copy.start()

    for copy in small:
        copy.start()
    strip[...] = jnp.zeros_like(strip)
    for copy in small:
        copy.wait()
    fill_weights(weights, plain_ref[...], None)
    if edge is None:
        chunk = 2 * tall

        def factors(step, carry):
            base = pl.multiple_of(step * chunk, 8)
            second_out[pl.ds(base, chunk), :], third_out[pl.ds(base, chunk), :] = time_factors(
                cells[pl.ds(base, chunk), :], rates_ref[...], steps
            )
            return carry

        lax.fori_loop(0, cells.shape[0] // chunk, factors, 0)
    for copy in copies(state):
        copy.wait()
    begin = block * here - REACH + room

    def gather(source, start, extent):
        for x in range(width):
            strip[x % 2, pl.ds(room, extent), :] = source(x)
            gathered[pl.ds(x * tall, tall), :] = strip[x % 2, pl.ds(begin - start, tall), :]
        return times_matrix(gathered[...], weights)

    first_out[chip] = gather(lambda x: near[x], near_start, broad)

    far_start = window_start(here, block, window, size)
    strip[...] = jnp.zeros_like(strip)

    def far_slot(by, carry):
        first_out[(chip - by - 1 + chips) % chips] = gather(lambda x: far[by, x], far_start, window)
        return carry

    lax.fori_loop(0, count, far_slot, 0)
    if edge is not None:
        two = REACH * tall
        for n in range(steps):
            left = edges[n, :two, :]
            right = edges[n, two:, :]
            if n and n % 2 == 0:
                left = left + first_out[n // 2 - 1, :two, :]
                right = right + first_out[n // 2 - 1, two:, :]
            second_out[n] = left
            third_out[n] = right
        second_out[steps] = cells[:two, :]
        third_out[steps] = cells[cells.shape[0] - two :, :]


def time_factors(kappa, rates, steps):
    inverse = 1.0 / (1.0 + rates + 4.0 * kappa)
    power = inverse
    for _ in range(steps - 1):
        power = power * inverse
    return inverse, ALPHA / (1.0 - ALPHA * power)


def rim_kernel(block, count, spans, edge, state, other, kappa, rates, basis, *rest):
    outs, scratch = rest[count : count + 2], rest[count + 2 :]
    modes_kernel(block, count, spans, edge, state, other, kappa, rates, basis, *rest[:count], scratch[0], *outs, *scratch[1:])


def fill_kernel(block, count, spans, state, other, edge_low, edge_high, kappa, rates, basis, *rest):
    bundle, scratch = rest[count], rest[count + 1 :]
    modal, inverse, ending, ends, turned, sems = scratch[:6]
    steps = edge_low.shape[0] - 1
    sides = [pltpu.make_async_copy(edge, ends.at[i], sems.at[i]) for i, edge in enumerate((edge_low, edge_high))]
    for copy in sides:
        copy.start()
    inner = scratch[6:]
    modes_kernel(block, count, spans, None, state, other, kappa, rates, basis, *rest[:count], modal, inverse, ending, *inner)
    plain_ref, rates_ref, cells = inner[5], inner[6], inner[8]
    turned[pl.ds(0, plain_ref.shape[0]), :] = jnp.transpose(plain_ref[...])
    turned[pl.ds(plain_ref.shape[0], 8), :] = jnp.broadcast_to(rates_ref[...], (8, plain_ref.shape[1]))
    for copy in sides:
        copy.wait()
    copies = [
        pltpu.make_async_copy(source, bundle.at[pl.ds(start, source.shape[0]), :], sems.at[2 + i])
        for i, (source, start) in enumerate(bundle_parts(modal, cells, inverse, ending, ends, turned, steps))
    ]
    for copy in copies:
        copy.start()
    for copy in copies:
        copy.wait()


def bundle_parts(modal, cells, inverse, ending, ends, turned, steps):
    parts = [modal.at[m] for m in range(steps // 2 - 1)] + [cells, inverse, ending]
    parts += [ends.at[side, n] for side in range(2) for n in range(steps)] + [turned]
    placed = []
    at = 0
    for part in parts:
        placed.append((part, at))
        at += part.shape[0]
    return placed


def relax_kernel(
    block, middle, left, right, bundle, out,
    known, source, older, newer, gathered, weights, modal, kappa, inverse, ending, ends, turned, loads,
):
    steps, inner, depth = middle.shape
    tall = block + 2 * REACH
    chunk = REACH * tall
    columns = inner // tall + 2 * REACH
    total = inner + 4 * chunk
    pad = older.shape[1] - total
    front = pad // 2
    own = pl.ds(chunk, total - 2 * chunk)
    parts = bundle_parts(modal, kappa.at[own, :], inverse.at[own, :], ending.at[own, :], ends, turned, steps)
    copies = [
        pltpu.make_async_copy(bundle.at[pl.ds(start, target.shape[0]), :], target, loads.at[i])
        for i, (target, start) in enumerate(parts)
    ]
    for copy in copies:
        copy.start()
    older[:, :front, :] = jnp.zeros((steps, front, depth), F32)
    older[:, front + total :, :] = jnp.zeros((steps, pad - front, depth), F32)
    for ghost, base in ((left, 0), (right, total - chunk)):
        kappa[pl.ds(base, chunk), :] = ghost[steps]
    copies[-1].wait()
    fill_weights(weights, turned[:depth, :], None)
    for base in (0, total - chunk):
        at = pl.ds(base, chunk)
        inverse[at, :], ending[at, :] = time_factors(kappa[at, :], turned[depth : depth + 1, :], steps)

    def solve(values, inv, end):
        last = values(0) * inv
        for n in range(1, steps):
            last = (values(n) + last) * inv
        return end * last

    def first(value, base):
        inv = inverse[pl.ds(base, chunk), :]
        run = solve(value, inv, ending[pl.ds(base, chunk), :])
        for n in range(steps):
            run = (known[n, pl.ds(base, chunk), :] + run) * inv
            older[n, pl.ds(base + front, chunk), :] = run

    def keep(value, base):
        def kept(n):
            made = value(n)
            known[n, pl.ds(base, chunk), :] = made
            return made

        return kept

    first(keep(lambda n: left[n], 0), 0)
    first(keep(lambda n: right[n], total - chunk), total - chunk)
    for copy in copies[:-1]:
        copy.wait()
    first(keep(lambda n: ends[0, n], chunk), chunk)
    first(keep(lambda n: ends[1, n], total - 2 * chunk), total - 2 * chunk)

    def first_middle(step, carry):
        at = pl.multiple_of(step * chunk, 8)
        base = pl.multiple_of(at + 2 * chunk, 8)

        def value(n):
            made = middle[n, pl.ds(at, chunk), :]
            if n and n % 2 == 0:
                made = made + modal[n // 2 - 1, pl.ds(at, chunk), :]
            return made

        first(keep(value, base), base)
        return carry

    lax.fori_loop(0, inner // chunk, first_middle, 0)

    def term(field, base, size, n):
        beside = (
            field[n, pl.ds(base + front - 1, size), :]
            + field[n, pl.ds(base + front + 1, size), :]
            + field[n, pl.ds(base + front - tall, size), :]
            + field[n, pl.ds(base + front + tall, size), :]
        )
        return known[n, pl.ds(base, size), :] + kappa[pl.ds(base, size), :] * beside

    def second(step, carry):
        base = pl.multiple_of(step * chunk, 8) + tall
        inv = inverse[pl.ds(base, chunk), :]

        def value(n):
            made = term(older, base, chunk, n)
            source[n, :chunk, :] = made
            return made

        run = solve(value, inv, ending[pl.ds(base, chunk), :])
        for n in range(steps):
            run = (source[n, :chunk, :] + run) * inv
            newer[n, pl.ds(base + front, chunk), :] = run
        return carry

    lax.fori_loop(0, (columns + 2) // 2, second, 0)

    def third(base):
        inv = inverse[pl.ds(base, block), :]

        def value(n):
            made = term(newer, base, block, n)
            source[n, :block, :] = made
            return made

        run = solve(value, inv, ending[pl.ds(base, block), :])
        for n in range(steps):
            run = (source[n, :block, :] + run) * inv
            gathered[pl.ds(n * block, block), :] = run
        gathered[...] = times_matrix(gathered[...], weights)

    def third_pair(step, carry):
        at = pl.multiple_of(step * 2 * tall, 8)
        to = pl.multiple_of(step * 2 * block, 8)
        for which in range(2):
            third(at + chunk + which * tall + REACH)
            for n in range(steps):
                out[n, pl.ds(to + which * block, block), :] = gathered[pl.ds(n * block, block), :]
        return carry

    lax.fori_loop(0, columns // 2, third_pair, 0)


SPACES = {"v": pltpu.VMEM, "h": pltpu.HBM}


def call(kernel, outs, spaces, scratch, flops, *operands, limit=None):
    shapes = [jax.ShapeDtypeStruct(shape, F32) for shape, _ in outs]
    return pl.pallas_call(
        kernel,
        out_shape=shapes,
        in_specs=[pl.BlockSpec(memory_space=SPACES[space]) for space in spaces],
        out_specs=[pl.BlockSpec(memory_space=SPACES[space]) for _, space in outs],
        scratch_shapes=scratch,
        cost_estimate=pl.CostEstimate(flops=flops, bytes_accessed=10**6, transcendentals=0),
        compiler_params=pltpu.CompilerParams(vmem_limit_bytes=60 * MIB if limit is None else limit),
    )(*operands)


def paired(array):
    count = lax.axis_size("tm")
    return lax.ppermute(array, "tm", [(i, i ^ 1) for i in range(count)])


def exchanged(array):
    return lax.all_to_all(array, "tm", split_axis=0, concat_axis=0, tiled=True)


def near_begin(device, block, broad, size):
    return jnp.clip((block * device - REACH) // 8 * 8, 0, size - broad)


def window_start(device, block, window, size):
    return jnp.clip(block * device - 4, 0, size - window)


def spread(mine, other, here, block, window, by):
    count = lax.axis_size("tm")
    start = window_start((here + 2 * by) % count, block, window, mine.shape[1])
    rows = jnp.where(
        here % 2 == 1,
        lax.dynamic_slice_in_dim(mine, start, window, 1),
        lax.dynamic_slice_in_dim(other, start, window, 1),
    )
    return lax.ppermute(rows, "tm", [(i, (i + 2 * by) % count) for i in range(count - 2)])


def correction(state, force, u_init, kappa, rates, basis):
    steps = lax.axis_size("tm")
    here = lax.axis_index("tm")
    chips = steps // 2
    columns, size, depth = u_init.shape
    block = size // steps
    tall = block + 2 * REACH
    chunk = REACH * tall
    window = block + 8
    broad = (block + 23) // 8 * 8
    inside = columns - 2 * REACH
    total = columns * tall + 2 * chunk
    front = (tall + 15) // 8 * 8
    square = pltpu.VMEM((2 * depth, 2 * depth), BF16)
    constants = [pltpu.VMEM((depth, depth), F32), pltpu.VMEM((1, depth), F32)]
    mine = state[0]
    other = paired(mine)
    low = shifted(mine[-1], "tx", 1)
    high = shifted(mine[0], "tx", -1)
    rates_row = rates.reshape(1, depth)
    pieces = []
    for by in range(1, chips):
        pieces.append(spread(mine, other, here, block, window, by))

    def residual(inner, count, flops):
        return call(
            functools.partial(residual_kernel, steps, inner),
            [((steps, count * tall, depth), "h")],
            "hhhhhhhhh",
            [
                pltpu.VMEM((columns, size + 16, depth), F32),
                pltpu.VMEM(u_init.shape, F32),
                pltpu.VMEM(u_init.shape, F32),
                pltpu.VMEM((steps, count * tall, depth), F32),
                pltpu.VMEM((2, size + 8, depth), F32),
                pltpu.VMEM((depth, size), F32),
                pltpu.VMEM((size, depth), F32),
                square,
                pltpu.VMEM((2, size, depth), F32),
                *constants,
                pltpu.SemaphoreType.DMA((3, columns)),
                pltpu.SemaphoreType.DMA((count // 2,)),
                pltpu.SemaphoreType.DMA((5,)),
            ],
            flops,
            mine, other, u_init, force[0], low, high, kappa, rates_row, basis,
        )[0]

    edge = residual(False, 2 * REACH, 2 * 10**9)
    edge = exchanged(edge)
    middle = residual(True, columns - 2 * REACH, 6 * 10**9)
    middle = exchanged(middle)
    kappa_wide = jnp.pad(kappa, ((0, 0), (REACH, REACH)))
    kappa_mine = lax.dynamic_slice_in_dim(kappa_wide, here * block, tall, 1)
    kappa_cells = jnp.broadcast_to(kappa_mine[:, :, None], kappa_mine.shape + (depth,)).reshape(-1, depth)

    def modes_scratch(width):
        return [
            pltpu.VMEM((width, broad, depth), F32),
            pltpu.VMEM((chips - 1, width, window, depth), F32),
            pltpu.VMEM((2, broad + 32, depth), F32),
            pltpu.VMEM((width * tall, depth), F32),
            square,
            *constants,
            pltpu.VMEM((steps, 2 * chunk, depth), F32),
            pltpu.VMEM((columns * tall, depth), F32),
            pltpu.SemaphoreType.DMA((2 * chips,)),
            pltpu.SemaphoreType.DMA((4,)),
        ]

    edge_low, edge_high = call(
        functools.partial(rim_kernel, block, chips - 1, [(0, REACH), (columns - REACH, columns)]),
        [((steps + 1, chunk, depth), "v")] * 2,
        "h" * (5 + chips),
        [pltpu.VMEM((chips, 2 * chunk, depth), F32)] + modes_scratch(2 * REACH),
        10**9,
        edge, mine, other, kappa_cells, rates_row, basis, *pieces,
    )
    left = shifted(edge_high, "tx", 1)
    right = shifted(edge_low, "tx", -1)
    far = [
        pltpu.VMEM((chips, inside * tall, depth), F32),
        pltpu.VMEM((columns * tall, depth), F32),
        pltpu.VMEM((columns * tall, depth), F32),
        pltpu.VMEM((2, steps + 1, chunk, depth), F32),
        pltpu.VMEM((depth + 8, depth), F32),
    ]
    rows = (chips - 1) * inside * tall + 3 * columns * tall + 2 * steps * chunk + depth + 8
    room = 16 * (middle.size + 2 * left.size + u_init.size)
    rows = max(rows, -(-(room + MIB) // (4096 * depth)) * 1024)
    bundle = call(
        functools.partial(fill_kernel, block, chips - 1, [(REACH, columns - REACH)]),
        [((rows, depth), "h")],
        "h" * (6 + chips),
        far + [pltpu.SemaphoreType.DMA((2 * steps + chips + 8,))] + modes_scratch(inside),
        10**9,
        mine, other, edge_low, edge_high, kappa_cells, rates_row, basis, *pieces,
    )[0]
    wide = pltpu.VMEM((total, depth), F32)
    back = call(
        functools.partial(relax_kernel, block),
        [((steps, columns * block, depth), "v")],
        "vvvh",
        [
            pltpu.VMEM((steps, total, depth), F32),
            pltpu.VMEM((steps, chunk, depth), F32),
            pltpu.VMEM((steps, total + 2 * front, depth), F32),
            pltpu.VMEM((steps, total + 2 * front, depth), F32),
            pltpu.VMEM((steps * block, depth), F32),
            square,
            far[0],
            wide,
            wide,
            wide,
            *far[3:],
            pltpu.SemaphoreType.DMA((2 * steps + chips + 3,)),
        ],
        10**9,
        middle, left, right, bundle,
        limit=VMEM_BYTES - room,
    )[0]
    arrived = exchanged(back).reshape(steps, columns, block, depth)
    return jnp.transpose(arrived, (1, 0, 2, 3)).reshape(1, columns, size, depth)


def solution(mesh):
    return jax.shard_map(
        correction,
        mesh=mesh,
        in_specs=(
            P("tm", "tx", None, None),
            P("tm", "tx", None, None),
            P("tx", None, None),
            P("tx", None),
            P(),
            P(),
        ),
        out_specs=P("tm", "tx", None, None),
        check_vma=False,
    )
```

time: 113 us -> 129 us (1.14)
  waiting for transfers between devices: 12.9 us -> 37.3 us
  local copies, waits for them, and re-layouts: 9.82 us -> 4.94 us
  starting transfers between devices: 31.4 us -> 27.3 us
  other arithmetic: 0.2 us -> 2.64 us
  blocking collectives: 30.7 us -> 29.2 us
    ppermute x7 -> x4, waiting for transfers between devices: 4.31 us -> 24.2 us  [the longest x3 24.2 us: spread(): lax.ppermute(rows, 'tm', [(i, (i + 2 * by) % count) for i in range(count...]
    ppermute x4, waiting for transfers between devices: 6.6 us -> 11.3 us  [shifted(): return lax.ppermute(array, axis, pairs)]
    all_to_all x2, starting transfers between devices: 11.1 us -> 7.2 us  [exchanged(): return lax.all_to_all(array, 'tm', split_axis=0, concat_axis=0, tiled=True)]
    dynamic_slice x1, local copies, waits for them, and re-layouts: 2.76 us -> 0.08 us  [correction(): kappa_mine = lax.dynamic_slice_in_dim(kappa_wide, here * block, tall, 1)]
    select_n x0 -> x1, other arithmetic: none -> 2.64 us  [spread(): jnp.where(here % 2 == 1, lax.dynamic_slice_in_dim(mine, start, window, 1)...]
    ppermute x4, starting transfers between devices: 12.3 us -> 10.6 us  [shifted(): return lax.ppermute(array, axis, pairs)]
    ppermute x7 -> x4, starting transfers between devices: 8.02 us -> 9.57 us  [the longest x3 9.07 us: spread(): lax.ppermute(rows, 'tm', [(i, (i + 2 * by) % count) for i in range(count...]
    all_to_all x1, blocking collectives: 30.7 us -> 29.2 us  [exchanged(): return lax.all_to_all(array, 'tm', split_axis=0, concat_axis=0, tiled=True)]
  transfers between devices with their start and end apart: 13 -> 10, of which waited for: 5 -> 8; matrix products, arithmetic and copies ran while one was open for 5% -> 4% of each run, Pallas kernels for 16% -> 13%
where the time goes in v2:
time: 129 us; the launch traced here: 128 us
  waiting for transfers between devices  37.3 us (29%)
  blocking collectives  29.2 us (23%)
  starting transfers between devices  27.3 us (21%)
  Pallas kernels  26.8 us (21%)
  local copies, waits for them, and re-layouts  4.94 us (4%)
  other arithmetic  2.64 us (2%)
    all_to_all x1, blocking collectives, exchanged(): return lax.all_to_all(array, 'tm', split_axis=0, concat_axis=0, tiled=True)  29.2 us
    pallas_call x5, Pallas kernels, call(): pl.pallas_call(kernel, out_shape=shapes, in_specs=[pl.BlockSpec(memory_sp...  26.8 us
    ppermute x3, waiting for transfers between devices, spread(): lax.ppermute(rows, 'tm', [(i, (i + 2 * by) % count) for i in range(count...  24.2 us
    ppermute x4, waiting for transfers between devices, shifted(): return lax.ppermute(array, axis, pairs)  11.3 us
    ppermute x4, starting transfers between devices, shifted(): return lax.ppermute(array, axis, pairs)  10.6 us
    ppermute x3, starting transfers between devices, spread(): lax.ppermute(rows, 'tm', [(i, (i + 2 * by) % count) for i in range(count...  9.07 us
    all_to_all x2, starting transfers between devices, exchanged(): return lax.all_to_all(array, 'tm', split_axis=0, concat_axis=0, tiled=True)  7.2 us
    select_n x1, other arithmetic, spread(): jnp.where(here % 2 == 1, lax.dynamic_slice_in_dim(mine, start, window, 1)...  2.64 us
  transfers between devices with their start and end apart: 10, of which 8 were waited for; matrix products, arithmetic and copies ran while one was open for 4% of the time, Pallas kernels for 13%

profile of v2, /device:TPU:0, one launch (start us, length us, event | category | flops | bytes accessed | tf_op | source)
XLA Modules:
  0.0 128.5 jit_solution(11490984290241507405)
XLA Ops:
  0.0 0.5 collective-permute-start
  0.5 1.0 slice_bitcast_fusion
  1.5 4.5 %collective-permute-start.1 = (f32[256,128]{1,0:T(8,128)S(1)}, f32[256,128]{1,0:T(8,128)S(1)}, u32[]{:S(2)}, u32[]{:S(2)}) collective-permute-start(f32[256,128]{1,0:T(8,128)S(1)} %get-tuple-element.13), channel_id=1, source_target_pairs={{0,1},{1,2},{2,3},{4,5},{5,6},{6,7},{8,9},{9,10},{10,11},{12,13},{... | collective-permute-start | bytes 393224 | tf_op jit(solution)/shard_map/ppermute | solution.py:31
  6.0 1.3 %collective-permute-start.2 = (f32[256,128]{1,0:T(8,128)S(1)}, f32[256,128]{1,0:T(8,128)S(1)}, u32[]{:S(2)}, u32[]{:S(2)}) collective-permute-start(f32[256,128]{1,0:T(8,128)S(1)} %get-tuple-element.12), channel_id=1, source_target_pairs={{1,0},{2,1},{3,2},{5,4},{6,5},{7,6},{9,8},{10,9},{11,10},{13,12},{... | collective-permute-start | bytes 393224 | tf_op jit(solution)/shard_map/ppermute | solution.py:31
  7.3 2.1 %collective-permute-done.1.low = f32[256,128]{1,0:T(8,128)S(1)} collective-permute-done((f32[256,128]{1,0:T(8,128)S(1)}, f32[256,128]{1,0:T(8,128)S(1)}, u32[]{:S(2)}, u32[]{:S(2)}) %collective-permute-start.1) | collective-permute-done | bytes 131104 | tf_op jit(solution)/shard_map/ppermute | solution.py:31
  9.4 0.0 copy-start.5
  9.4 4.1 %collective-permute-done.2.high = f32[256,128]{1,0:T(8,128)S(1)} collective-permute-done((f32[256,128]{1,0:T(8,128)S(1)}, f32[256,128]{1,0:T(8,128)S(1)}, u32[]{:S(2)}, u32[]{:S(2)}) %collective-permute-start.2) | collective-permute-done | bytes 131104 | tf_op jit(solution)/shard_map/ppermute | solution.py:31
  13.5 0.0 copy-start.6
  13.5 0.0 collective-permute-done.other
  13.5 0.0 copy-start
  13.5 0.0 copy-done.5
  13.5 0.6 copy-done.6
  14.1 0.7 copy-done
  14.8 4.5 %shard_map.65 = f32[8,144,128]{2,1,0:T(8,128)} custom-call(f32[16,256,128]{2,1,0:T(8,128)} %bitcast.18, f32[16,256,128]{2,1,0:T(8,128)} %copy-done, f32[16,256,128]{2,1,0:T(8,128)} %initial.3, f32[16,256,128]{2,1,0:T(8,128)} %bitcast.23, f32[256,128]{1,0:T(8,128)} %copy-done.5, f32[256,128]{1,0:T(8,128)} %copy-done.6, f32[16,256]{1,0:T(8,128)} %kappa.3, ...), custom_call_target="tpu_custom_call" | custom-call | flops 2000000000 | bytes 1000000 | tf_op jit(solution)/shard_map/pallas_call | solution.py:450
  19.3 3.6 %all-to-all-start.1 = ((f32[8,144,128]{2,1,0:T(8,128)}), f32[8,144,128]{2,1,0:T(8,128)S(1)}, u32[]{:S(2)}, u32[]{:S(2)}) async-start(f32[8,144,128]{2,1,0:T(8,128)} %shard_map.65), calls=%async_computation.1 | async-start | bytes 1179648 | tf_op jit(solution)/shard_map/all_to_all | solution.py:467
  22.9 8.6 %shard_map.64 = f32[8,432,128]{2,1,0:T(8,128)} custom-call(f32[16,256,128]{2,1,0:T(8,128)} %bitcast.19, f32[16,256,128]{2,1,0:T(8,128)} %copy-done, f32[16,256,128]{2,1,0:T(8,128)} %initial.3, f32[16,256,128]{2,1,0:T(8,128)} %bitcast.24, f32[256,128]{1,0:T(8,128)} %copy-done.5, f32[256,128]{1,0:T(8,128)} %copy-done.6, f32[16,256]{1,0:T(8,128)} %kappa.3, ...), custom_call_target="tpu_custom_call" | custom-call | flops 6000000000 | bytes 1000000 | tf_op jit(solution)/shard_map/pallas_call | solution.py:450
  31.5 1.8 %all-to-all-done.1.edge = f32[8,144,128]{2,1,0:T(8,128)S(1)} async-done(((f32[8,144,128]{2,1,0:T(8,128)}), f32[8,144,128]{2,1,0:T(8,128)S(1)}, u32[]{:S(2)}, u32[]{:S(2)}) %all-to-all-start.1) | async-done | bytes 589856 | tf_op jit(solution)/shard_map/all_to_all | solution.py:467
  33.3 0.0 copy-start.1
  33.3 3.6 %all-to-all-start = ((f32[8,432,128]{2,1,0:T(8,128)}), f32[8,432,128]{2,1,0:T(8,128)S(1)}, u32[]{:S(2)}, u32[]{:S(2)}) async-start(f32[8,432,128]{2,1,0:T(8,128)} %shard_map.64), calls=%async_computation | async-start | bytes 3538944 | tf_op jit(solution)/shard_map/all_to_all | solution.py:467
  36.9 0.0 copy-start.7
  37.0 2.6 %bitcast_select_fusion = (f32[16,40,128]{2,1,0:T(8,128)}, f32[16,40,128]{2,1,0:T(8,128)}, f32[16,40,128]{2,1,0:T(8,128)}) fusion(f32[16,256,128]{2,1,0:T(8,128)} %copy-done, s32[]{:T(128)S(6)} %min.12, f32[1,16,256,128]{3,2,1,0:T(8,128)} %param.6, pred[]{:T(512)S(6)} %eq.12, s32[]{:T(128)S(6)} %min.11, s32[]{:T(128)S(6)} %min.10), kind=kLoop, calls=%fused_computation | loop fusion | flops 245760 | bytes 2949133 | tf_op jit(solution)/shard_map/jit(_where)/select_n | solution.py:481
  39.6 0.0 copy-done.1
  39.6 3.8 %collective-permute-start.3 = (f32[16,40,128]{2,1,0:T(8,128)}, f32[16,40,128]{2,1,0:T(8,128)S(1)}, u32[]{:S(2)}, u32[]{:S(2)}) collective-permute-start(f32[16,40,128]{2,1,0:T(8,128)} %get-tuple-element.11), channel_id=1, source_target_pairs={{0,8},{4,12},{8,16},{12,20},{16,24},{20,28},{1,9},{5,13},{9,17},{1... | collective-permute-start | bytes 983048 | tf_op jit(solution)/shard_map/ppermute | solution.py:486
  43.5 3.3 %collective-permute-start.4 = (f32[16,40,128]{2,1,0:T(8,128)}, f32[16,40,128]{2,1,0:T(8,128)S(1)}, u32[]{:S(2)}, u32[]{:S(2)}) collective-permute-start(f32[16,40,128]{2,1,0:T(8,128)} %get-tuple-element.10), channel_id=1, source_target_pairs={{0,16},{4,20},{8,24},{12,28},{16,0},{20,4},{1,17},{5,21},{9,25},{1... | collective-permute-start | bytes 983048 | tf_op jit(solution)/shard_map/ppermute | solution.py:486
  46.8 1.9 %collective-permute-start.5 = (f32[16,40,128]{2,1,0:T(8,128)}, f32[16,40,128]{2,1,0:T(8,128)S(1)}, u32[]{:S(2)}, u32[]{:S(2)}) collective-permute-start(f32[16,40,128]{2,1,0:T(8,128)} %get-tuple-element.9), channel_id=1, source_target_pairs={{0,24},{4,28},{8,0},{12,4},{16,8},{20,12},{1,25},{5,29},{9,1},{13,... | collective-permute-start | bytes 983048 | tf_op jit(solution)/shard_map/ppermute | solution.py:486
  48.7 0.0 copy-done.7
  48.7 0.1 pad_dynamic-slice_fusion
  48.8 0.1 broadcast_in_dim.8
  48.9 15.4 %collective-permute-done.3.rest_0_ = f32[16,40,128]{2,1,0:T(8,128)S(1)} collective-permute-done((f32[16,40,128]{2,1,0:T(8,128)}, f32[16,40,128]{2,1,0:T(8,128)S(1)}, u32[]{:S(2)}, u32[]{:S(2)}) %collective-permute-start.3) | collective-permute-done | bytes 327712 | tf_op jit(solution)/shard_map/ppermute | solution.py:486
  64.3 0.0 copy-start.2
  64.3 6.7 %collective-permute-done.4.rest_1_ = f32[16,40,128]{2,1,0:T(8,128)S(1)} collective-permute-done((f32[16,40,128]{2,1,0:T(8,128)}, f32[16,40,128]{2,1,0:T(8,128)S(1)}, u32[]{:S(2)}, u32[]{:S(2)}) %collective-permute-start.4) | collective-permute-done | bytes 327712 | tf_op jit(solution)/shard_map/ppermute | solution.py:486
  71.0 0.0 copy-start.3
  71.1 2.1 %collective-permute-done.5.rest_2_ = f32[16,40,128]{2,1,0:T(8,128)S(1)} collective-permute-done((f32[16,40,128]{2,1,0:T(8,128)}, f32[16,40,128]{2,1,0:T(8,128)S(1)}, u32[]{:S(2)}, u32[]{:S(2)}) %collective-permute-start.5) | collective-permute-done | bytes 327712 | tf_op jit(solution)/shard_map/ppermute | solution.py:486
  73.1 0.0 copy-start.4
  73.1 0.9 broadcast_in_dim.9.kappa
  74.0 0.0 copy-done.2
  74.0 0.0 copy-done.3
  74.0 0.0 copy-done.4
  74.0 3.2 %shard_map.66 = (f32[9,72,128]{2,1,0:T(8,128)}, f32[9,72,128]{2,1,0:T(8,128)}) custom-call(f32[8,144,128]{2,1,0:T(8,128)} %copy-done.1, f32[16,256,128]{2,1,0:T(8,128)} %bitcast.20, f32[16,256,128]{2,1,0:T(8,128)} %copy-done, f32[576,128]{1,0:T(8,128)} %broadcast_in_dim.9.kappa, f32[1,128]{1,0:T(1,128)} %bitcast.27, f32[128,128]{1,0:T(8,128)} %basis.7, ...), custom_call_target="tpu_custom_call" | custom-call | flops 1000000000 | bytes 1000000 | tf_op jit(solution)/shard_map/pallas_call | solution.py:450
  77.2 3.5 %collective-permute-start.6 = (f32[9,72,128]{2,1,0:T(8,128)}, f32[9,72,128]{2,1,0:T(8,128)S(1)}, u32[]{:S(2)}, u32[]{:S(2)}) collective-permute-start(f32[9,72,128]{2,1,0:T(8,128)} %get-tuple-element.7.edge_high), channel_id=1, source_target_pairs={{0,1},{1,2},{2,3},{4,5},{5,6},{6,7},{8,9},{9,10},{10,11},{12,13},{... | collective-permute-start | bytes 995336 | tf_op jit(solution)/shard_map/ppermute | solution.py:31
  80.7 1.3 %collective-permute-start.7 = (f32[9,72,128]{2,1,0:T(8,128)}, f32[9,72,128]{2,1,0:T(8,128)S(1)}, u32[]{:S(2)}, u32[]{:S(2)}) collective-permute-start(f32[9,72,128]{2,1,0:T(8,128)} %get-tuple-element.8.edge_low), channel_id=1, source_target_pairs={{1,0},{2,1},{3,2},{5,4},{6,5},{7,6},{9,8},{10,9},{11,10},{13,12},{... | collective-permute-start | bytes 995336 | tf_op jit(solution)/shard_map/ppermute | solution.py:31
  82.0 4.6 %shard_map.67.bundle = f32[37888,128]{1,0:T(8,128)} custom-call(f32[16,256,128]{2,1,0:T(8,128)} %bitcast.21, f32[16,256,128]{2,1,0:T(8,128)} %copy-done, f32[9,72,128]{2,1,0:T(8,128)} %get-tuple-element.8.edge_low, f32[9,72,128]{2,1,0:T(8,128)} %get-tuple-element.7.edge_high, f32[576,128]{1,0:T(8,128)} %broadcast_in_dim.9.kappa, f32[1,128]{1,0:T(1,128)} %bitcast.28, ...), custom_call_target="tpu_custom_call" | custom-call | flops 1000000000 | bytes 1000000 | tf_op jit(solution)/shard_map/pallas_call | solution.py:450
  86.7 1.1 collective-permute-done.6.left
  87.7 4.0 %collective-permute-done.7.right = f32[9,72,128]{2,1,0:T(8,128)S(1)} collective-permute-done((f32[9,72,128]{2,1,0:T(8,128)}, f32[9,72,128]{2,1,0:T(8,128)S(1)}, u32[]{:S(2)}, u32[]{:S(2)}) %collective-permute-start.7) | collective-permute-done | bytes 331808 | tf_op jit(solution)/shard_map/ppermute | solution.py:31
  91.8 0.0 all-to-all-done.middle
  91.8 5.9 %shard_map.68 = f32[8,512,128]{2,1,0:T(8,128)S(1)} custom-call(f32[8,432,128]{2,1,0:T(8,128)S(1)} %all-to-all-done.middle, f32[9,72,128]{2,1,0:T(8,128)S(1)} %collective-permute-done.6.left, f32[9,72,128]{2,1,0:T(8,128)S(1)} %collective-permute-done.7.right, f32[37888,128]{1,0:T(8,128)} %shard_map.67.bundle), custom_call_target="tpu_custom_call" | custom-call | flops 1000000000 | bytes 1000000 | tf_op jit(solution)/shard_map/pallas_call | solution.py:450
  97.6 29.2 %all_to_all.15 = f32[8,512,128]{2,1,0:T(8,128)S(1)} all-to-all(f32[8,512,128]{2,1,0:T(8,128)S(1)} %shard_map.68), channel_id=1, replica_groups=mesh['tm'=8,'tx'=4] {'tm'}, dimensions={0} | all-to-all | bytes 4194304 | tf_op jit(solution)/shard_map/all_to_all | solution.py:467
  126.9 1.6 %copy.7 = f32[16,8,32,128]{3,2,1,0:T(8,128)} copy(f32[16,8,32,128]{3,2,0,1:T(8,128)S(1)} %bitcast.22) | data formatting | bytes 4194304 | tf_op jit(solution)/shard_map/transpose | solution.py:611
Async XLA Ops:
  0.0 13.5 %collective-permute-start = (f32[16,256,128]{2,1,0:T(8,128)}, f32[16,256,128]{2,1,0:T(8,128)S(1)}, u32[]{:S(2)}, u32[]{:S(2)}) collective-permute-start(f32[16,256,128]{2,1,0:T(8,128)} %bitcast.17), channel_id=1, source_target_pairs={{0,4},{4,0},{8,12},{12,8},{16,20},{20,16},{24,28},{28,24},{1,5},{5... | collective-permute-start | bytes 6291464 | tf_op jit(solution)/shard_map/ppermute | solution.py:463
  1.5 7.9 %collective-permute-start.1 = (f32[256,128]{1,0:T(8,128)S(1)}, f32[256,128]{1,0:T(8,128)S(1)}, u32[]{:S(2)}, u32[]{:S(2)}) collective-permute-start(f32[256,128]{1,0:T(8,128)S(1)} %get-tuple-element.13), channel_id=1, source_target_pairs={{0,1},{1,2},{2,3},{4,5},{5,6},{6,7},{8,9},{9,10},{10,11},{12,13},{... | collective-permute-start | bytes 393224 | tf_op jit(solution)/shard_map/ppermute | solution.py:31
  6.0 7.5 %collective-permute-start.2 = (f32[256,128]{1,0:T(8,128)S(1)}, f32[256,128]{1,0:T(8,128)S(1)}, u32[]{:S(2)}, u32[]{:S(2)}) collective-permute-start(f32[256,128]{1,0:T(8,128)S(1)} %get-tuple-element.12), channel_id=1, source_target_pairs={{1,0},{2,1},{3,2},{5,4},{6,5},{7,6},{9,8},{10,9},{11,10},{13,12},{... | collective-permute-start | bytes 393224 | tf_op jit(solution)/shard_map/ppermute | solution.py:31
  9.4 4.1 %copy-start.5 = (f32[256,128]{1,0:T(8,128)}, f32[256,128]{1,0:T(8,128)S(1)}, u32[]{:S(2)}) copy-start(f32[256,128]{1,0:T(8,128)S(1)} %collective-permute-done.1.low) | copy-start | bytes 393220
  13.5 0.7 copy-start.6
  13.5 1.4 %copy-start = (f32[16,256,128]{2,1,0:T(8,128)}, f32[16,256,128]{2,1,0:T(8,128)S(1)}, u32[]{:S(2)}) copy-start(f32[16,256,128]{2,1,0:T(8,128)S(1)} %collective-permute-done.other) | copy-start | bytes 6291460
  19.3 14.0 %all-to-all-start.1 = ((f32[8,144,128]{2,1,0:T(8,128)}), f32[8,144,128]{2,1,0:T(8,128)S(1)}, u32[]{:S(2)}, u32[]{:S(2)}) async-start(f32[8,144,128]{2,1,0:T(8,128)} %shard_map.65), calls=%async_computation.1 | async-start | bytes 1179648 | tf_op jit(solution)/shard_map/all_to_all | solution.py:467
  33.3 6.3 %copy-start.1 = (f32[8,144,128]{2,1,0:T(8,128)}, f32[8,144,128]{2,1,0:T(8,128)S(1)}, u32[]{:S(2)}) copy-start(f32[8,144,128]{2,1,0:T(8,128)S(1)} %all-to-all-done.1.edge) | copy-start | bytes 1769476
  33.3 58.4 %all-to-all-start = ((f32[8,432,128]{2,1,0:T(8,128)}), f32[8,432,128]{2,1,0:T(8,128)S(1)}, u32[]{:S(2)}, u32[]{:S(2)}) async-start(f32[8,432,128]{2,1,0:T(8,128)} %shard_map.64), calls=%async_computation | async-start | bytes 3538944 | tf_op jit(solution)/shard_map/all_to_all | solution.py:467
  36.9 11.8 %copy-start.7 = (f32[16,256]{1,0:T(8,128)S(1)}, f32[16,256]{1,0:T(8,128)}, u32[]{:S(2)}) copy-start(f32[16,256]{1,0:T(8,128)} %kappa.3) | copy-start | bytes 49156
  39.6 24.7 %collective-permute-start.3 = (f32[16,40,128]{2,1,0:T(8,128)}, f32[16,40,128]{2,1,0:T(8,128)S(1)}, u32[]{:S(2)}, u32[]{:S(2)}) collective-permute-start(f32[16,40,128]{2,1,0:T(8,128)} %get-tuple-element.11), channel_id=1, source_target_pairs={{0,8},{4,12},{8,16},{12,20},{16,24},{20,28},{1,9},{5,13},{9,17},{1... | collective-permute-start | bytes 983048 | tf_op jit(solution)/shard_map/ppermute | solution.py:486
  43.5 27.6 %collective-permute-start.4 = (f32[16,40,128]{2,1,0:T(8,128)}, f32[16,40,128]{2,1,0:T(8,128)S(1)}, u32[]{:S(2)}, u32[]{:S(2)}) collective-permute-start(f32[16,40,128]{2,1,0:T(8,128)} %get-tuple-element.10), channel_id=1, source_target_pairs={{0,16},{4,20},{8,24},{12,28},{16,0},{20,4},{1,17},{5,21},{9,25},{1... | collective-permute-start | bytes 983048 | tf_op jit(solution)/shard_map/ppermute | solution.py:486
  46.8 26.3 %collective-permute-start.5 = (f32[16,40,128]{2,1,0:T(8,128)}, f32[16,40,128]{2,1,0:T(8,128)S(1)}, u32[]{:S(2)}, u32[]{:S(2)}) collective-permute-start(f32[16,40,128]{2,1,0:T(8,128)} %get-tuple-element.9), channel_id=1, source_target_pairs={{0,24},{4,28},{8,0},{12,4},{16,8},{20,12},{1,25},{5,29},{9,1},{13,... | collective-permute-start | bytes 983048 | tf_op jit(solution)/shard_map/ppermute | solution.py:486
  64.3 9.7 %copy-start.2 = (f32[16,40,128]{2,1,0:T(8,128)}, f32[16,40,128]{2,1,0:T(8,128)S(1)}, u32[]{:S(2)}) copy-start(f32[16,40,128]{2,1,0:T(8,128)S(1)} %collective-permute-done.3.rest_0_) | copy-start | bytes 983044
  71.0 3.0 %copy-start.3 = (f32[16,40,128]{2,1,0:T(8,128)}, f32[16,40,128]{2,1,0:T(8,128)S(1)}, u32[]{:S(2)}) copy-start(f32[16,40,128]{2,1,0:T(8,128)S(1)} %collective-permute-done.4.rest_1_) | copy-start | bytes 983044
  73.1 0.9 copy-start.4
  77.2 10.5 %collective-permute-start.6 = (f32[9,72,128]{2,1,0:T(8,128)}, f32[9,72,128]{2,1,0:T(8,128)S(1)}, u32[]{:S(2)}, u32[]{:S(2)}) collective-permute-start(f32[9,72,128]{2,1,0:T(8,128)} %get-tuple-element.7.edge_high), channel_id=1, source_target_pairs={{0,1},{1,2},{2,3},{4,5},{5,6},{6,7},{8,9},{9,10},{10,11},{12,13},{... | collective-permute-start | bytes 995336 | tf_op jit(solution)/shard_map/ppermute | solution.py:31
  80.7 11.1 %collective-permute-start.7 = (f32[9,72,128]{2,1,0:T(8,128)}, f32[9,72,128]{2,1,0:T(8,128)S(1)}, u32[]{:S(2)}, u32[]{:S(2)}) collective-permute-start(f32[9,72,128]{2,1,0:T(8,128)} %get-tuple-element.8.edge_low), channel_id=1, source_target_pairs={{1,0},{2,1},{3,2},{5,4},{6,5},{7,6},{9,8},{10,9},{11,10},{13,12},{... | collective-permute-start | bytes 995336 | tf_op jit(solution)/shard_map/ppermute | solution.py:31

commit v3 on v2

--- a/solution.py
+++ b/solution.py
@@ -70,16 +70,32 @@
     odd = step_here % 2 == 1
     first = step_here == 0
     if inner:
-        mine = list(range(2, columns - 2))
-        wide = list(range(1, columns - 1))
+        group = 4 if (columns - 4) % 4 == 0 else 2
+        count = (columns - 4) // group
+        spans = [(2 + group * step, group) for step in range(count)]
+        wide = [(1 if step == 0 else start + 1, group + 2 if step == 0 else group) for step, (start, _) in enumerate(spans)]
     else:
-        mine = [0, 1, columns - 2, columns - 1]
-        wide = [0, 1, 2, columns - 3, columns - 2, columns - 1]
-
-    def load(kind, x):
-        source, target = ((state, here), (other, past), (force, pushed))[kind]
-        target = target.at[x, pl.ds(8, size), :] if kind == 0 else target.at[x]
-        return pltpu.make_async_copy(source.at[x], target, loads.at[kind, x])
+        group = 2
+        count = 2
+        spans = [(0, 2), (columns - 2, 2)]
+        wide = [(0, 3), (columns - 3, 3)]
+
+    def load(kind, step, source=None):
+        start, extent = (wide if kind == 0 else spans)[step]
+        take = pl.ds(start, extent)
+        source = (state, other, force)[kind] if source is None else source
+        target = here.at[take, pl.ds(8, size), :] if kind == 0 else (past, pushed)[kind - 1].at[take]
+        return pltpu.make_async_copy(source.at[take], target, loads.at[kind, step])
+
+    def arrive(step):
+        start = pl.ds(0, group)
+        pltpu.make_async_copy(force.at[start], pushed.at[start], loads.at[2, step]).wait()
+        if inner:
+            pltpu.make_async_copy(state.at[start], here.at[start, pl.ds(8, size), :], loads.at[0, step]).wait()
+
+        @pl.when(jnp.logical_or(odd, first))
+        def _():
+            pltpu.make_async_copy(other.at[start], past.at[start], loads.at[1, step]).wait()
 
     def level(x):
         return here[x, pl.ds(8, size), :]
@@ -91,20 +107,19 @@
     levels[...] = jnp.zeros_like(levels)
     for copy in small:
         copy.start()
-    for x in wide:
-        load(0, x).start()
-        if x in mine:
-            load(2, x).start()
+    for step in range(count):
+        load(0, step).start()
+        load(2, step).start()
 
     @pl.when(odd)
     def _():
-        for x in mine:
-            load(1, x).start()
+        for step in range(count):
+            load(1, step).start()
 
     @pl.when(first)
     def _():
-        for x in mine:
-            pltpu.make_async_copy(initial.at[x], past.at[x], loads.at[1, x]).start()
+        for step in range(count):
+            load(1, step, initial).start()
 
     here[:, :8, :] = jnp.zeros((columns, 8, depth), F32)
     here[:, 8 + size :, :] = jnp.zeros((columns, 8, depth), F32)
@@ -118,62 +133,62 @@
         where = pl.ds(part * depth, depth)
         turned[where, :] = jnp.transpose(levels[:, where])
 
-    def column(x, left, right, base, which):
-        load(2, x).wait()
-
-        @pl.when(jnp.logical_or(odd, first))
-        def _():
-            load(1, x).wait()
-
+    def residual(x, left, right, across):
         center = level(x)
-        up = here[x, pl.ds(7, size), :]
-        down = here[x, pl.ds(9, size), :]
         square = center * center
-        beside = left + right + up + down
-        across = jnp.broadcast_to(pltpu.roll(turned[...], (depth - x) % depth, 1)[:, :1], (size, depth))
-        value = (
+        beside = left + right + here[x, pl.ds(7, size), :] + here[x, pl.ds(9, size), :]
+        return (
             pushed[x]
             - center
             + jnp.where(jnp.logical_or(odd, first), past[x], 0.0)
             - across * (4.0 * center - beside)
             - 0.5 * (square * center) / (1.0 + square)
         )
-        value_high, value_low = split(value)
-        center_high, center_low = split(center)
-        joined_high = jnp.concatenate([value_high, center_high], axis=1)
-        joined_low = jnp.concatenate([value_low, center_low], axis=1)
-        product = dot(joined_high, weights[...])
-        modal = product[:, :depth] + product[:, depth:] + dot(joined_low, weights[:, :depth])
-        cut(modal, rows.at[which], parts, base, blocks)
+
+    def columns_of(x, group, sides_of, base):
+        rolled = turned[...] if isinstance(x, int) else pltpu.roll(turned[...], depth - x, 1)
+        at = x if isinstance(x, int) else 0
+        for begin in range(0, group, 2):
+            highs, lows = [], []
+            for which in range(begin, begin + 2):
+                across = jnp.broadcast_to(rolled[:, at + which : at + which + 1], (size, depth))
+                value_high, value_low = split(residual(x + which, *sides_of(x + which), across))
+                center_high, center_low = split(level(x + which))
+                highs.append(jnp.concatenate([value_high, center_high], axis=1))
+                lows.append(jnp.concatenate([value_low, center_low], axis=1))
+            product = dot(jnp.concatenate(highs, axis=0), weights[...])
+            modal = product[:, :depth] + product[:, depth:] + dot(jnp.concatenate(lows, axis=0), weights[:, :depth])
+            for which in range(2):
+                part = modal[which * size : (which + 1) * size]
+                cut(part, rows.at[begin + which], parts, base + (begin + which) * tall, blocks)
 
     def store(step):
-        where = pl.ds(pl.multiple_of(step * 2 * tall, 8), 2 * tall)
+        where = pl.ds(pl.multiple_of(step * group * tall, 8), group * tall)
         return pltpu.make_async_copy(parts.at[:, where, :], out.at[:, where, :], stores.at[step])
 
     if inner:
-        load(0, 1).wait()
-        load(0, 2).wait()
+        pair_of = pl.ds(0, 2)
+        pltpu.make_async_copy(state.at[pair_of], here.at[pair_of, pl.ds(8, size), :], loads.at[0, 0]).wait()
 
         def pair(step, carry):
-            base = pl.multiple_of(step * 2 * tall, 8)
-            for which in range(2):
-                x = 2 + 2 * step + which
-                load(0, x + 1).wait()
-                column(x, level(x - 1), level(x + 1), base + which * tall, which)
+            base = pl.multiple_of(step * group * tall, 8)
+            x = 2 + group * step
+            arrive(step)
+            columns_of(x, group, lambda at: (level(at - 1), level(at + 1)), base)
             store(step).start()
             return carry
 
-        lax.fori_loop(0, len(mine) // 2, pair, 0)
+        lax.fori_loop(0, count, pair, 0)
     else:
-        for x in wide:
-            load(0, x).wait()
-        column(0, sides[0], level(1), 0, 0)
-        column(1, level(0), level(2), tall, 1)
+        for step in range(count):
+            load(0, step).wait()
+            arrive(step)
+        columns_of(0, 2, lambda at: (sides[0] if at == 0 else level(0), level(at + 1)), 0)
         store(0).start()
-        column(columns - 2, level(columns - 3), level(columns - 1), 2 * tall, 0)
-        column(columns - 1, level(columns - 2), sides[1], 3 * tall, 1)
+        last = columns - 1
+        columns_of(last - 1, 2, lambda at: (level(at - 1), sides[1] if at == last else level(last)), 2 * tall)
         store(1).start()
-    for step in range(len(mine) // 2):
+    for step in range(count):
         store(step).wait()
 
 
@@ -240,19 +255,22 @@
         copy.wait()
     begin = block * here - REACH + room
 
+    def keep(slot, value):
+        first_out[pl.ds(pl.multiple_of(slot * (width * tall), 8), width * tall), :] = value
+
     def gather(source, start, extent):
         for x in range(width):
             strip[x % 2, pl.ds(room, extent), :] = source(x)
             gathered[pl.ds(x * tall, tall), :] = strip[x % 2, pl.ds(begin - start, tall), :]
         return times_matrix(gathered[...], weights)
 
-    first_out[chip] = gather(lambda x: near[x], near_start, broad)
+    keep(chip, gather(lambda x: near[x], near_start, broad))
 
     far_start = window_start(here, block, window, size)
     strip[...] = jnp.zeros_like(strip)
 
     def far_slot(by, carry):
-        first_out[(chip - by - 1 + chips) % chips] = gather(lambda x: far[by, x], far_start, window)
+        keep((chip - by - 1 + chips) % chips, gather(lambda x: far[by, x], far_start, window))
         return carry
 
     lax.fori_loop(0, count, far_slot, 0)
@@ -262,12 +280,13 @@
             left = edges[n, :two, :]
             right = edges[n, two:, :]
             if n and n % 2 == 0:
-                left = left + first_out[n // 2 - 1, :two, :]
-                right = right + first_out[n // 2 - 1, two:, :]
-            second_out[n] = left
-            third_out[n] = right
-        second_out[steps] = cells[:two, :]
-        third_out[steps] = cells[cells.shape[0] - two :, :]
+                at = (n // 2 - 1) * 2 * two
+                left = left + first_out[at : at + two, :]
+                right = right + first_out[at + two : at + 2 * two, :]
+            second_out[n * two : (n + 1) * two, :] = left
+            third_out[n * two : (n + 1) * two, :] = right
+        second_out[steps * two :, :] = cells[:two, :]
+        third_out[steps * two :, :] = cells[cells.shape[0] - two :, :]
 
 
 def time_factors(kappa, rates, steps):
@@ -286,7 +305,6 @@
 def fill_kernel(block, count, spans, state, other, edge_low, edge_high, kappa, rates, basis, *rest):
     bundle, scratch = rest[count], rest[count + 1 :]
     modal, inverse, ending, ends, turned, sems = scratch[:6]
-    steps = edge_low.shape[0] - 1
     sides = [pltpu.make_async_copy(edge, ends.at[i], sems.at[i]) for i, edge in enumerate((edge_low, edge_high))]
     for copy in sides:
         copy.start()
@@ -299,7 +317,7 @@
         copy.wait()
     copies = [
         pltpu.make_async_copy(source, bundle.at[pl.ds(start, source.shape[0]), :], sems.at[2 + i])
-        for i, (source, start) in enumerate(bundle_parts(modal, cells, inverse, ending, ends, turned, steps))
+        for i, (source, start) in enumerate(bundle_parts(modal, cells, inverse, ending, ends, turned))
     ]
     for copy in copies:
         copy.start()
@@ -307,12 +325,10 @@
         copy.wait()
 
 
-def bundle_parts(modal, cells, inverse, ending, ends, turned, steps):
-    parts = [modal.at[m] for m in range(steps // 2 - 1)] + [cells, inverse, ending]
-    parts += [ends.at[side, n] for side in range(2) for n in range(steps)] + [turned]
+def bundle_parts(modal, cells, inverse, ending, ends, turned):
     placed = []
     at = 0
-    for part in parts:
+    for part in (cells, inverse, ending, ends.at[0], ends.at[1], turned, modal):
         placed.append((part, at))
         at += part.shape[0]
     return placed
@@ -330,7 +346,7 @@
     pad = older.shape[1] - total
     front = pad // 2
     own = pl.ds(chunk, total - 2 * chunk)
-    parts = bundle_parts(modal, kappa.at[own, :], inverse.at[own, :], ending.at[own, :], ends, turned, steps)
+    parts = bundle_parts(modal, kappa.at[own, :], inverse.at[own, :], ending.at[own, :], ends, turned)
     copies = [
         pltpu.make_async_copy(bundle.at[pl.ds(start, target.shape[0]), :], target, loads.at[i])
         for i, (target, start) in enumerate(parts)
@@ -340,8 +356,8 @@
     older[:, :front, :] = jnp.zeros((steps, front, depth), F32)
     older[:, front + total :, :] = jnp.zeros((steps, pad - front, depth), F32)
     for ghost, base in ((left, 0), (right, total - chunk)):
-        kappa[pl.ds(base, chunk), :] = ghost[steps]
-    copies[-1].wait()
+        kappa[pl.ds(base, chunk), :] = ghost[steps * chunk :, :]
+    copies[5].wait()
     fill_weights(weights, turned[:depth, :], None)
     for base in (0, total - chunk):
         at = pl.ds(base, chunk)
@@ -368,12 +384,13 @@
 
         return kept
 
-    first(keep(lambda n: left[n], 0), 0)
-    first(keep(lambda n: right[n], total - chunk), total - chunk)
-    for copy in copies[:-1]:
+    first(keep(lambda n: left[n * chunk : (n + 1) * chunk, :], 0), 0)
+    first(keep(lambda n: right[n * chunk : (n + 1) * chunk, :], total - chunk), total - chunk)
+    for copy in copies[:5]:
         copy.wait()
-    first(keep(lambda n: ends[0, n], chunk), chunk)
-    first(keep(lambda n: ends[1, n], total - 2 * chunk), total - 2 * chunk)
+    first(keep(lambda n: ends[0, n * chunk : (n + 1) * chunk, :], chunk), chunk)
+    first(keep(lambda n: ends[1, n * chunk : (n + 1) * chunk, :], total - 2 * chunk), total - 2 * chunk)
+    copies[6].wait()
 
     def first_middle(step, carry):
         at = pl.multiple_of(step * chunk, 8)
@@ -382,7 +399,7 @@
         def value(n):
             made = middle[n, pl.ds(at, chunk), :]
             if n and n % 2 == 0:
-                made = made + modal[n // 2 - 1, pl.ds(at, chunk), :]
+                made = made + modal[pl.ds((n // 2 - 1) * inner + at, chunk), :]
             return made
 
         first(keep(value, base), base)
@@ -520,15 +537,15 @@
                 pltpu.VMEM(u_init.shape, F32),
                 pltpu.VMEM(u_init.shape, F32),
                 pltpu.VMEM((steps, count * tall, depth), F32),
-                pltpu.VMEM((2, size + 8, depth), F32),
+                pltpu.VMEM((4, size + 8, depth), F32),
                 pltpu.VMEM((depth, size), F32),
                 pltpu.VMEM((size, depth), F32),
                 square,
                 pltpu.VMEM((2, size, depth), F32),
                 *constants,
-                pltpu.SemaphoreType.DMA((3, columns)),
-                pltpu.SemaphoreType.DMA((count // 2,)),
-                pltpu.SemaphoreType.DMA((5,)),
+                pltpu.SemaphoreType.DMA((3, max(count // 4, 2) if count % 4 == 0 else count // 2)),
+                pltpu.SemaphoreType.DMA((max(count // 4, 2) if count % 4 == 0 else count // 2,)),
+                pltpu.SemaphoreType.DMA((3 if inner else 5,)),
             ],
             flops,
             mine, other, u_init, force[0], low, high, kappa, rates_row, basis,
@@ -558,29 +575,29 @@
 
     edge_low, edge_high = call(
         functools.partial(rim_kernel, block, chips - 1, [(0, REACH), (columns - REACH, columns)]),
-        [((steps + 1, chunk, depth), "v")] * 2,
+        [(((steps + 1) * chunk, depth), "v")] * 2,
         "h" * (5 + chips),
-        [pltpu.VMEM((chips, 2 * chunk, depth), F32)] + modes_scratch(2 * REACH),
+        [pltpu.VMEM((chips * 2 * chunk, depth), F32)] + modes_scratch(2 * REACH),
         10**9,
         edge, mine, other, kappa_cells, rates_row, basis, *pieces,
     )
     left = shifted(edge_high, "tx", 1)
     right = shifted(edge_low, "tx", -1)
     far = [
-        pltpu.VMEM((chips, inside * tall, depth), F32),
+        pltpu.VMEM((chips * inside * tall, depth), F32),
         pltpu.VMEM((columns * tall, depth), F32),
         pltpu.VMEM((columns * tall, depth), F32),
-        pltpu.VMEM((2, steps + 1, chunk, depth), F32),
+        pltpu.VMEM((2, (steps + 1) * chunk, depth), F32),
         pltpu.VMEM((depth + 8, depth), F32),
     ]
-    rows = (chips - 1) * inside * tall + 3 * columns * tall + 2 * steps * chunk + depth + 8
+    rows = chips * inside * tall + 3 * columns * tall + 2 * (steps + 1) * chunk + depth + 8
     room = 16 * (middle.size + 2 * left.size + u_init.size)
     rows = max(rows, -(-(room + MIB) // (4096 * depth)) * 1024)
     bundle = call(
         functools.partial(fill_kernel, block, chips - 1, [(REACH, columns - REACH)]),
         [((rows, depth), "h")],
         "h" * (6 + chips),
-        far + [pltpu.SemaphoreType.DMA((2 * steps + chips + 8,))] + modes_scratch(inside),
+        far + [pltpu.SemaphoreType.DMA((9,))] + modes_scratch(inside),
         10**9,
         mine, other, edge_low, edge_high, kappa_cells, rates_row, basis, *pieces,
     )[0]
@@ -601,7 +618,7 @@
             wide,
             wide,
             *far[3:],
-            pltpu.SemaphoreType.DMA((2 * steps + chips + 3,)),
+            pltpu.SemaphoreType.DMA((7,)),
         ],
         10**9,
         middle, left, right, bundle,

time: 129 us -> 127 us (0.984)
  Pallas kernels: 26.8 us -> 21.7 us
  waiting for transfers between devices: 37.3 us -> 40.6 us
    pallas_call x5, Pallas kernels: 26.8 us -> 21.7 us  [call(): pl.pallas_call(kernel, out_shape=shapes, in_specs=[pl.BlockSpec(memory_sp...]
    all_to_all x2, waiting for transfers between devices: 1.79 us -> 4.93 us  [exchanged(): return lax.all_to_all(array, 'tm', split_axis=0, concat_axis=0, tiled=True)]
  transfers between devices with their start and end apart: 10 -> 10, of which waited for: 8 -> 8; matrix products, arithmetic and copies ran while one was open for 4% -> 4% of each run, Pallas kernels for 13% -> 10%
where the time goes in v3:
time: 127 us
  waiting for transfers between devices  40.6 us (32%)
  blocking collectives  29.2 us (23%)
  starting transfers between devices  27.4 us (22%)
  Pallas kernels  21.7 us (17%)
  local copies, waits for them, and re-layouts  4.94 us (4%)
  other arithmetic  2.64 us (2%)
    all_to_all x1, blocking collectives, exchanged(): return lax.all_to_all(array, 'tm', split_axis=0, concat_axis=0, tiled=True)  29.2 us
    ppermute x3, waiting for transfers between devices, spread(): lax.ppermute(rows, 'tm', [(i, (i + 2 * by) % count) for i in range(count...  24.2 us
    pallas_call x5, Pallas kernels, call(): pl.pallas_call(kernel, out_shape=shapes, in_specs=[pl.BlockSpec(memory_sp...  21.7 us
    ppermute x4, waiting for transfers between devices, shifted(): return lax.ppermute(array, axis, pairs)  11.4 us
    ppermute x4, starting transfers between devices, shifted(): return lax.ppermute(array, axis, pairs)  10.6 us
    ppermute x3, starting transfers between devices, spread(): lax.ppermute(rows, 'tm', [(i, (i + 2 * by) % count) for i in range(count...  9.07 us
    all_to_all x2, starting transfers between devices, exchanged(): return lax.all_to_all(array, 'tm', split_axis=0, concat_axis=0, tiled=True)  7.27 us
    all_to_all x2, waiting for transfers between devices, exchanged(): return lax.all_to_all(array, 'tm', split_axis=0, concat_axis=0, tiled=True)  4.93 us
  transfers between devices with their start and end apart: 10, of which 8 were waited for; matrix products, arithmetic and copies ran while one was open for 4% of the time, Pallas kernels for 10%

profile of v3, /device:TPU:0, one launch (start us, length us, event | category | flops | bytes accessed | tf_op | source)
XLA Modules:
  0.0 126.7 jit_solution(2630109782099732577)
XLA Ops:
  0.0 0.5 collective-permute-start
  0.5 1.0 slice_bitcast_fusion
  1.5 4.5 %collective-permute-start.1 = (f32[256,128]{1,0:T(8,128)S(1)}, f32[256,128]{1,0:T(8,128)S(1)}, u32[]{:S(2)}, u32[]{:S(2)}) collective-permute-start(f32[256,128]{1,0:T(8,128)S(1)} %get-tuple-element.13), channel_id=1, source_target_pairs={{0,1},{1,2},{2,3},{4,5},{5,6},{6,7},{8,9},{9,10},{10,11},{12,13},{... | collective-permute-start | bytes 393224 | tf_op jit(solution)/shard_map/ppermute | solution.py:31
  6.0 1.3 %collective-permute-start.2 = (f32[256,128]{1,0:T(8,128)S(1)}, f32[256,128]{1,0:T(8,128)S(1)}, u32[]{:S(2)}, u32[]{:S(2)}) collective-permute-start(f32[256,128]{1,0:T(8,128)S(1)} %get-tuple-element.12), channel_id=1, source_target_pairs={{1,0},{2,1},{3,2},{5,4},{6,5},{7,6},{9,8},{10,9},{11,10},{13,12},{... | collective-permute-start | bytes 393224 | tf_op jit(solution)/shard_map/ppermute | solution.py:31
  7.3 2.1 %collective-permute-done.1.low = f32[256,128]{1,0:T(8,128)S(1)} collective-permute-done((f32[256,128]{1,0:T(8,128)S(1)}, f32[256,128]{1,0:T(8,128)S(1)}, u32[]{:S(2)}, u32[]{:S(2)}) %collective-permute-start.1) | collective-permute-done | bytes 131104 | tf_op jit(solution)/shard_map/ppermute | solution.py:31
  9.4 0.0 copy-start.5
  9.4 4.1 %collective-permute-done.2.high = f32[256,128]{1,0:T(8,128)S(1)} collective-permute-done((f32[256,128]{1,0:T(8,128)S(1)}, f32[256,128]{1,0:T(8,128)S(1)}, u32[]{:S(2)}, u32[]{:S(2)}) %collective-permute-start.2) | collective-permute-done | bytes 131104 | tf_op jit(solution)/shard_map/ppermute | solution.py:31
  13.5 0.0 copy-start.6
  13.5 0.0 collective-permute-done.other
  13.5 0.0 copy-start
  13.5 0.0 copy-done.5
  13.5 0.6 copy-done.6
  14.1 0.7 copy-done
  14.8 3.1 %shard_map.65 = f32[8,144,128]{2,1,0:T(8,128)} custom-call(f32[16,256,128]{2,1,0:T(8,128)} %bitcast.18, f32[16,256,128]{2,1,0:T(8,128)} %copy-done, f32[16,256,128]{2,1,0:T(8,128)} %initial.3, f32[16,256,128]{2,1,0:T(8,128)} %bitcast.23, f32[256,128]{1,0:T(8,128)} %copy-done.5, f32[256,128]{1,0:T(8,128)} %copy-done.6, f32[16,256]{1,0:T(8,128)} %kappa.3, ...), custom_call_target="tpu_custom_call" | custom-call | flops 2000000000 | bytes 1000000 | tf_op jit(solution)/shard_map/pallas_call | solution.py:467
  17.9 3.7 %all-to-all-start.1 = ((f32[8,144,128]{2,1,0:T(8,128)}), f32[8,144,128]{2,1,0:T(8,128)S(1)}, u32[]{:S(2)}, u32[]{:S(2)}) async-start(f32[8,144,128]{2,1,0:T(8,128)} %shard_map.65), calls=%async_computation.1 | async-start | bytes 1179648 | tf_op jit(solution)/shard_map/all_to_all | solution.py:484
  21.6 5.5 %shard_map.64 = f32[8,432,128]{2,1,0:T(8,128)} custom-call(f32[16,256,128]{2,1,0:T(8,128)} %bitcast.19, f32[16,256,128]{2,1,0:T(8,128)} %copy-done, f32[16,256,128]{2,1,0:T(8,128)} %initial.3, f32[16,256,128]{2,1,0:T(8,128)} %bitcast.24, f32[256,128]{1,0:T(8,128)} %copy-done.5, f32[256,128]{1,0:T(8,128)} %copy-done.6, f32[16,256]{1,0:T(8,128)} %kappa.3, ...), custom_call_target="tpu_custom_call" | custom-call | flops 6000000000 | bytes 1000000 | tf_op jit(solution)/shard_map/pallas_call | solution.py:467
  27.1 4.9 %all-to-all-done.1.edge = f32[8,144,128]{2,1,0:T(8,128)S(1)} async-done(((f32[8,144,128]{2,1,0:T(8,128)}), f32[8,144,128]{2,1,0:T(8,128)S(1)}, u32[]{:S(2)}, u32[]{:S(2)}) %all-to-all-start.1) | async-done | bytes 589856 | tf_op jit(solution)/shard_map/all_to_all | solution.py:484
  32.0 0.0 copy-start.1
  32.0 3.6 %all-to-all-start = ((f32[8,432,128]{2,1,0:T(8,128)}), f32[8,432,128]{2,1,0:T(8,128)S(1)}, u32[]{:S(2)}, u32[]{:S(2)}) async-start(f32[8,432,128]{2,1,0:T(8,128)} %shard_map.64), calls=%async_computation | async-start | bytes 3538944 | tf_op jit(solution)/shard_map/all_to_all | solution.py:484
  35.6 0.0 copy-start.7
  35.7 2.6 %bitcast_select_fusion = (f32[16,40,128]{2,1,0:T(8,128)}, f32[16,40,128]{2,1,0:T(8,128)}, f32[16,40,128]{2,1,0:T(8,128)}) fusion(f32[16,256,128]{2,1,0:T(8,128)} %copy-done, s32[]{:T(128)S(6)} %min.12, f32[1,16,256,128]{3,2,1,0:T(8,128)} %param.6, pred[]{:T(512)S(6)} %eq.12, s32[]{:T(128)S(6)} %min.11, s32[]{:T(128)S(6)} %min.10), kind=kLoop, calls=%fused_computation | loop fusion | flops 245760 | bytes 2949133 | tf_op jit(solution)/shard_map/jit(_where)/select_n | solution.py:498
  38.3 0.0 copy-done.1
  38.3 3.8 %collective-permute-start.3 = (f32[16,40,128]{2,1,0:T(8,128)}, f32[16,40,128]{2,1,0:T(8,128)S(1)}, u32[]{:S(2)}, u32[]{:S(2)}) collective-permute-start(f32[16,40,128]{2,1,0:T(8,128)} %get-tuple-element.11), channel_id=1, source_target_pairs={{0,8},{4,12},{8,16},{12,20},{16,24},{20,28},{1,9},{5,13},{9,17},{1... | collective-permute-start | bytes 983048 | tf_op jit(solution)/shard_map/ppermute | solution.py:503
  42.2 3.3 %collective-permute-start.4 = (f32[16,40,128]{2,1,0:T(8,128)}, f32[16,40,128]{2,1,0:T(8,128)S(1)}, u32[]{:S(2)}, u32[]{:S(2)}) collective-permute-start(f32[16,40,128]{2,1,0:T(8,128)} %get-tuple-element.10), channel_id=1, source_target_pairs={{0,16},{4,20},{8,24},{12,28},{16,0},{20,4},{1,17},{5,21},{9,25},{1... | collective-permute-start | bytes 983048 | tf_op jit(solution)/shard_map/ppermute | solution.py:503
  45.5 1.9 %collective-permute-start.5 = (f32[16,40,128]{2,1,0:T(8,128)}, f32[16,40,128]{2,1,0:T(8,128)S(1)}, u32[]{:S(2)}, u32[]{:S(2)}) collective-permute-start(f32[16,40,128]{2,1,0:T(8,128)} %get-tuple-element.9), channel_id=1, source_target_pairs={{0,24},{4,28},{8,0},{12,4},{16,8},{20,12},{1,25},{5,29},{9,1},{13,... | collective-permute-start | bytes 983048 | tf_op jit(solution)/shard_map/ppermute | solution.py:503
  47.4 0.0 copy-done.7
  47.4 0.1 pad_dynamic-slice_fusion
  47.5 0.1 broadcast_in_dim.8
  47.6 15.4 %collective-permute-done.3.rest_0_ = f32[16,40,128]{2,1,0:T(8,128)S(1)} collective-permute-done((f32[16,40,128]{2,1,0:T(8,128)}, f32[16,40,128]{2,1,0:T(8,128)S(1)}, u32[]{:S(2)}, u32[]{:S(2)}) %collective-permute-start.3) | collective-permute-done | bytes 327712 | tf_op jit(solution)/shard_map/ppermute | solution.py:503
  63.0 0.0 copy-start.2
  63.0 6.7 %collective-permute-done.4.rest_1_ = f32[16,40,128]{2,1,0:T(8,128)S(1)} collective-permute-done((f32[16,40,128]{2,1,0:T(8,128)}, f32[16,40,128]{2,1,0:T(8,128)S(1)}, u32[]{:S(2)}, u32[]{:S(2)}) %collective-permute-start.4) | collective-permute-done | bytes 327712 | tf_op jit(solution)/shard_map/ppermute | solution.py:503
  69.7 0.0 copy-start.3
  69.7 2.1 %collective-permute-done.5.rest_2_ = f32[16,40,128]{2,1,0:T(8,128)S(1)} collective-permute-done((f32[16,40,128]{2,1,0:T(8,128)}, f32[16,40,128]{2,1,0:T(8,128)S(1)}, u32[]{:S(2)}, u32[]{:S(2)}) %collective-permute-start.5) | collective-permute-done | bytes 327712 | tf_op jit(solution)/shard_map/ppermute | solution.py:503
  71.8 0.0 copy-start.4
  71.8 0.9 broadcast_in_dim.9.kappa
  72.7 0.0 copy-done.2
  72.7 0.0 copy-done.3
  72.7 0.0 copy-done.4
  72.7 3.2 %shard_map.66 = (f32[648,128]{1,0:T(8,128)}, f32[648,128]{1,0:T(8,128)}) custom-call(f32[8,144,128]{2,1,0:T(8,128)} %copy-done.1, f32[16,256,128]{2,1,0:T(8,128)} %bitcast.20, f32[16,256,128]{2,1,0:T(8,128)} %copy-done, f32[576,128]{1,0:T(8,128)} %broadcast_in_dim.9.kappa, f32[1,128]{1,0:T(1,128)} %bitcast.27, f32[128,128]{1,0:T(8,128)} %basis.7, ...), custom_call_target="tpu_custom_call" | custom-call | flops 1000000000 | bytes 1000000 | tf_op jit(solution)/shard_map/pallas_call | solution.py:467
  75.9 3.5 %collective-permute-start.6 = (f32[648,128]{1,0:T(8,128)}, f32[648,128]{1,0:T(8,128)S(1)}, u32[]{:S(2)}, u32[]{:S(2)}) collective-permute-start(f32[648,128]{1,0:T(8,128)} %get-tuple-element.7.edge_high), channel_id=1, source_target_pairs={{0,1},{1,2},{2,3},{4,5},{5,6},{6,7},{8,9},{9,10},{10,11},{12,13},{... | collective-permute-start | bytes 995336 | tf_op jit(solution)/shard_map/ppermute | solution.py:31
  79.4 1.3 %collective-permute-start.7 = (f32[648,128]{1,0:T(8,128)}, f32[648,128]{1,0:T(8,128)S(1)}, u32[]{:S(2)}, u32[]{:S(2)}) collective-permute-start(f32[648,128]{1,0:T(8,128)} %get-tuple-element.8.edge_low), channel_id=1, source_target_pairs={{1,0},{2,1},{3,2},{5,4},{6,5},{7,6},{9,8},{10,9},{11,10},{13,12},{... | collective-permute-start | bytes 995336 | tf_op jit(solution)/shard_map/ppermute | solution.py:31
  80.7 4.6 %shard_map.67.bundle = f32[37888,128]{1,0:T(8,128)} custom-call(f32[16,256,128]{2,1,0:T(8,128)} %bitcast.21, f32[16,256,128]{2,1,0:T(8,128)} %copy-done, f32[648,128]{1,0:T(8,128)} %get-tuple-element.8.edge_low, f32[648,128]{1,0:T(8,128)} %get-tuple-element.7.edge_high, f32[576,128]{1,0:T(8,128)} %broadcast_in_dim.9.kappa, f32[1,128]{1,0:T(1,128)} %bitcast.28, ...), custom_call_target="tpu_custom_call" | custom-call | flops 1000000000 | bytes 1000000 | tf_op jit(solution)/shard_map/pallas_call | solution.py:467
  85.3 1.2 collective-permute-done.6.left
  86.4 4.0 %collective-permute-done.7.right = f32[648,128]{1,0:T(8,128)S(1)} collective-permute-done((f32[648,128]{1,0:T(8,128)}, f32[648,128]{1,0:T(8,128)S(1)}, u32[]{:S(2)}, u32[]{:S(2)}) %collective-permute-start.7) | collective-permute-done | bytes 331808 | tf_op jit(solution)/shard_map/ppermute | solution.py:31
  90.5 0.0 all-to-all-done.middle
  90.5 5.4 %shard_map.68 = f32[8,512,128]{2,1,0:T(8,128)S(1)} custom-call(f32[8,432,128]{2,1,0:T(8,128)S(1)} %all-to-all-done.middle, f32[648,128]{1,0:T(8,128)S(1)} %collective-permute-done.6.left, f32[648,128]{1,0:T(8,128)S(1)} %collective-permute-done.7.right, f32[37888,128]{1,0:T(8,128)} %shard_map.67.bundle), custom_call_target="tpu_custom_call" | custom-call | flops 1000000000 | bytes 1000000 | tf_op jit(solution)/shard_map/pallas_call | solution.py:467
  95.9 29.2 %all_to_all.15 = f32[8,512,128]{2,1,0:T(8,128)S(1)} all-to-all(f32[8,512,128]{2,1,0:T(8,128)S(1)} %shard_map.68), channel_id=1, replica_groups=mesh['tm'=8,'tx'=4] {'tm'}, dimensions={0} | all-to-all | bytes 4194304 | tf_op jit(solution)/shard_map/all_to_all | solution.py:484
  125.1 1.6 %copy.7 = f32[16,8,32,128]{3,2,1,0:T(8,128)} copy(f32[16,8,32,128]{3,2,0,1:T(8,128)S(1)} %bitcast.22) | data formatting | bytes 4194304 | tf_op jit(solution)/shard_map/transpose | solution.py:628
Async XLA Ops:
  0.0 13.5 %collective-permute-start = (f32[16,256,128]{2,1,0:T(8,128)}, f32[16,256,128]{2,1,0:T(8,128)S(1)}, u32[]{:S(2)}, u32[]{:S(2)}) collective-permute-start(f32[16,256,128]{2,1,0:T(8,128)} %bitcast.17), channel_id=1, source_target_pairs={{0,4},{4,0},{8,12},{12,8},{16,20},{20,16},{24,28},{28,24},{1,5},{5... | collective-permute-start | bytes 6291464 | tf_op jit(solution)/shard_map/ppermute | solution.py:480
  1.5 7.9 %collective-permute-start.1 = (f32[256,128]{1,0:T(8,128)S(1)}, f32[256,128]{1,0:T(8,128)S(1)}, u32[]{:S(2)}, u32[]{:S(2)}) collective-permute-start(f32[256,128]{1,0:T(8,128)S(1)} %get-tuple-element.13), channel_id=1, source_target_pairs={{0,1},{1,2},{2,3},{4,5},{5,6},{6,7},{8,9},{9,10},{10,11},{12,13},{... | collective-permute-start | bytes 393224 | tf_op jit(solution)/shard_map/ppermute | solution.py:31
  6.0 7.5 %collective-permute-start.2 = (f32[256,128]{1,0:T(8,128)S(1)}, f32[256,128]{1,0:T(8,128)S(1)}, u32[]{:S(2)}, u32[]{:S(2)}) collective-permute-start(f32[256,128]{1,0:T(8,128)S(1)} %get-tuple-element.12), channel_id=1, source_target_pairs={{1,0},{2,1},{3,2},{5,4},{6,5},{7,6},{9,8},{10,9},{11,10},{13,12},{... | collective-permute-start | bytes 393224 | tf_op jit(solution)/shard_map/ppermute | solution.py:31
  9.4 4.1 %copy-start.5 = (f32[256,128]{1,0:T(8,128)}, f32[256,128]{1,0:T(8,128)S(1)}, u32[]{:S(2)}) copy-start(f32[256,128]{1,0:T(8,128)S(1)} %collective-permute-done.1.low) | copy-start | bytes 393220
  13.5 0.7 copy-start.6
  13.5 1.4 %copy-start = (f32[16,256,128]{2,1,0:T(8,128)}, f32[16,256,128]{2,1,0:T(8,128)S(1)}, u32[]{:S(2)}) copy-start(f32[16,256,128]{2,1,0:T(8,128)S(1)} %collective-permute-done.other) | copy-start | bytes 6291460
  17.9 14.1 %all-to-all-start.1 = ((f32[8,144,128]{2,1,0:T(8,128)}), f32[8,144,128]{2,1,0:T(8,128)S(1)}, u32[]{:S(2)}, u32[]{:S(2)}) async-start(f32[8,144,128]{2,1,0:T(8,128)} %shard_map.65), calls=%async_computation.1 | async-start | bytes 1179648 | tf_op jit(solution)/shard_map/all_to_all | solution.py:484
  32.0 6.3 %copy-start.1 = (f32[8,144,128]{2,1,0:T(8,128)}, f32[8,144,128]{2,1,0:T(8,128)S(1)}, u32[]{:S(2)}) copy-start(f32[8,144,128]{2,1,0:T(8,128)S(1)} %all-to-all-done.1.edge) | copy-start | bytes 1769476
  32.0 58.4 %all-to-all-start = ((f32[8,432,128]{2,1,0:T(8,128)}), f32[8,432,128]{2,1,0:T(8,128)S(1)}, u32[]{:S(2)}, u32[]{:S(2)}) async-start(f32[8,432,128]{2,1,0:T(8,128)} %shard_map.64), calls=%async_computation | async-start | bytes 3538944 | tf_op jit(solution)/shard_map/all_to_all | solution.py:484
  35.6 11.8 %copy-start.7 = (f32[16,256]{1,0:T(8,128)S(1)}, f32[16,256]{1,0:T(8,128)}, u32[]{:S(2)}) copy-start(f32[16,256]{1,0:T(8,128)} %kappa.3) | copy-start | bytes 49156
  38.3 24.7 %collective-permute-start.3 = (f32[16,40,128]{2,1,0:T(8,128)}, f32[16,40,128]{2,1,0:T(8,128)S(1)}, u32[]{:S(2)}, u32[]{:S(2)}) collective-permute-start(f32[16,40,128]{2,1,0:T(8,128)} %get-tuple-element.11), channel_id=1, source_target_pairs={{0,8},{4,12},{8,16},{12,20},{16,24},{20,28},{1,9},{5,13},{9,17},{1... | collective-permute-start | bytes 983048 | tf_op jit(solution)/shard_map/ppermute | solution.py:503
  42.2 27.6 %collective-permute-start.4 = (f32[16,40,128]{2,1,0:T(8,128)}, f32[16,40,128]{2,1,0:T(8,128)S(1)}, u32[]{:S(2)}, u32[]{:S(2)}) collective-permute-start(f32[16,40,128]{2,1,0:T(8,128)} %get-tuple-element.10), channel_id=1, source_target_pairs={{0,16},{4,20},{8,24},{12,28},{16,0},{20,4},{1,17},{5,21},{9,25},{1... | collective-permute-start | bytes 983048 | tf_op jit(solution)/shard_map/ppermute | solution.py:503
  45.5 26.3 %collective-permute-start.5 = (f32[16,40,128]{2,1,0:T(8,128)}, f32[16,40,128]{2,1,0:T(8,128)S(1)}, u32[]{:S(2)}, u32[]{:S(2)}) collective-permute-start(f32[16,40,128]{2,1,0:T(8,128)} %get-tuple-element.9), channel_id=1, source_target_pairs={{0,24},{4,28},{8,0},{12,4},{16,8},{20,12},{1,25},{5,29},{9,1},{13,... | collective-permute-start | bytes 983048 | tf_op jit(solution)/shard_map/ppermute | solution.py:503
  63.0 9.7 %copy-start.2 = (f32[16,40,128]{2,1,0:T(8,128)}, f32[16,40,128]{2,1,0:T(8,128)S(1)}, u32[]{:S(2)}) copy-start(f32[16,40,128]{2,1,0:T(8,128)S(1)} %collective-permute-done.3.rest_0_) | copy-start | bytes 983044
  69.7 3.0 %copy-start.3 = (f32[16,40,128]{2,1,0:T(8,128)}, f32[16,40,128]{2,1,0:T(8,128)S(1)}, u32[]{:S(2)}) copy-start(f32[16,40,128]{2,1,0:T(8,128)S(1)} %collective-permute-done.4.rest_1_) | copy-start | bytes 983044
  71.8 0.9 copy-start.4
  75.9 10.5 %collective-permute-start.6 = (f32[648,128]{1,0:T(8,128)}, f32[648,128]{1,0:T(8,128)S(1)}, u32[]{:S(2)}, u32[]{:S(2)}) collective-permute-start(f32[648,128]{1,0:T(8,128)} %get-tuple-element.7.edge_high), channel_id=1, source_target_pairs={{0,1},{1,2},{2,3},{4,5},{5,6},{6,7},{8,9},{9,10},{10,11},{12,13},{... | collective-permute-start | bytes 995336 | tf_op jit(solution)/shard_map/ppermute | solution.py:31
  79.4 11.1 %collective-permute-start.7 = (f32[648,128]{1,0:T(8,128)}, f32[648,128]{1,0:T(8,128)S(1)}, u32[]{:S(2)}, u32[]{:S(2)}) collective-permute-start(f32[648,128]{1,0:T(8,128)} %get-tuple-element.8.edge_low), channel_id=1, source_target_pairs={{1,0},{2,1},{3,2},{5,4},{6,5},{7,6},{9,8},{10,9},{11,10},{13,12},{... | collective-permute-start | bytes 995336 | tf_op jit(solution)/shard_map/ppermute | solution.py:31

commit v4 on v3

--- a/solution.py
+++ b/solution.py
@@ -58,6 +58,43 @@
     depth = value.shape[1]
     wide = dot(jnp.concatenate(split(value), axis=1), weights[...])
     return wide[:, :depth] + wide[:, depth:]
+
+
+def pack_kernel(block, count, mine, other, *rest):
+    outs, windows, loads = rest[:count], rest[count], rest[count + 1]
+    columns, size, _ = mine.shape
+    broad = windows.shape[2]
+    tall = block + 2 * REACH
+    here = lax.axis_index("tm")
+    odd = here % 2 == 1
+    targets = [(here + 2 * by) % (size // block) for by in range(1, count + 1)]
+    begins = [pl.multiple_of(near_begin(target, block, broad, size), 8) for target in targets]
+
+    def load(source, by):
+        return pltpu.make_async_copy(source.at[:, pl.ds(begins[by], broad), :], windows.at[by], loads.at[by])
+
+    @pl.when(odd)
+    def _():
+        for by in range(count):
+            load(mine, by).start()
+
+    @pl.when(jnp.logical_not(odd))
+    def _():
+        for by in range(count):
+            load(other, by).start()
+
+    for by in range(count):
+        load(mine, by).wait()
+
+    def pair(step, carry):
+        base = pl.multiple_of(step * 2 * tall, 8)
+        for by in range(count):
+            take = pl.ds(window_start(targets[by], block, tall, size) - begins[by], tall)
+            for which in range(2):
+                outs[by][pl.ds(base + which * tall, tall), :] = windows[by, 2 * step + which, take, :]
+        return carry
+
+    lax.fori_loop(0, columns // 2, pair, 0)
 
 
 def residual_kernel(
@@ -196,7 +233,6 @@
     pieces = rest[:count]
     first_out, second_out, third_out, near, far, strip, gathered, weights, plain_ref, rates_ref, edges, cells, loads, stores = rest[count:]
     broad, _ = near.shape[1:]
-    window = far.shape[2]
     chips = count + 1
     steps = 2 * chips
     size = block * steps
@@ -215,7 +251,8 @@
             take = pl.ds(start, stop - start)
             put = pl.ds(at, stop - start)
             made.append((source.at[take, pl.ds(near_start, broad), :], near.at[put]))
-            made += [(pieces[by].at[take], far.at[by, put]) for by in range(count)]
+            flat, into = pl.ds(start * tall, (stop - start) * tall), pl.ds(at * tall, (stop - start) * tall)
+            made += [(pieces[by].at[flat, :], far.at[by, into, :]) for by in range(count)]
             at += stop - start
         return [pltpu.make_async_copy(*ends, loads.at[i]) for i, ends in enumerate(made)]
 
@@ -266,11 +303,11 @@
 
     keep(chip, gather(lambda x: near[x], near_start, broad))
 
-    far_start = window_start(here, block, window, size)
+    far_start = window_start(here, block, tall, size)
     strip[...] = jnp.zeros_like(strip)
 
     def far_slot(by, carry):
-        keep((chip - by - 1 + chips) % chips, gather(lambda x: far[by, x], far_start, window))
+        keep((chip - by - 1 + chips) % chips, gather(lambda x: far[by, pl.ds(x * tall, tall), :], far_start, tall))
         return carry
 
     lax.fori_loop(0, count, far_slot, 0)
@@ -433,27 +470,30 @@
 
     lax.fori_loop(0, (columns + 2) // 2, second, 0)
 
-    def third(base):
+    def third(base, which):
         inv = inverse[pl.ds(base, block), :]
+        rows = pl.ds(which * block, block)
 
         def value(n):
             made = term(newer, base, block, n)
-            source[n, :block, :] = made
+            source[n, rows, :] = made
             return made
 
         run = solve(value, inv, ending[pl.ds(base, block), :])
         for n in range(steps):
-            run = (source[n, :block, :] + run) * inv
-            gathered[pl.ds(n * block, block), :] = run
-        gathered[...] = times_matrix(gathered[...], weights)
+            run = (source[n, rows, :] + run) * inv
+            gathered[pl.ds((which * steps + n) * block, block), :] = run
 
     def third_pair(step, carry):
         at = pl.multiple_of(step * 2 * tall, 8)
         to = pl.multiple_of(step * 2 * block, 8)
         for which in range(2):
-            third(at + chunk + which * tall + REACH)
+            third(at + chunk + which * tall + REACH, which)
+        gathered[...] = times_matrix(gathered[...], weights)
+        for which in range(2):
             for n in range(steps):
-                out[n, pl.ds(to + which * block, block), :] = gathered[pl.ds(n * block, block), :]
+                part = gathered[pl.ds((which * steps + n) * block, block), :]
+                out[n, pl.ds(to + which * block, block), :] = part
         return carry
 
     lax.fori_loop(0, columns // 2, third_pair, 0)
@@ -489,17 +529,11 @@
 
 
 def window_start(device, block, window, size):
-    return jnp.clip(block * device - 4, 0, size - window)
-
-
-def spread(mine, other, here, block, window, by):
+    return jnp.clip(block * device - REACH, 0, size - window)
+
+
+def spread(rows, by):
     count = lax.axis_size("tm")
-    start = window_start((here + 2 * by) % count, block, window, mine.shape[1])
-    rows = jnp.where(
-        here % 2 == 1,
-        lax.dynamic_slice_in_dim(mine, start, window, 1),
-        lax.dynamic_slice_in_dim(other, start, window, 1),
-    )
     return lax.ppermute(rows, "tm", [(i, (i + 2 * by) % count) for i in range(count - 2)])
 
 
@@ -511,7 +545,6 @@
     block = size // steps
     tall = block + 2 * REACH
     chunk = REACH * tall
-    window = block + 8
     broad = (block + 23) // 8 * 8
     inside = columns - 2 * REACH
     total = columns * tall + 2 * chunk
@@ -523,9 +556,17 @@
     low = shifted(mine[-1], "tx", 1)
     high = shifted(mine[0], "tx", -1)
     rates_row = rates.reshape(1, depth)
+    packed = call(
+        functools.partial(pack_kernel, block, chips - 1),
+        [((columns * tall, depth), "v")] * (chips - 1),
+        "hh",
+        [pltpu.VMEM((chips - 1, columns, broad, depth), F32), pltpu.SemaphoreType.DMA((chips - 1,))],
+        10**7,
+        mine, other,
+    )
     pieces = []
     for by in range(1, chips):
-        pieces.append(spread(mine, other, here, block, window, by))
+        pieces.append(spread(packed[by - 1], by))
 
     def residual(inner, count, flops):
         return call(
@@ -562,7 +603,7 @@
     def modes_scratch(width):
         return [
             pltpu.VMEM((width, broad, depth), F32),
-            pltpu.VMEM((chips - 1, width, window, depth), F32),
+            pltpu.VMEM((chips - 1, width * tall, depth), F32),
             pltpu.VMEM((2, broad + 32, depth), F32),
             pltpu.VMEM((width * tall, depth), F32),
             square,
@@ -611,7 +652,7 @@
             pltpu.VMEM((steps, chunk, depth), F32),
             pltpu.VMEM((steps, total + 2 * front, depth), F32),
             pltpu.VMEM((steps, total + 2 * front, depth), F32),
-            pltpu.VMEM((steps * block, depth), F32),
+            pltpu.VMEM((2 * steps * block, depth), F32),
             square,
             far[0],
             wide,

time: 127 us -> 126 us (level)
  other arithmetic: 2.64 us -> 0 us
  Pallas kernels: 21.7 us -> 24 us
    select_n x1 -> x0, other arithmetic: 2.64 us -> none  [spread(): jnp.where(here % 2 == 1, lax.dynamic_slice_in_dim(mine, start, window, 1)...]
    pallas_call x5 -> x6, Pallas kernels: 21.7 us -> 24 us  [call(): pl.pallas_call(kernel, out_shape=shapes, in_specs=[pl.BlockSpec(memory_sp...]
  transfers between devices with their start and end apart: 10 -> 10, of which waited for: 8 -> 8; matrix products, arithmetic and copies ran while one was open for 4% -> 2% of each run, Pallas kernels for 10% -> 12%
where the time goes in v4:
time: 126 us; the launch traced here: 125 us
  waiting for transfers between devices  39.5 us (31%)
  blocking collectives  29.3 us (23%)
  starting transfers between devices  27.4 us (22%)
  Pallas kernels  24 us (19%)
  local copies, waits for them, and re-layouts  4.91 us (4%)
    all_to_all x1, blocking collectives, exchanged(): return lax.all_to_all(array, 'tm', split_axis=0, concat_axis=0, tiled=True)  29.3 us
    pallas_call x6, Pallas kernels, call(): pl.pallas_call(kernel, out_shape=shapes, in_specs=[pl.BlockSpec(memory_sp...  24 us
    ppermute x3, waiting for transfers between devices, spread(): lax.ppermute(rows, 'tm', [(i, (i + 2 * by) % count) for i in range(count...  23.1 us
    ppermute x4, waiting for transfers between devices, shifted(): return lax.ppermute(array, axis, pairs)  11.4 us
    ppermute x4, starting transfers between devices, shifted(): return lax.ppermute(array, axis, pairs)  10.6 us
    ppermute x3, starting transfers between devices, spread(): lax.ppermute(rows, 'tm', [(i, (i + 2 * by) % count) for i in range(count...  9.11 us
    all_to_all x2, starting transfers between devices, exchanged(): return lax.all_to_all(array, 'tm', split_axis=0, concat_axis=0, tiled=True)  7.27 us
    all_to_all x2, waiting for transfers between devices, exchanged(): return lax.all_to_all(array, 'tm', split_axis=0, concat_axis=0, tiled=True)  4.93 us
  transfers between devices with their start and end apart: 10, of which 8 were waited for; matrix products, arithmetic and copies ran while one was open for 2% of the time, Pallas kernels for 12%

profile of v4, /device:TPU:0, one launch (start us, length us, event | category | flops | bytes accessed | tf_op | source)
XLA Modules:
  0.0 125.2 jit_solution(5009038928666799122)
XLA Ops:
  0.0 0.5 collective-permute-start
  0.5 1.0 slice_bitcast_fusion
  1.5 4.5 %collective-permute-start.1 = (f32[256,128]{1,0:T(8,128)S(1)}, f32[256,128]{1,0:T(8,128)S(1)}, u32[]{:S(2)}, u32[]{:S(2)}) collective-permute-start(f32[256,128]{1,0:T(8,128)S(1)} %get-tuple-element.16), channel_id=1, source_target_pairs={{0,1},{1,2},{2,3},{4,5},{5,6},{6,7},{8,9},{9,10},{10,11},{12,13},{... | collective-permute-start | bytes 393224 | tf_op jit(solution)/shard_map/ppermute | solution.py:31
  6.0 1.3 %collective-permute-start.2 = (f32[256,128]{1,0:T(8,128)S(1)}, f32[256,128]{1,0:T(8,128)S(1)}, u32[]{:S(2)}, u32[]{:S(2)}) collective-permute-start(f32[256,128]{1,0:T(8,128)S(1)} %get-tuple-element.15), channel_id=1, source_target_pairs={{1,0},{2,1},{3,2},{5,4},{6,5},{7,6},{9,8},{10,9},{11,10},{13,12},{... | collective-permute-start | bytes 393224 | tf_op jit(solution)/shard_map/ppermute | solution.py:31
  7.3 2.1 %collective-permute-done.1.low = f32[256,128]{1,0:T(8,128)S(1)} collective-permute-done((f32[256,128]{1,0:T(8,128)S(1)}, f32[256,128]{1,0:T(8,128)S(1)}, u32[]{:S(2)}, u32[]{:S(2)}) %collective-permute-start.1) | collective-permute-done | bytes 131104 | tf_op jit(solution)/shard_map/ppermute | solution.py:31
  9.4 0.0 copy-start.5
  9.4 4.1 %collective-permute-done.2.high = f32[256,128]{1,0:T(8,128)S(1)} collective-permute-done((f32[256,128]{1,0:T(8,128)S(1)}, f32[256,128]{1,0:T(8,128)S(1)}, u32[]{:S(2)}, u32[]{:S(2)}) %collective-permute-start.2) | collective-permute-done | bytes 131104 | tf_op jit(solution)/shard_map/ppermute | solution.py:31
  13.5 0.0 copy-start.6
  13.5 0.0 collective-permute-done.other
  13.5 0.0 copy-start
  13.5 0.0 copy-done.5
  13.5 0.6 copy-done.6
  14.1 0.7 copy-done
  14.8 3.1 %shard_map.65 = f32[8,144,128]{2,1,0:T(8,128)} custom-call(f32[16,256,128]{2,1,0:T(8,128)} %bitcast.12, f32[16,256,128]{2,1,0:T(8,128)} %copy-done, f32[16,256,128]{2,1,0:T(8,128)} %initial.3, f32[16,256,128]{2,1,0:T(8,128)} %bitcast.18, f32[256,128]{1,0:T(8,128)} %copy-done.5, f32[256,128]{1,0:T(8,128)} %copy-done.6, f32[16,256]{1,0:T(8,128)} %kappa.3, ...), custom_call_target="tpu_custom_call" | custom-call | flops 2000000000 | bytes 1000000 | tf_op jit(solution)/shard_map/pallas_call | solution.py:507
  17.9 3.7 %all-to-all-start.1 = ((f32[8,144,128]{2,1,0:T(8,128)}), f32[8,144,128]{2,1,0:T(8,128)S(1)}, u32[]{:S(2)}, u32[]{:S(2)}) async-start(f32[8,144,128]{2,1,0:T(8,128)} %shard_map.65), calls=%async_computation.1 | async-start | bytes 1179648 | tf_op jit(solution)/shard_map/all_to_all | solution.py:524
  21.6 5.5 %shard_map.64 = f32[8,432,128]{2,1,0:T(8,128)} custom-call(f32[16,256,128]{2,1,0:T(8,128)} %bitcast.13, f32[16,256,128]{2,1,0:T(8,128)} %copy-done, f32[16,256,128]{2,1,0:T(8,128)} %initial.3, f32[16,256,128]{2,1,0:T(8,128)} %bitcast.19, f32[256,128]{1,0:T(8,128)} %copy-done.5, f32[256,128]{1,0:T(8,128)} %copy-done.6, f32[16,256]{1,0:T(8,128)} %kappa.3, ...), custom_call_target="tpu_custom_call" | custom-call | flops 6000000000 | bytes 1000000 | tf_op jit(solution)/shard_map/pallas_call | solution.py:507
  27.1 4.9 %all-to-all-done.1.edge = f32[8,144,128]{2,1,0:T(8,128)S(1)} async-done(((f32[8,144,128]{2,1,0:T(8,128)}), f32[8,144,128]{2,1,0:T(8,128)S(1)}, u32[]{:S(2)}, u32[]{:S(2)}) %all-to-all-start.1) | async-done | bytes 589856 | tf_op jit(solution)/shard_map/all_to_all | solution.py:524
  32.0 0.0 copy-start.1
  32.0 3.6 %all-to-all-start = ((f32[8,432,128]{2,1,0:T(8,128)}), f32[8,432,128]{2,1,0:T(8,128)S(1)}, u32[]{:S(2)}, u32[]{:S(2)}) async-start(f32[8,432,128]{2,1,0:T(8,128)} %shard_map.64), calls=%async_computation | async-start | bytes 3538944 | tf_op jit(solution)/shard_map/all_to_all | solution.py:524
  35.6 0.0 copy-start.7
  35.6 2.3 %shard_map.66 = (f32[576,128]{1,0:T(8,128)}, f32[576,128]{1,0:T(8,128)}, f32[576,128]{1,0:T(8,128)}) custom-call(f32[16,256,128]{2,1,0:T(8,128)} %bitcast.14, f32[16,256,128]{2,1,0:T(8,128)} %copy-done), custom_call_target="tpu_custom_call" | custom-call | flops 10000000 | bytes 1000000 | tf_op jit(solution)/shard_map/pallas_call | solution.py:507
  38.0 0.0 copy-done.1
  38.0 3.8 %collective-permute-start.3 = (f32[576,128]{1,0:T(8,128)}, f32[576,128]{1,0:T(8,128)S(1)}, u32[]{:S(2)}, u32[]{:S(2)}) collective-permute-start(f32[576,128]{1,0:T(8,128)} %get-tuple-element.10), channel_id=1, source_target_pairs={{0,8},{4,12},{8,16},{12,20},{16,24},{20,28},{1,9},{5,13},{9,17},{1... | collective-permute-start | bytes 884744 | tf_op jit(solution)/shard_map/ppermute | solution.py:537
  41.8 3.4 %collective-permute-start.4 = (f32[576,128]{1,0:T(8,128)}, f32[576,128]{1,0:T(8,128)S(1)}, u32[]{:S(2)}, u32[]{:S(2)}) collective-permute-start(f32[576,128]{1,0:T(8,128)} %get-tuple-element.11), channel_id=1, source_target_pairs={{0,16},{4,20},{8,24},{12,28},{16,0},{20,4},{1,17},{5,21},{9,25},{1... | collective-permute-start | bytes 884744 | tf_op jit(solution)/shard_map/ppermute | solution.py:537
  45.2 1.9 %collective-permute-start.5 = (f32[576,128]{1,0:T(8,128)}, f32[576,128]{1,0:T(8,128)S(1)}, u32[]{:S(2)}, u32[]{:S(2)}) collective-permute-start(f32[576,128]{1,0:T(8,128)} %get-tuple-element.12), channel_id=1, source_target_pairs={{0,24},{4,28},{8,0},{12,4},{16,8},{20,12},{1,25},{5,29},{9,1},{13,... | collective-permute-start | bytes 884744 | tf_op jit(solution)/shard_map/ppermute | solution.py:537
  47.1 0.0 copy-done.7
  47.1 0.1 pad_dynamic-slice_fusion
  47.2 0.1 broadcast_in_dim.8
  47.3 15.1 %collective-permute-done.3.rest_0_ = f32[576,128]{1,0:T(8,128)S(1)} collective-permute-done((f32[576,128]{1,0:T(8,128)}, f32[576,128]{1,0:T(8,128)S(1)}, u32[]{:S(2)}, u32[]{:S(2)}) %collective-permute-start.3) | collective-permute-done | bytes 294944 | tf_op jit(solution)/shard_map/ppermute | solution.py:537
  62.3 0.0 copy-start.2
  62.3 6.0 %collective-permute-done.4.rest_1_ = f32[576,128]{1,0:T(8,128)S(1)} collective-permute-done((f32[576,128]{1,0:T(8,128)}, f32[576,128]{1,0:T(8,128)S(1)}, u32[]{:S(2)}, u32[]{:S(2)}) %collective-permute-start.4) | collective-permute-done | bytes 294944 | tf_op jit(solution)/shard_map/ppermute | solution.py:537
  68.3 0.0 copy-start.3
  68.3 2.1 %collective-permute-done.5.rest_2_ = f32[576,128]{1,0:T(8,128)S(1)} collective-permute-done((f32[576,128]{1,0:T(8,128)}, f32[576,128]{1,0:T(8,128)S(1)}, u32[]{:S(2)}, u32[]{:S(2)}) %collective-permute-start.5) | collective-permute-done | bytes 294944 | tf_op jit(solution)/shard_map/ppermute | solution.py:537
  70.4 0.0 copy-start.4
  70.4 0.9 broadcast_in_dim.9.kappa
  71.3 0.0 copy-done.2
  71.3 0.0 copy-done.3
  71.3 0.0 copy-done.4
  71.3 3.2 %shard_map.67 = (f32[648,128]{1,0:T(8,128)}, f32[648,128]{1,0:T(8,128)}) custom-call(f32[8,144,128]{2,1,0:T(8,128)} %copy-done.1, f32[16,256,128]{2,1,0:T(8,128)} %bitcast.15, f32[16,256,128]{2,1,0:T(8,128)} %copy-done, f32[576,128]{1,0:T(8,128)} %broadcast_in_dim.9.kappa, f32[1,128]{1,0:T(1,128)} %bitcast.22, f32[128,128]{1,0:T(8,128)} %basis.7, ...), custom_call_target="tpu_custom_call" | custom-call | flops 1000000000 | bytes 1000000 | tf_op jit(solution)/shard_map/pallas_call | solution.py:507
  74.5 3.5 %collective-permute-start.6 = (f32[648,128]{1,0:T(8,128)}, f32[648,128]{1,0:T(8,128)S(1)}, u32[]{:S(2)}, u32[]{:S(2)}) collective-permute-start(f32[648,128]{1,0:T(8,128)} %get-tuple-element.13.edge_high), channel_id=1, source_target_pairs={{0,1},{1,2},{2,3},{4,5},{5,6},{6,7},{8,9},{9,10},{10,11},{12,13},{... | collective-permute-start | bytes 995336 | tf_op jit(solution)/shard_map/ppermute | solution.py:31
  78.0 1.3 %collective-permute-start.7 = (f32[648,128]{1,0:T(8,128)}, f32[648,128]{1,0:T(8,128)S(1)}, u32[]{:S(2)}, u32[]{:S(2)}) collective-permute-start(f32[648,128]{1,0:T(8,128)} %get-tuple-element.14.edge_low), channel_id=1, source_target_pairs={{1,0},{2,1},{3,2},{5,4},{6,5},{7,6},{9,8},{10,9},{11,10},{13,12},{... | collective-permute-start | bytes 995336 | tf_op jit(solution)/shard_map/ppermute | solution.py:31
  79.3 4.5 %shard_map.68.bundle = f32[37888,128]{1,0:T(8,128)} custom-call(f32[16,256,128]{2,1,0:T(8,128)} %bitcast.16, f32[16,256,128]{2,1,0:T(8,128)} %copy-done, f32[648,128]{1,0:T(8,128)} %get-tuple-element.14.edge_low, f32[648,128]{1,0:T(8,128)} %get-tuple-element.13.edge_high, f32[576,128]{1,0:T(8,128)} %broadcast_in_dim.9.kappa, f32[1,128]{1,0:T(1,128)} %bitcast.23, ...), custom_call_target="tpu_custom_call" | custom-call | flops 1000000000 | bytes 1000000 | tf_op jit(solution)/shard_map/pallas_call | solution.py:507
  83.8 1.2 collective-permute-done.6.left
  85.0 4.0 %collective-permute-done.7.right = f32[648,128]{1,0:T(8,128)S(1)} collective-permute-done((f32[648,128]{1,0:T(8,128)}, f32[648,128]{1,0:T(8,128)S(1)}, u32[]{:S(2)}, u32[]{:S(2)}) %collective-permute-start.7) | collective-permute-done | bytes 331808 | tf_op jit(solution)/shard_map/ppermute | solution.py:31
  89.0 0.0 all-to-all-done.middle
  89.1 5.4 %shard_map.69 = f32[8,512,128]{2,1,0:T(8,128)S(1)} custom-call(f32[8,432,128]{2,1,0:T(8,128)S(1)} %all-to-all-done.middle, f32[648,128]{1,0:T(8,128)S(1)} %collective-permute-done.6.left, f32[648,128]{1,0:T(8,128)S(1)} %collective-permute-done.7.right, f32[37888,128]{1,0:T(8,128)} %shard_map.68.bundle), custom_call_target="tpu_custom_call" | custom-call | flops 1000000000 | bytes 1000000 | tf_op jit(solution)/shard_map/pallas_call | solution.py:507
  94.4 29.3 %all_to_all.15 = f32[8,512,128]{2,1,0:T(8,128)S(1)} all-to-all(f32[8,512,128]{2,1,0:T(8,128)S(1)} %shard_map.69), channel_id=1, replica_groups=mesh['tm'=8,'tx'=4] {'tm'}, dimensions={0} | all-to-all | bytes 4194304 | tf_op jit(solution)/shard_map/all_to_all | solution.py:524
  123.7 1.5 %copy.7 = f32[16,8,32,128]{3,2,1,0:T(8,128)} copy(f32[16,8,32,128]{3,2,0,1:T(8,128)S(1)} %bitcast.17) | data formatting | bytes 4194304 | tf_op jit(solution)/shard_map/transpose | solution.py:669
Async XLA Ops:
  0.0 13.5 %collective-permute-start = (f32[16,256,128]{2,1,0:T(8,128)}, f32[16,256,128]{2,1,0:T(8,128)S(1)}, u32[]{:S(2)}, u32[]{:S(2)}) collective-permute-start(f32[16,256,128]{2,1,0:T(8,128)} %bitcast.11), channel_id=1, source_target_pairs={{0,4},{4,0},{8,12},{12,8},{16,20},{20,16},{24,28},{28,24},{1,5},{5... | collective-permute-start | bytes 6291464 | tf_op jit(solution)/shard_map/ppermute | solution.py:520
  1.5 7.9 %collective-permute-start.1 = (f32[256,128]{1,0:T(8,128)S(1)}, f32[256,128]{1,0:T(8,128)S(1)}, u32[]{:S(2)}, u32[]{:S(2)}) collective-permute-start(f32[256,128]{1,0:T(8,128)S(1)} %get-tuple-element.16), channel_id=1, source_target_pairs={{0,1},{1,2},{2,3},{4,5},{5,6},{6,7},{8,9},{9,10},{10,11},{12,13},{... | collective-permute-start | bytes 393224 | tf_op jit(solution)/shard_map/ppermute | solution.py:31
  6.0 7.5 %collective-permute-start.2 = (f32[256,128]{1,0:T(8,128)S(1)}, f32[256,128]{1,0:T(8,128)S(1)}, u32[]{:S(2)}, u32[]{:S(2)}) collective-permute-start(f32[256,128]{1,0:T(8,128)S(1)} %get-tuple-element.15), channel_id=1, source_target_pairs={{1,0},{2,1},{3,2},{5,4},{6,5},{7,6},{9,8},{10,9},{11,10},{13,12},{... | collective-permute-start | bytes 393224 | tf_op jit(solution)/shard_map/ppermute | solution.py:31
  9.4 4.1 %copy-start.5 = (f32[256,128]{1,0:T(8,128)}, f32[256,128]{1,0:T(8,128)S(1)}, u32[]{:S(2)}) copy-start(f32[256,128]{1,0:T(8,128)S(1)} %collective-permute-done.1.low) | copy-start | bytes 393220
  13.5 0.7 copy-start.6
  13.5 1.4 %copy-start = (f32[16,256,128]{2,1,0:T(8,128)}, f32[16,256,128]{2,1,0:T(8,128)S(1)}, u32[]{:S(2)}) copy-start(f32[16,256,128]{2,1,0:T(8,128)S(1)} %collective-permute-done.other) | copy-start | bytes 6291460
  17.9 14.1 %all-to-all-start.1 = ((f32[8,144,128]{2,1,0:T(8,128)}), f32[8,144,128]{2,1,0:T(8,128)S(1)}, u32[]{:S(2)}, u32[]{:S(2)}) async-start(f32[8,144,128]{2,1,0:T(8,128)} %shard_map.65), calls=%async_computation.1 | async-start | bytes 1179648 | tf_op jit(solution)/shard_map/all_to_all | solution.py:524
  32.0 5.9 %copy-start.1 = (f32[8,144,128]{2,1,0:T(8,128)}, f32[8,144,128]{2,1,0:T(8,128)S(1)}, u32[]{:S(2)}) copy-start(f32[8,144,128]{2,1,0:T(8,128)S(1)} %all-to-all-done.1.edge) | copy-start | bytes 1769476
  32.0 57.0 %all-to-all-start = ((f32[8,432,128]{2,1,0:T(8,128)}), f32[8,432,128]{2,1,0:T(8,128)S(1)}, u32[]{:S(2)}, u32[]{:S(2)}) async-start(f32[8,432,128]{2,1,0:T(8,128)} %shard_map.64), calls=%async_computation | async-start | bytes 3538944 | tf_op jit(solution)/shard_map/all_to_all | solution.py:524
  35.6 11.5 %copy-start.7 = (f32[16,256]{1,0:T(8,128)S(1)}, f32[16,256]{1,0:T(8,128)}, u32[]{:S(2)}) copy-start(f32[16,256]{1,0:T(8,128)} %kappa.3) | copy-start | bytes 49156
  38.0 24.4 %collective-permute-start.3 = (f32[576,128]{1,0:T(8,128)}, f32[576,128]{1,0:T(8,128)S(1)}, u32[]{:S(2)}, u32[]{:S(2)}) collective-permute-start(f32[576,128]{1,0:T(8,128)} %get-tuple-element.10), channel_id=1, source_target_pairs={{0,8},{4,12},{8,16},{12,20},{16,24},{20,28},{1,9},{5,13},{9,17},{1... | collective-permute-start | bytes 884744 | tf_op jit(solution)/shard_map/ppermute | solution.py:537
  41.8 26.6 %collective-permute-start.4 = (f32[576,128]{1,0:T(8,128)}, f32[576,128]{1,0:T(8,128)S(1)}, u32[]{:S(2)}, u32[]{:S(2)}) collective-permute-start(f32[576,128]{1,0:T(8,128)} %get-tuple-element.11), channel_id=1, source_target_pairs={{0,16},{4,20},{8,24},{12,28},{16,0},{20,4},{1,17},{5,21},{9,25},{1... | collective-permute-start | bytes 884744 | tf_op jit(solution)/shard_map/ppermute | solution.py:537
  45.2 25.3 %collective-permute-start.5 = (f32[576,128]{1,0:T(8,128)}, f32[576,128]{1,0:T(8,128)S(1)}, u32[]{:S(2)}, u32[]{:S(2)}) collective-permute-start(f32[576,128]{1,0:T(8,128)} %get-tuple-element.12), channel_id=1, source_target_pairs={{0,24},{4,28},{8,0},{12,4},{16,8},{20,12},{1,25},{5,29},{9,1},{13,... | collective-permute-start | bytes 884744 | tf_op jit(solution)/shard_map/ppermute | solution.py:537
  62.3 8.9 %copy-start.2 = (f32[576,128]{1,0:T(8,128)}, f32[576,128]{1,0:T(8,128)S(1)}, u32[]{:S(2)}) copy-start(f32[576,128]{1,0:T(8,128)S(1)} %collective-permute-done.3.rest_0_) | copy-start | bytes 884740
  68.3 3.0 %copy-start.3 = (f32[576,128]{1,0:T(8,128)}, f32[576,128]{1,0:T(8,128)S(1)}, u32[]{:S(2)}) copy-start(f32[576,128]{1,0:T(8,128)S(1)} %collective-permute-done.4.rest_1_) | copy-start | bytes 884740
  70.4 0.9 copy-start.4
  74.5 10.5 %collective-permute-start.6 = (f32[648,128]{1,0:T(8,128)}, f32[648,128]{1,0:T(8,128)S(1)}, u32[]{:S(2)}, u32[]{:S(2)}) collective-permute-start(f32[648,128]{1,0:T(8,128)} %get-tuple-element.13.edge_high), channel_id=1, source_target_pairs={{0,1},{1,2},{2,3},{4,5},{5,6},{6,7},{8,9},{9,10},{10,11},{12,13},{... | collective-permute-start | bytes 995336 | tf_op jit(solution)/shard_map/ppermute | solution.py:31
  78.0 11.1 %collective-permute-start.7 = (f32[648,128]{1,0:T(8,128)}, f32[648,128]{1,0:T(8,128)S(1)}, u32[]{:S(2)}, u32[]{:S(2)}) collective-permute-start(f32[648,128]{1,0:T(8,128)} %get-tuple-element.14.edge_low), channel_id=1, source_target_pairs={{1,0},{2,1},{3,2},{5,4},{6,5},{7,6},{9,8},{10,9},{11,10},{13,12},{... | collective-permute-start | bytes 995336 | tf_op jit(solution)/shard_map/ppermute | solution.py:31
